TPU v7x, 256 devices: a whole 4x4x8 slice. The times are simulated.
256 devices in a mesh: val: 8 (over x, z_lo), pts: 32 (over z_hi, y, core).
Axes of the slice: x: 4, y: 4, z: 8 (z_hi: 4, z_lo: 2; z = z_hi * 2 + z_lo), core: 2. Of those that a mesh axis runs over, the one named last changes fastest.
Arguments:
- trial: bfloat16 [512, 16384], P('val', 'pts'), may hold values from -6 to 6
- energy_gap: float32 [512, 512], P('val', 'pts'), may hold values from 0.5 to 3.5
- orb_val: bfloat16 [512, 16384], P('val'), may hold values from -0.25 to 0.25
- orb_cond: bfloat16 [512, 16384], P('pts'), may hold values from -0.25 to 0.25
- kernel: bfloat16 [16384, 16384], P('pts', 'val'), may hold values from -0.046875 to 0.046875
Outputs:
- first_step: bfloat16 [512, 16384], P('val', 'pts')
- filtered: bfloat16 [512, 16384], P('val', 'pts')
All inputs are finite; a program needn't handle non-finite values.
Results may differ from a plain program's by a relative error of at most 0.029.
Values may be sent and summed in bfloat16 or wider, within the bound.
No kernel may reach another device: no remote copies, remote signals or barrier semaphores. Data moves between devices by JAX's collectives and lax.ppermute only.
A program may use at most 64 MiB of HBM per device.

v0:
```python
import functools

import jax
import jax.numpy as jnp
from jax import lax
from jax.experimental import pallas as pl
from jax.experimental.pallas import tpu as pltpu
from jax.sharding import Mesh, PartitionSpec as P

K = 32
CENTER = 2.0
HALF_WIDTH = 1.5

FINE = (("x", 4), ("zl", 2), ("zh", 4), ("y", 4), ("core", 2))
VAL = ("x", "zl")
RING = ("zh", "y")
PTS = ("zh", "y", "core")

BF16 = jnp.bfloat16
F32 = jnp.float32
VMEM = pl.BlockSpec(memory_space=pltpu.VMEM)
VMEM_LIMIT = 16 << 20


def swap_cores(array):
    return lax.ppermute(array, "core", [(0, 1), (1, 0)])


def exchange(array, axes):
    return lax.all_to_all(array, axes, 0, 0, tiled=True)


def cost(flops, moved):
    return pl.CostEstimate(flops=int(flops), bytes_accessed=int(moved), transcendentals=0)


def call(kernel, inputs, outputs, flops, scalars=0):
    smem = pl.BlockSpec(memory_space=pltpu.SMEM)
    moved = sum(2 * a.size for a in inputs) + sum(2 * o.size for o in outputs)
    return pl.pallas_call(
        kernel,
        in_specs=[smem] * scalars + [VMEM] * (len(inputs) - scalars),
        out_specs=[VMEM] * len(outputs),
        out_shape=list(outputs),
        compiler_params=pltpu.CompilerParams(vmem_limit_bytes=VMEM_LIMIT),
        cost_estimate=cost(flops, moved),
    )(*inputs)


def shape(dims, dtype=BF16):
    return jax.ShapeDtypeStruct(tuple(dims), dtype)


def encode_points(h_ref, xt_ref, val_ref, cond_ref, cond_other_ref, out_ref, width):
    pieces, _, piece = out_ref.shape
    per_block = width // piece
    conds = 2 * cond_ref.shape[0]
    cols = min(256, piece)

    def block(g, carry):
        base = pl.multiple_of((2 * g + h_ref[0]) * width, width)
        for first in range(0, width, cols):
            at = pl.ds(pl.multiple_of(base + first, cols), cols)
            cond = jnp.concatenate([cond_ref[:, at], cond_other_ref[:, at]], 0).astype(F32)
            val = val_ref[:, at]
            total = jnp.zeros((K, cols), F32)
            for c in range(0, conds, 4):
                part = jnp.dot(xt_ref[c * K : (c + 4) * K, :], val, preferred_element_type=F32)
                for i in range(4):
                    total = total + part[i * K : (i + 1) * K] * cond[c + i : c + i + 1]
            out_ref[g * per_block + first // piece, :, first % piece : first % piece + cols] = total.astype(BF16)
        return carry

    lax.fori_loop(0, pieces // per_block, block, 0)


def encode_first(width, h_ref, own_ref, other_ref, val_ref, cond_ref, cond_other_ref, out_ref, xt_ref):
    rows = own_ref.shape[1]
    xt_ref[:rows] = own_ref[...].astype(F32).T.astype(BF16)
    xt_ref[rows:] = other_ref[...].astype(F32).T.astype(BF16)
    encode_points(h_ref, xt_ref, val_ref, cond_ref, cond_other_ref, out_ref, width)


def stepped(xt, gap, coupled):
    scale = (gap - CENTER) * (1.0 / HALF_WIDTH)
    scale = jnp.broadcast_to(scale[:, None, :], (gap.shape[0], K, gap.shape[1])).reshape(xt.shape)
    return xt.astype(F32) * scale + coupled * (2.0 / HALF_WIDTH)


def encode_next(
    width, h_ref, part_ref, recv_ref, old_ref, gap_ref, val_ref, cond_ref, cond_other_ref, out_ref, xt_ref
):
    half = old_ref.shape[0] // 2
    conds = half // K
    for side in range(2):
        here = slice(side * half, (side + 1) * half)
        there = slice((1 - side) * half, (2 - side) * half)
        coupled = part_ref[here] + recv_ref[there].astype(F32)
        gap = gap_ref[side * conds : (side + 1) * conds]
        xt_ref[here] = stepped(old_ref[here], gap, coupled).astype(BF16)
    encode_points(h_ref, xt_ref, val_ref, cond_ref, cond_other_ref, out_ref, width)


def encode(kernel, h, whole, orb_val, cond, cond_other, pieces, piece, width):
    rows = 2 * cond.shape[0] * K
    val_count, points = orb_val.shape
    return call(
        functools.partial(kernel, width),
        (h, *whole, orb_val, cond, cond_other),
        (shape((pieces, K, piece)), shape((rows, val_count))),
        rows * val_count * points,
        1,
    )


def total_kernel(in_ref, out_ref):
    total = in_ref[0].astype(F32)
    for index in range(1, in_ref.shape[0]):
        total = total + in_ref[index].astype(F32)
    total = total.astype(BF16)
    for copy in range(out_ref.shape[0]):
        out_ref[copy] = total


def summed(array, copies):
    return call(total_kernel, (array,), (shape((copies, *array.shape[1:])),), array.size)[0]


def apply_kernel(pieces, width, h_ref, own_ref, other_ref, kernel_ref, out_ref):
    piece = own_ref.shape[2]
    even = h_ref[0] == 0

    def added(ref, q):
        total = ref[q].astype(F32)
        for index in range(q + pieces, ref.shape[0], pieces):
            total = total + ref[index].astype(F32)
        return total

    total = jnp.zeros((K, kernel_ref.shape[0]), F32)
    for q in range(pieces):
        own, other = added(own_ref, q), added(other_ref, q)
        for side in range(2):
            fit = jnp.where(even, own, other) if side == 0 else jnp.where(even, other, own)
            at = q * piece
            first = width * (2 * (at // width) + side) + at % width
            total = total + lax.dot_general(
                fit.astype(BF16),
                kernel_ref[:, first : first + piece],
                (((1,), (1,)), ((), ())),
                preferred_element_type=F32,
            )
    total = total.astype(BF16)
    for copy in range(out_ref.shape[0]):
        out_ref[copy] = total


def applied(h, own, other, kernel, pieces, copies):
    rows = kernel.shape[0]
    return call(
        functools.partial(apply_kernel, pieces, rows),
        (h, own, other, kernel),
        (shape((copies, K, rows)),),
        2 * K * kernel.size,
        1,
    )[0]


def decode_kernel(h_ref, field_ref, val_ref, cond_ref, cond_other_ref, part_ref, send_ref):
    blocks, _, width = field_ref.shape
    part_ref[...] = jnp.zeros_like(part_ref)

    def block(g, carry):
        at = pl.ds(pl.multiple_of((2 * g + h_ref[0]) * width, width), width)
        cond = jnp.concatenate([cond_ref[:, at], cond_other_ref[:, at]], 0).astype(F32)
        field = field_ref[g].astype(F32)
        val = val_ref[:, at]
        for c in range(0, cond.shape[0], 4):
            pairs = jnp.concatenate([cond[c + i : c + i + 1] * field for i in range(4)], 0).astype(BF16)
            part_ref[c * K : (c + 4) * K, :] += lax.dot_general(
                pairs, val, (((1,), (1,)), ((), ())), preferred_element_type=F32
            )
        return carry

    lax.fori_loop(0, blocks, block, 0)
    send_ref[...] = part_ref[part_ref.shape[0] - send_ref.shape[0] :].astype(BF16)


def decode(h, field, orb_val, cond, cond_other, sent):
    rows = 2 * cond.shape[0] * K
    val_count, points = orb_val.shape
    return call(
        decode_kernel,
        (h, field, orb_val, cond, cond_other),
        (shape((rows, val_count), F32), shape((sent, val_count))),
        rows * val_count * points,
        1,
    )


def turn_kernel(xt_ref, out_ref):
    out_ref[...] = xt_ref[: out_ref.shape[1]].astype(F32).T.astype(BF16)


def turned(xt, rows):
    return call(turn_kernel, (xt,), (shape((xt.shape[1], rows)),), xt.size)[0]


def finish_kernel(part_ref, recv_ref, xt_ref, gap_ref, trial_ref, out_ref):
    rows = recv_ref.shape[0]
    coupled = part_ref[:rows] + recv_ref[...].astype(F32)
    second = stepped(xt_ref[:rows], gap_ref[: rows // K], coupled)
    out_ref[...] = (2.0 * second.T - trial_ref[...].astype(F32)).astype(BF16)


def finish(part, recv, xt, gap, trial):
    return call(finish_kernel, (part, recv, xt, gap, trial), (shape(trial.shape),), 8 * trial.size)[0]


def field_of(encoded, h, kernel, sizes):
    ring = sizes["zh"] * sizes["y"]
    shares = exchange(encoded, (*VAL, "y"))
    shares = exchange(summed(shares, ring), RING)
    image = applied(h, shares, swap_cores(shares), kernel, sizes["y"], sizes["x"] * sizes["zl"])
    return exchange(summed(exchange(image, VAL), ring), RING)


def on_device(sizes, trial, energy_gap, orb_val, orb_cond, kernel):
    width = kernel.shape[0]
    pieces = sizes["x"] * sizes["zl"] * sizes["y"]
    piece = kernel.shape[1] // 2 // sizes["y"]
    own_rows = trial.shape[1]
    h = lax.axis_index("core").astype(jnp.int32).reshape(1)
    cond_other = swap_cores(orb_cond)
    trial_other = swap_cores(trial)
    gap = energy_gap.T
    gap = jnp.concatenate([gap, swap_cores(gap)], 0)
    orbitals = (orb_val, orb_cond, cond_other)

    encoded, xt = encode(encode_first, h, (trial, trial_other), *orbitals, pieces, piece, width)
    field = field_of(encoded, h, kernel, sizes)
    part, sent = decode(h, field, *orbitals, 2 * own_rows)
    encoded, xt = encode(encode_next, h, (part, swap_cores(sent), xt, gap), *orbitals, pieces, piece, width)
    first_step = turned(xt, own_rows)
    field = field_of(encoded, h, kernel, sizes)
    part, sent = decode(h, field, *orbitals, own_rows)
    filtered = finish(part, swap_cores(sent), xt, gap, trial)
    return first_step, filtered


def build(mesh, fine):
    split = Mesh(mesh.devices.reshape([size for _, size in fine]), [name for name, _ in fine])
    placed = (P(VAL, PTS), P(VAL, PTS), P(VAL, None), P(PTS, None), P(PTS, VAL))
    return jax.shard_map(
        functools.partial(on_device, dict(fine)),
        mesh=split,
        in_specs=placed,
        out_specs=(P(VAL, PTS), P(VAL, PTS)),
        check_vma=False,
    )


def solution(mesh):
    return build(mesh, FINE)
```

profile of v0, /device:TPU:1, one launch (start us, length us, event | category | flops | bytes accessed | tf_op | source)
XLA Modules:
  0.0 179.9 jit_solution(12201480664845840892)
XLA Ops:
  0.6 3.3 %collective-permute-start.1 = (bf16[16,16384]{1,0:T(8,128)(2,1)}, bf16[16,16384]{1,0:T(8,128)(2,1)S(1)}, u32[]{:S(2)}, u32[]{:S(2)}) collective-permute-start(bf16[16,16384]{1,0:T(8,128)(2,1)} %cond_ref.7), channel_id=1, source_target_pairs={{0,1},{1,0},{2,3},{3,2},{4,5},{5,4},{6,7},{7,6},{8,9},{9,8},{10,11... | collective-permute-start | bytes 1572872 | tf_op jit(solution)/shard_map/ppermute | solution.py:26
  3.9 0.1 collective-permute-start
  4.0 1.7 collective-permute-done.other_ref
  5.8 0.0 collective-permute-done.1.cond_other_ref
  5.8 0.0 copy-start.1
  5.8 1.6 copy-done.1
  7.4 0.0 copy-start.3
  7.4 1.0 copy-done.3
  8.4 0.0 copy-start.5
  8.4 0.8 copy-done.5
  9.2 7.0 %shard_map.68 = (bf16[32,32,256]{2,1,0:T(8,128)(2,1)S(1)}, bf16[1024,64]{1,0:T(8,128)(2,1)S(1)}) custom-call(s32[1]{0:T(128)} %bitcast.h_ref, bf16[64,512]{1,0:T(8,128)(2,1)S(1)} %copy-done.5, bf16[64,512]{1,0:T(8,128)(2,1)S(1)} %collective-permute-done.other_ref, bf16[64,16384]{1,0:T(8,128)(2,1)S(1)} %copy-done.1, bf16[16,16384]{1,0:T(8,128)(2,1)S(1)} %copy-done.3, ...), custom_call_target="tpu_custom_call" | custom-call | flops 1073741824 | bytes 3932162 | tf_op jit(solution)/shard_map/pallas_call | solution.py:40
  16.2 0.0 copy-start
  16.3 16.8 %all_to_all.40.in_ref = bf16[32,32,256]{2,1,0:T(8,128)(2,1)S(1)} all-to-all(bf16[32,32,256]{2,1,0:T(8,128)(2,1)S(1)} %get-tuple-element.10), channel_id=1, replica_groups=mesh['x'=4,'zl'=2,'zh'=4,'y'=4,'core'=2] {'x','zl','y'}, dimensions={0} | all-to-all | bytes 1048576 | tf_op jit(solution)/shard_map/all_to_all | solution.py:30
  33.1 0.1 shard_map.69
  33.2 19.5 %all_to_all.41.own_ref = bf16[16,32,256]{2,1,0:T(8,128)(2,1)S(1)} all-to-all(bf16[16,32,256]{2,1,0:T(8,128)(2,1)S(1)} %shard_map.69), channel_id=1, replica_groups=mesh['x'=4,'zl'=2,'zh'=4,'y'=4,'core'=2] {'zh','y'}, dimensions={0} | all-to-all | bytes 524288 | tf_op jit(solution)/shard_map/all_to_all | solution.py:30
  52.7 0.0 copy-start.2
  52.7 0.0 copy-start.4
  52.7 3.3 %collective-permute-start.2 = (bf16[16,32,256]{2,1,0:T(8,128)(2,1)S(1)}, bf16[16,32,256]{2,1,0:T(8,128)(2,1)S(1)}, u32[]{:S(2)}, u32[]{:S(2)}) collective-permute-start(bf16[16,32,256]{2,1,0:T(8,128)(2,1)S(1)} %all_to_all.41.own_ref), channel_id=1, source_target_pairs={{0,1},{1,0},{2,3},{3,2},{4,5},{5,4},{6,7},{7,6},{8,9},{9,8},{10,11... | collective-permute-start | bytes 786440 | tf_op jit(solution)/shard_map/ppermute | solution.py:26
  55.9 1.2 collective-permute-done.2.other_ref
  57.1 0.0 copy-done
  57.1 0.7 shard_map.70
  57.8 9.2 %all_to_all.42.in_ref = bf16[8,32,512]{2,1,0:T(8,128)(2,1)S(1)} all-to-all(bf16[8,32,512]{2,1,0:T(8,128)(2,1)S(1)} %shard_map.70), channel_id=1, replica_groups=mesh['x'=4,'zl'=2,'zh'=4,'y'=4,'core'=2] {'x','zl'}, dimensions={0} | all-to-all | bytes 524288 | tf_op jit(solution)/shard_map/all_to_all | solution.py:30
  67.0 0.1 shard_map.71
  67.1 20.6 %all_to_all.43.field_ref = bf16[16,32,512]{2,1,0:T(8,128)(2,1)S(1)} all-to-all(bf16[16,32,512]{2,1,0:T(8,128)(2,1)S(1)} %shard_map.71), channel_id=1, replica_groups=mesh['x'=4,'zl'=2,'zh'=4,'y'=4,'core'=2] {'zh','y'}, dimensions={0} | all-to-all | bytes 1048576 | tf_op jit(solution)/shard_map/all_to_all | solution.py:30
  87.7 0.0 copy-done.2
  87.7 0.0 copy-done.4
  87.7 6.9 %shard_map.72 = (f32[1024,64]{1,0:T(8,128)S(1)}, bf16[1024,64]{1,0:T(8,128)(2,1)S(1)}) custom-call(s32[1]{0:T(128)} %bitcast.h_ref, bf16[16,32,512]{2,1,0:T(8,128)(2,1)S(1)} %all_to_all.43.field_ref, bf16[64,16384]{1,0:T(8,128)(2,1)S(1)} %copy-done.2, bf16[16,16384]{1,0:T(8,128)(2,1)S(1)} %copy-done.4, ...), custom_call_target="tpu_custom_call" | custom-call | flops 1073741824 | bytes 3932162 | tf_op jit(solution)/shard_map/pallas_call | solution.py:40
  94.6 2.0 %collective-permute-start.3 = (bf16[1024,64]{1,0:T(8,128)(2,1)S(1)}, bf16[1024,64]{1,0:T(8,128)(2,1)S(1)}, u32[]{:S(2)}, u32[]{:S(2)}) collective-permute-start(bf16[1024,64]{1,0:T(8,128)(2,1)S(1)} %get-tuple-element.12), channel_id=1, source_target_pairs={{0,1},{1,0},{2,3},{3,2},{4,5},{5,4},{6,7},{7,6},{8,9},{9,8},{10,11... | collective-permute-start | bytes 393224 | tf_op jit(solution)/shard_map/ppermute | solution.py:26
  96.6 0.0 copy-done.7
  96.6 0.1 collective-permute-start.4
  96.7 1.1 collective-permute-done.4
  97.8 0.0 collective-permute-done.3.recv_ref
  97.8 7.0 %shard_map.73 = (bf16[32,32,256]{2,1,0:T(8,128)(2,1)S(1)}, bf16[1024,64]{1,0:T(8,128)(2,1)S(1)}) custom-call(s32[1]{0:T(128)} %bitcast.h_ref, f32[1024,64]{1,0:T(8,128)S(1)} %get-tuple-element.11.part_ref, bf16[1024,64]{1,0:T(8,128)(2,1)S(1)} %collective-permute-done.3.recv_ref, bf16[1024,64]{1,0:T(8,128)(2,1)S(1)} %get-tuple-element.13.old_ref, ...), custom_call_target="tpu_custom_call" | custom-call | flops 1073741824 | bytes 4198402 | tf_op jit(solution)/shard_map/pallas_call | solution.py:40
  104.8 14.1 %all_to_all.44.in_ref = bf16[32,32,256]{2,1,0:T(8,128)(2,1)S(1)} all-to-all(bf16[32,32,256]{2,1,0:T(8,128)(2,1)S(1)} %get-tuple-element.15), channel_id=1, replica_groups=mesh['x'=4,'zl'=2,'zh'=4,'y'=4,'core'=2] {'x','zl','y'}, dimensions={0} | all-to-all | bytes 1048576 | tf_op jit(solution)/shard_map/all_to_all | solution.py:30
  118.9 0.1 shard_map.75
  119.0 15.3 %all_to_all.45.own_ref = bf16[16,32,256]{2,1,0:T(8,128)(2,1)S(1)} all-to-all(bf16[16,32,256]{2,1,0:T(8,128)(2,1)S(1)} %shard_map.75), channel_id=1, replica_groups=mesh['x'=4,'zl'=2,'zh'=4,'y'=4,'core'=2] {'zh','y'}, dimensions={0} | all-to-all | bytes 524288 | tf_op jit(solution)/shard_map/all_to_all | solution.py:30
  134.3 3.4 %collective-permute-start.5 = (bf16[16,32,256]{2,1,0:T(8,128)(2,1)S(1)}, bf16[16,32,256]{2,1,0:T(8,128)(2,1)S(1)}, u32[]{:S(2)}, u32[]{:S(2)}) collective-permute-start(bf16[16,32,256]{2,1,0:T(8,128)(2,1)S(1)} %all_to_all.45.own_ref), channel_id=1, source_target_pairs={{0,1},{1,0},{2,3},{3,2},{4,5},{5,4},{6,7},{7,6},{8,9},{9,8},{10,11... | collective-permute-start | bytes 786440 | tf_op jit(solution)/shard_map/ppermute | solution.py:26
  137.6 1.2 collective-permute-done.5.other_ref
  138.8 0.7 shard_map.76
  139.6 9.2 %all_to_all.46.in_ref = bf16[8,32,512]{2,1,0:T(8,128)(2,1)S(1)} all-to-all(bf16[8,32,512]{2,1,0:T(8,128)(2,1)S(1)} %shard_map.76), channel_id=1, replica_groups=mesh['x'=4,'zl'=2,'zh'=4,'y'=4,'core'=2] {'x','zl'}, dimensions={0} | all-to-all | bytes 524288 | tf_op jit(solution)/shard_map/all_to_all | solution.py:30
  148.7 0.1 shard_map.77
  148.8 20.5 %all_to_all.47.field_ref = bf16[16,32,512]{2,1,0:T(8,128)(2,1)S(1)} all-to-all(bf16[16,32,512]{2,1,0:T(8,128)(2,1)S(1)} %shard_map.77), channel_id=1, replica_groups=mesh['x'=4,'zl'=2,'zh'=4,'y'=4,'core'=2] {'zh','y'}, dimensions={0} | all-to-all | bytes 1048576 | tf_op jit(solution)/shard_map/all_to_all | solution.py:30
  169.3 6.9 %shard_map.78 = (f32[1024,64]{1,0:T(8,128)S(1)}, bf16[512,64]{1,0:T(8,128)(2,1)S(1)}) custom-call(s32[1]{0:T(128)} %bitcast.h_ref, bf16[16,32,512]{2,1,0:T(8,128)(2,1)S(1)} %all_to_all.47.field_ref, bf16[64,16384]{1,0:T(8,128)(2,1)S(1)} %copy-done.2, bf16[16,16384]{1,0:T(8,128)(2,1)S(1)} %copy-done.4, bf16[16,16384]{1,0:T(8,128)(2,1)S(1)} %collective-permute-done.1.cond_other_ref), custom_call_target="tpu_custom_call" | custom-call | flops 1073741824 | bytes 3866626 | tf_op jit(solution)/shard_map/pallas_call | solution.py:40
  176.2 2.0 %collective-permute-start.6 = (bf16[512,64]{1,0:T(8,128)(2,1)S(1)}, bf16[512,64]{1,0:T(8,128)(2,1)S(1)}, u32[]{:S(2)}, u32[]{:S(2)}) collective-permute-start(bf16[512,64]{1,0:T(8,128)(2,1)S(1)} %get-tuple-element.17), channel_id=1, source_target_pairs={{0,1},{1,0},{2,3},{3,2},{4,5},{5,4},{6,7},{7,6},{8,9},{9,8},{10,11... | collective-permute-start | bytes 196616 | tf_op jit(solution)/shard_map/ppermute | solution.py:26
  178.2 0.7 shard_map.74
  178.9 0.3 collective-permute-done.6.recv_ref
  179.2 0.0 copy-done.6
  179.2 0.8 shard_map.79
  (3 shorter events, 0.0 us)
Async XLA Ops:
  0.6 5.1 %collective-permute-start.1 = (bf16[16,16384]{1,0:T(8,128)(2,1)}, bf16[16,16384]{1,0:T(8,128)(2,1)S(1)}, u32[]{:S(2)}, u32[]{:S(2)}) collective-permute-start(bf16[16,16384]{1,0:T(8,128)(2,1)} %cond_ref.7), channel_id=1, source_target_pairs={{0,1},{1,0},{2,3},{3,2},{4,5},{5,4},{6,7},{7,6},{8,9},{9,8},{10,11... | collective-permute-start | bytes 1572872 | tf_op jit(solution)/shard_map/ppermute | solution.py:26
  3.9 1.8 %collective-permute-start = (bf16[64,512]{1,0:T(8,128)(2,1)}, bf16[64,512]{1,0:T(8,128)(2,1)S(1)}, u32[]{:S(2)}, u32[]{:S(2)}) collective-permute-start(bf16[64,512]{1,0:T(8,128)(2,1)} %trial_ref.1), channel_id=1, source_target_pairs={{0,1},{1,0},{2,3},{3,2},{4,5},{5,4},{6,7},{7,6},{8,9},{9,8},{10,11... | collective-permute-start | bytes 196616 | tf_op jit(solution)/shard_map/ppermute | solution.py:26
  5.8 1.6 copy-start.1
  7.4 1.0 copy-start.3
  8.4 0.8 copy-start.5
  16.2 40.9 %copy-start = (bf16[512,2048]{1,0:T(8,128)(2,1)S(1)}, bf16[512,2048]{1,0:T(8,128)(2,1)}, u32[]{:S(2)}) copy-start(bf16[512,2048]{1,0:T(8,128)(2,1)} %kernel_ref.3) | copy-start | bytes 6291460
  52.7 35.0 %copy-start.2 = (bf16[64,16384]{1,0:T(8,128)(2,1)S(1)}, bf16[64,16384]{1,0:T(8,128)(2,1)}, u32[]{:S(2)}) copy-start(bf16[64,16384]{1,0:T(8,128)(2,1)} %val_ref.7) | copy-start | bytes 6291460
  52.7 35.0 %copy-start.4 = (bf16[16,16384]{1,0:T(8,128)(2,1)S(1)}, bf16[16,16384]{1,0:T(8,128)(2,1)}, u32[]{:S(2)}) copy-start(bf16[16,16384]{1,0:T(8,128)(2,1)} %cond_ref.7) | copy-start | bytes 1572868
  52.7 4.4 %collective-permute-start.2 = (bf16[16,32,256]{2,1,0:T(8,128)(2,1)S(1)}, bf16[16,32,256]{2,1,0:T(8,128)(2,1)S(1)}, u32[]{:S(2)}, u32[]{:S(2)}) collective-permute-start(bf16[16,32,256]{2,1,0:T(8,128)(2,1)S(1)} %all_to_all.41.own_ref), channel_id=1, source_target_pairs={{0,1},{1,0},{2,3},{3,2},{4,5},{5,4},{6,7},{7,6},{8,9},{9,8},{10,11... | collective-permute-start | bytes 786440 | tf_op jit(solution)/shard_map/ppermute | solution.py:26
  87.7 9.0 %copy-start.7 = (f32[64,16]{0,1:T(8,128)S(1)}, f32[64,16]{0,1:T(8,128)}, u32[]{:S(2)}) copy-start(f32[64,16]{0,1:T(8,128)} %param.6) | copy-start | bytes 12292
  94.6 3.2 %collective-permute-start.3 = (bf16[1024,64]{1,0:T(8,128)(2,1)S(1)}, bf16[1024,64]{1,0:T(8,128)(2,1)S(1)}, u32[]{:S(2)}, u32[]{:S(2)}) collective-permute-start(bf16[1024,64]{1,0:T(8,128)(2,1)S(1)} %get-tuple-element.12), channel_id=1, source_target_pairs={{0,1},{1,0},{2,3},{3,2},{4,5},{5,4},{6,7},{7,6},{8,9},{9,8},{10,11... | collective-permute-start | bytes 393224 | tf_op jit(solution)/shard_map/ppermute | solution.py:26
  96.6 1.2 collective-permute-start.4
  134.3 4.5 %collective-permute-start.5 = (bf16[16,32,256]{2,1,0:T(8,128)(2,1)S(1)}, bf16[16,32,256]{2,1,0:T(8,128)(2,1)S(1)}, u32[]{:S(2)}, u32[]{:S(2)}) collective-permute-start(bf16[16,32,256]{2,1,0:T(8,128)(2,1)S(1)} %all_to_all.45.own_ref), channel_id=1, source_target_pairs={{0,1},{1,0},{2,3},{3,2},{4,5},{5,4},{6,7},{7,6},{8,9},{9,8},{10,11... | collective-permute-start | bytes 786440 | tf_op jit(solution)/shard_map/ppermute | solution.py:26
  169.3 9.9 %copy-start.6 = (bf16[64,512]{1,0:T(8,128)(2,1)S(1)}, bf16[64,512]{1,0:T(8,128)(2,1)}, u32[]{:S(2)}) copy-start(bf16[64,512]{1,0:T(8,128)(2,1)} %trial_ref.1) | copy-start | bytes 196612
  176.2 3.0 %collective-permute-start.6 = (bf16[512,64]{1,0:T(8,128)(2,1)S(1)}, bf16[512,64]{1,0:T(8,128)(2,1)S(1)}, u32[]{:S(2)}, u32[]{:S(2)}) collective-permute-start(bf16[512,64]{1,0:T(8,128)(2,1)S(1)} %get-tuple-element.17), channel_id=1, source_target_pairs={{0,1},{1,0},{2,3},{3,2},{4,5},{5,4},{6,7},{7,6},{8,9},{9,8},{10,11... | collective-permute-start | bytes 196616 | tf_op jit(solution)/shard_map/ppermute | solution.py:26
where the time goes:
time: 180 us
  blocking collectives  125 us (69%)
  Pallas kernels  31.1 us (17%)
  starting transfers between devices  14.2 us (8%)
  waiting for transfers between devices  5.4 us (3%)
  local copies, waits for them, and re-layouts  3.49 us (2%)
    all_to_all x8, blocking collectives, exchange(): return lax.all_to_all(array, axes, 0, 0, tiled=True)  125 us
    pallas_call x12, Pallas kernels, call(): pl.pallas_call(kernel, in_specs=[smem] * scalars + [VMEM] * (len(inputs)...  31.1 us
    ppermute x7, starting transfers between devices, swap_cores(): return lax.ppermute(array, 'core', [(0, 1), (1, 0)])  14.2 us
    ppermute x7, waiting for transfers between devices, swap_cores(): return lax.ppermute(array, 'core', [(0, 1), (1, 0)])  5.4 us
  transfers between devices with their start and end apart: 7, of which 5 were waited for; matrix products, arithmetic and copies ran while one was open for 0% of the time, Pallas kernels for 0%

commit v1 on v0

v1 whole, which is shorter than its diff:
```python
import functools

import jax
import jax.numpy as jnp
from jax import lax
from jax.experimental import pallas as pl
from jax.experimental.pallas import tpu as pltpu
from jax.sharding import Mesh, PartitionSpec as P

K = 32
CENTER = 2.0
HALF_WIDTH = 1.5

FINE = (("x", 4), ("zl", 2), ("zh", 4), ("y", 4), ("core", 2))
VAL = ("x", "zl")
RING = ("zh", "y")
PTS = ("zh", "y", "core")

BF16 = jnp.bfloat16
F32 = jnp.float32
VMEM = pl.BlockSpec(memory_space=pltpu.VMEM)
VMEM_LIMIT = 16 << 20
UNROLL = 2


def swap_cores(array):
    return lax.ppermute(array, "core", [(0, 1), (1, 0)])


def exchange(array, axes):
    return lax.all_to_all(array, axes, 0, 0, tiled=True)


def cost(flops, moved):
    return pl.CostEstimate(flops=int(flops), bytes_accessed=int(moved), transcendentals=0)


def call(kernel, inputs, outputs, flops, scalars=0):
    smem = pl.BlockSpec(memory_space=pltpu.SMEM)
    moved = sum(2 * a.size for a in inputs) + sum(2 * o.size for o in outputs)
    return pl.pallas_call(
        kernel,
        in_specs=[smem] * scalars + [VMEM] * (len(inputs) - scalars),
        out_specs=[VMEM] * len(outputs),
        out_shape=list(outputs),
        compiler_params=pltpu.CompilerParams(vmem_limit_bytes=VMEM_LIMIT),
        cost_estimate=cost(flops, moved),
    )(*inputs)


def shape(dims, dtype=BF16):
    return jax.ShapeDtypeStruct(tuple(dims), dtype)


def block_of(ref, g, h_ref, width):
    return ref[:, pl.ds(pl.multiple_of((2 * g + h_ref[0]) * width, width), width)]


def encode_points(h_ref, xt_refs, val_ref, cond_refs, out_ref, width):
    pieces, _, piece = out_ref.shape
    per_block = width // piece
    cols = min(256, piece)

    def block(g, carry):
        base = pl.multiple_of((2 * g + h_ref[0]) * width, width)
        for first in range(0, width, cols):
            at = pl.ds(pl.multiple_of(base + first, cols), cols)
            val = val_ref[:, at]
            total = jnp.zeros((K, cols), F32)
            for xt_ref, cond_ref in zip(xt_refs, cond_refs):
                cond = cond_ref[:, at].astype(F32)
                for c in range(0, cond.shape[0], 4):
                    part = jnp.dot(xt_ref[c * K : (c + 4) * K, :], val, preferred_element_type=F32)
                    for i in range(4):
                        total = total + part[i * K : (i + 1) * K] * cond[c + i : c + i + 1]
            out_ref[g * per_block + first // piece, :, first % piece : first % piece + cols] = total.astype(BF16)
        return carry

    lax.fori_loop(0, pieces // per_block, block, 0, unroll=UNROLL)


def encode_first(
    width,
    h_ref,
    own_ref,
    other_ref,
    gap_ref,
    gap_other_ref,
    val_ref,
    cond_ref,
    cond_other_ref,
    out_ref,
    xt_ref,
    xt_other_ref,
    scale_ref,
):
    conds = gap_ref.shape[0]
    scale_ref[:conds] = (gap_ref[...] - CENTER) * (1.0 / HALF_WIDTH)
    scale_ref[conds:] = (gap_other_ref[...] - CENTER) * (1.0 / HALF_WIDTH)
    xt_ref[...] = own_ref[...].astype(F32).T.astype(BF16)
    xt_other_ref[...] = other_ref[...].astype(F32).T.astype(BF16)
    encode_points(h_ref, (xt_ref, xt_other_ref), val_ref, (cond_ref, cond_other_ref), out_ref, width)


def stepped(xt, scale, coupled):
    scale = jnp.broadcast_to(scale[:, None, :], (scale.shape[0], K, scale.shape[1])).reshape(xt.shape)
    return xt.astype(F32) * scale + coupled * (2.0 / HALF_WIDTH)


def encode_next(
    width,
    h_ref,
    part_ref,
    recv_ref,
    old_ref,
    old_other_ref,
    scale_ref,
    val_ref,
    cond_ref,
    cond_other_ref,
    out_ref,
    xt_ref,
    xt_other_ref,
):
    half = old_ref.shape[0]
    conds = half // K
    for side, (old, new) in enumerate(((old_ref, xt_ref), (old_other_ref, xt_other_ref))):
        here = slice(side * half, (side + 1) * half)
        there = slice((1 - side) * half, (2 - side) * half)
        coupled = part_ref[here] + recv_ref[there].astype(F32)
        scale = scale_ref[side * conds : (side + 1) * conds]
        new[...] = stepped(old[...], scale, coupled).astype(BF16)
    encode_points(h_ref, (xt_ref, xt_other_ref), val_ref, (cond_ref, cond_other_ref), out_ref, width)


def encode(kernel, h, whole, orbitals, pieces, piece, width, *more):
    val_count, points = orbitals[0].shape
    rows = orbitals[1].shape[0] * K
    return call(
        functools.partial(kernel, width),
        (h, *whole, *orbitals),
        (shape((pieces, K, piece)), shape((rows, val_count)), shape((rows, val_count)), *more),
        2 * rows * val_count * points,
        1,
    )


def total_kernel(in_ref, out_ref):
    total = in_ref[0].astype(F32)
    for index in range(1, in_ref.shape[0]):
        total = total + in_ref[index].astype(F32)
    total = total.astype(BF16)
    for copy in range(out_ref.shape[0]):
        out_ref[copy] = total


def summed(array, copies):
    return call(total_kernel, (array,), (shape((copies, *array.shape[1:])),), array.size)[0]


def apply_kernel(pieces, width, h_ref, own_ref, other_ref, kernel_ref, out_ref):
    piece = own_ref.shape[2]
    even = h_ref[0] == 0

    def added(ref, q):
        total = ref[q].astype(F32)
        for index in range(q + pieces, ref.shape[0], pieces):
            total = total + ref[index].astype(F32)
        return total

    total = jnp.zeros((K, kernel_ref.shape[0]), F32)
    for q in range(pieces):
        own, other = added(own_ref, q), added(other_ref, q)
        for side in range(2):
            fit = jnp.where(even, own, other) if side == 0 else jnp.where(even, other, own)
            at = q * piece
            first = width * (2 * (at // width) + side) + at % width
            total = total + lax.dot_general(
                fit.astype(BF16),
                kernel_ref[:, first : first + piece],
                (((1,), (1,)), ((), ())),
                preferred_element_type=F32,
            )
    total = total.astype(BF16)
    for copy in range(out_ref.shape[0]):
        out_ref[copy] = total


def applied(h, own, other, kernel, pieces, copies):
    rows = kernel.shape[0]
    return call(
        functools.partial(apply_kernel, pieces, rows),
        (h, own, other, kernel),
        (shape((copies, K, rows)),),
        2 * K * kernel.size,
        1,
    )[0]


def stack_kernel(*refs):
    out_ref = refs[-1]
    for index, ref in enumerate(refs[:-1]):
        out_ref[index] = ref[0]


def stacked(arrays):
    return call(stack_kernel, arrays, (shape((len(arrays), *arrays[0].shape[1:])),), arrays[0].size)[0]


def decode_kernel(steps, y_step, sizes, more, h_ref, zh_ref, y_ref, field_ref, val_ref, cond_ref, cond_other_ref, *refs):
    part_ref = refs[1] if more else refs[0]
    width = field_ref.shape[2]
    y = lax.rem(y_ref[0] + sizes["y"] - y_step, sizes["y"])
    for index, z_step in enumerate(steps):
        g = lax.rem(zh_ref[0] + sizes["zh"] - z_step, sizes["zh"]) * sizes["y"] + y
        field = field_ref[index].astype(F32)
        val = block_of(val_ref, g, h_ref, width)
        row = 0
        for ref in (cond_ref, cond_other_ref):
            cond = block_of(ref, g, h_ref, width).astype(F32)
            for c in range(0, cond.shape[0], 4):
                pairs = jnp.concatenate([cond[c + i : c + i + 1] * field for i in range(4)], 0).astype(BF16)
                rows = slice(row, row + 4 * K)
                added = lax.dot_general(pairs, val, (((1,), (1,)), ((), ())), preferred_element_type=F32)
                if index == 0:
                    part_ref[rows, :] = refs[0][rows, :] + added if more else added
                else:
                    part_ref[rows, :] += added
                row += 4 * K
    if len(refs) > more + 1:
        send_ref = refs[-1]
        send_ref[...] = part_ref[part_ref.shape[0] - send_ref.shape[0] :].astype(BF16)


def behind(count):
    return sorted(range(1, count), key=lambda step: -min(step, count - step))


def shifted(array, axis, count, step):
    return lax.ppermute(array, axis, [(i, (i + step) % count) for i in range(count)])


def decode(field, place, orbitals, sizes, sent):
    val_count = orbitals[0].shape[0]
    rows = 2 * orbitals[1].shape[0] * K
    steps = [0, *behind(sizes["zh"])]
    field = stacked([field, *(shifted(field, "zh", sizes["zh"], step) for step in steps[1:])])
    far = behind(sizes["y"])
    fields = {step: shifted(field, "y", sizes["y"], step) for step in far}
    fields[0] = field
    parts = ()
    for y_step in (0, *reversed(far)):
        here = fields[y_step]
        outputs = (shape((rows, val_count), F32),)
        if y_step == far[0]:
            outputs += (shape((sent, val_count)),)
        parts = call(
            functools.partial(decode_kernel, steps, y_step, sizes, len(parts)),
            (*place, here, *orbitals, *parts),
            outputs,
            2 * rows * val_count * here.shape[0] * here.shape[2],
            len(place),
        )
    return parts


def turn_kernel(xt_ref, out_ref):
    out_ref[...] = xt_ref[...].astype(F32).T.astype(BF16)


def turned(xt):
    return call(turn_kernel, (xt,), (shape(xt.shape[::-1]),), xt.size)[0]


def finish_kernel(part_ref, recv_ref, xt_ref, scale_ref, trial_ref, out_ref):
    rows = recv_ref.shape[0]
    coupled = part_ref[:rows] + recv_ref[...].astype(F32)
    second = stepped(xt_ref[...], scale_ref[: rows // K], coupled)
    out_ref[...] = (2.0 * second.T - trial_ref[...].astype(F32)).astype(BF16)


def finish(part, recv, xt, scale, trial):
    return call(finish_kernel, (part, recv, xt, scale, trial), (shape(trial.shape),), 8 * trial.size)[0]


def field_of(encoded, h, kernel, sizes):
    ring = sizes["zh"] * sizes["y"]
    shares = exchange(encoded, (*VAL, "y"))
    shares = exchange(summed(shares, ring), RING)
    image = applied(h, shares, swap_cores(shares), kernel, sizes["y"], sizes["x"] * sizes["zl"])
    return summed(exchange(image, VAL), 1)


def on_device(sizes, trial, energy_gap, orb_val, orb_cond, kernel):
    width = kernel.shape[0]
    pieces = sizes["x"] * sizes["zl"] * sizes["y"]
    piece = kernel.shape[1] // 2 // sizes["y"]
    place = [lax.axis_index(axis).astype(jnp.int32).reshape(1) for axis in ("core", "zh", "y")]
    h = place[0]
    orbitals = (orb_val, orb_cond, swap_cores(orb_cond))
    gap = energy_gap.T
    whole = (trial, swap_cores(trial), gap, swap_cores(gap))
    scale = shape((2 * gap.shape[0], gap.shape[1]), F32)

    encoded, xt, xt_other, scale = encode(encode_first, h, whole, orbitals, pieces, piece, width, scale)
    field = field_of(encoded, h, kernel, sizes)
    part, sent = decode(field, place, orbitals, sizes, 2 * xt.shape[0])
    whole = (part, swap_cores(sent), xt, xt_other, scale)
    encoded, xt, _ = encode(encode_next, h, whole, orbitals, pieces, piece, width)
    first_step = turned(xt)
    field = field_of(encoded, h, kernel, sizes)
    part, sent = decode(field, place, orbitals, sizes, xt.shape[0])
    filtered = finish(part, swap_cores(sent), xt, scale, trial)
    return first_step, filtered


def build(mesh, fine):
    split = Mesh(mesh.devices.reshape([size for _, size in fine]), [name for name, _ in fine])
    placed = (P(VAL, PTS), P(VAL, PTS), P(VAL, None), P(PTS, None), P(PTS, VAL))
    return jax.shard_map(
        functools.partial(on_device, dict(fine)),
        mesh=split,
        in_specs=placed,
        out_specs=(P(VAL, PTS), P(VAL, PTS)),
        check_vma=False,
    )


def solution(mesh):
    return build(mesh, FINE)
```

time: 180 us -> 169 us (0.939)
  blocking collectives: 125 us -> 84.5 us
  starting transfers between devices: 14.2 us -> 34.2 us
  waiting for transfers between devices: 5.4 us -> 16.8 us
  Pallas kernels: 31.1 us -> 27.8 us
    all_to_all x8 -> x6, blocking collectives: 125 us -> 84.5 us  [exchange(): return lax.all_to_all(array, axes, 0, 0, tiled=True)]
    ppermute x0 -> x12, starting transfers between devices: none -> 15.4 us  [shifted(): lax.ppermute(array, axis, [(i, (i + step) % count) for i in range(count)])]
    ppermute x0 -> x12, waiting for transfers between devices: none -> 11.7 us  [shifted(): lax.ppermute(array, axis, [(i, (i + step) % count) for i in range(count)])]
    ppermute x7, starting transfers between devices: 14.2 us -> 18.9 us  [swap_cores(): return lax.ppermute(array, 'core', [(0, 1), (1, 0)])]
    pallas_call x12 -> x20, Pallas kernels: 31.1 us -> 27.8 us  [call(): pl.pallas_call(kernel, in_specs=[smem] * scalars + [VMEM] * (len(inputs)...]
    unnamed x16 -> x18, local copies, waits for them, and re-layouts: 3.49 us -> 4.19 us
  transfers between devices with their start and end apart: 7 -> 19, of which waited for: 5 -> 11; matrix products, arithmetic and copies ran while one was open for 0% -> 0% of each run, Pallas kernels for 0% -> 6%
where the time goes in v1:
time: 169 us; the launch traced here: 168 us
  blocking collectives  84.5 us (50%)
  starting transfers between devices  34.2 us (20%)
  Pallas kernels  27.8 us (16%)
  waiting for transfers between devices  16.8 us (10%)
  local copies, waits for them, and re-layouts  4.19 us (2%)
    all_to_all x6, blocking collectives, exchange(): return lax.all_to_all(array, axes, 0, 0, tiled=True)  84.5 us
    pallas_call x20, Pallas kernels, call(): pl.pallas_call(kernel, in_specs=[smem] * scalars + [VMEM] * (len(inputs)...  27.8 us
    ppermute x7, starting transfers between devices, swap_cores(): return lax.ppermute(array, 'core', [(0, 1), (1, 0)])  18.9 us
    ppermute x12, starting transfers between devices, shifted(): lax.ppermute(array, axis, [(i, (i + step) % count) for i in range(count)])  15.4 us
    ppermute x12, waiting for transfers between devices, shifted(): lax.ppermute(array, axis, [(i, (i + step) % count) for i in range(count)])  11.7 us
    ppermute x7, waiting for transfers between devices, swap_cores(): return lax.ppermute(array, 'core', [(0, 1), (1, 0)])  5.1 us
    unnamed x18, local copies, waits for them, and re-layouts  4.19 us
  transfers between devices with their start and end apart: 19, of which 11 were waited for; matrix products, arithmetic and copies ran while one was open for 0% of the time, Pallas kernels for 6%

profile of v1, /device:TPU:1, one launch (start us, length us, event | category | flops | bytes accessed | tf_op | source)
XLA Modules:
  0.0 168.3 jit_solution(14380557942539244744)
XLA Ops:
  0.6 3.3 %collective-permute-start.2 = (bf16[16,16384]{1,0:T(8,128)(2,1)}, bf16[16,16384]{1,0:T(8,128)(2,1)S(1)}, u32[]{:S(2)}, u32[]{:S(2)}) collective-permute-start(bf16[16,16384]{1,0:T(8,128)(2,1)} %cond_ref.19), channel_id=1, source_target_pairs={{0,1},{1,0},{2,3},{3,2},{4,5},{5,4},{6,7},{7,6},{8,9},{9,8},{10,11... | collective-permute-start | bytes 1572872 | tf_op jit(solution)/shard_map/ppermute | solution.py:27
  4.4 1.3 collective-permute-done.1.gap_other_ref
  5.8 1.6 copy-done
  7.4 1.0 copy-done.2
  8.4 0.8 copy-done.6
  9.9 5.7 %shard_map.68 = (bf16[32,32,256]{2,1,0:T(8,128)(2,1)S(1)}, bf16[512,64]{1,0:T(8,128)(2,1)S(1)}, bf16[512,64]{1,0:T(8,128)(2,1)S(1)}, f32[32,64]{1,0:T(8,128)S(1)}) custom-call(s32[1]{0:T(128)} %bitcast.h_ref, bf16[64,512]{1,0:T(8,128)(2,1)S(1)} %copy-done.6, bf16[64,512]{1,0:T(8,128)(2,1)S(1)} %collective-permute-done.other_ref, f32[16,64]{1,0:T(8,128)S(1)} %bitcast.5, ...), custom_call_target="tpu_custom_call" | custom-call | flops 1073741824 | bytes 3940354 | tf_op jit(solution)/shard_map/pallas_call | solution.py:41
  15.7 16.7 %all_to_all.30.in_ref = bf16[32,32,256]{2,1,0:T(8,128)(2,1)S(1)} all-to-all(bf16[32,32,256]{2,1,0:T(8,128)(2,1)S(1)} %get-tuple-element.12), channel_id=1, replica_groups=mesh['x'=4,'zl'=2,'zh'=4,'y'=4,'core'=2] {'x','zl','y'}, dimensions={0} | all-to-all | bytes 1048576 | tf_op jit(solution)/shard_map/all_to_all | solution.py:31
  32.5 19.5 %all_to_all.31.own_ref = bf16[16,32,256]{2,1,0:T(8,128)(2,1)S(1)} all-to-all(bf16[16,32,256]{2,1,0:T(8,128)(2,1)S(1)} %shard_map.69), channel_id=1, replica_groups=mesh['x'=4,'zl'=2,'zh'=4,'y'=4,'core'=2] {'zh','y'}, dimensions={0} | all-to-all | bytes 524288 | tf_op jit(solution)/shard_map/all_to_all | solution.py:31
  52.0 3.3 %collective-permute-start.3 = (bf16[16,32,256]{2,1,0:T(8,128)(2,1)S(1)}, bf16[16,32,256]{2,1,0:T(8,128)(2,1)S(1)}, u32[]{:S(2)}, u32[]{:S(2)}) collective-permute-start(bf16[16,32,256]{2,1,0:T(8,128)(2,1)S(1)} %all_to_all.31.own_ref), channel_id=1, source_target_pairs={{0,1},{1,0},{2,3},{3,2},{4,5},{5,4},{6,7},{7,6},{8,9},{9,8},{10,11... | collective-permute-start | bytes 786440 | tf_op jit(solution)/shard_map/ppermute | solution.py:27
  55.3 1.2 collective-permute-done.3.other_ref
  56.5 0.7 shard_map.70
  57.3 9.2 %all_to_all.32.in_ref = bf16[8,32,512]{2,1,0:T(8,128)(2,1)S(1)} all-to-all(bf16[8,32,512]{2,1,0:T(8,128)(2,1)S(1)} %shard_map.70), channel_id=1, replica_groups=mesh['x'=4,'zl'=2,'zh'=4,'y'=4,'core'=2] {'x','zl'}, dimensions={0} | all-to-all | bytes 524288 | tf_op jit(solution)/shard_map/all_to_all | solution.py:31
  66.5 1.6 collective-permute-start.6
  68.1 0.8 collective-permute-start.5
  68.9 2.3 %collective-permute-start.4 = (bf16[1,32,512]{2,1,0:T(8,128)(2,1)S(1)}, bf16[1,32,512]{2,1,0:T(8,128)(2,1)S(1)}, u32[]{:S(2)}, u32[]{:S(2)}) collective-permute-start(bf16[1,32,512]{2,1,0:T(8,128)(2,1)S(1)} %shard_map.71.refs_0_), channel_id=1, source_target_pairs={{0,16},{8,24},{16,0},{24,8},{1,17},{9,25},{17,1},{25,9},{2,18},{10... | collective-permute-start | bytes 98312 | tf_op jit(solution)/shard_map/ppermute | solution.py:240
  71.2 1.8 %collective-permute-done.5.refs_2_ = bf16[1,32,512]{2,1,0:T(8,128)(2,1)S(1)} collective-permute-done((bf16[1,32,512]{2,1,0:T(8,128)(2,1)S(1)}, bf16[1,32,512]{2,1,0:T(8,128)(2,1)S(1)}, u32[]{:S(2)}, u32[]{:S(2)}) %collective-permute-start.5) | collective-permute-done | bytes 32800 | tf_op jit(solution)/shard_map/ppermute | solution.py:240
  72.9 2.6 %collective-permute-done.4.refs_1_ = bf16[1,32,512]{2,1,0:T(8,128)(2,1)S(1)} collective-permute-done((bf16[1,32,512]{2,1,0:T(8,128)(2,1)S(1)}, bf16[1,32,512]{2,1,0:T(8,128)(2,1)S(1)}, u32[]{:S(2)}, u32[]{:S(2)}) %collective-permute-start.4) | collective-permute-done | bytes 32800 | tf_op jit(solution)/shard_map/ppermute | solution.py:240
  75.6 0.9 collective-permute-start.9
  77.1 1.5 collective-permute-start.7
  78.6 1.2 shard_map.73.refs_0_
  79.9 2.2 %shard_map.74.refs_0_ = f32[1024,64]{1,0:T(8,128)S(1)} custom-call(s32[1]{0:T(128)} %bitcast.h_ref, s32[1]{0:T(128)} %bitcast.1.zh_ref, s32[1]{0:T(128)} %bitcast.2.y_ref, bf16[4,32,512]{2,1,0:T(8,128)(2,1)} %collective-permute-done.9.field_ref, bf16[64,16384]{1,0:T(8,128)(2,1)S(1)} %copy-done.1, bf16[16,16384]{1,0:T(8,128)(2,1)S(1)} %copy-done.3, ...), custom_call_target="tpu_custom_call" | custom-call | flops 268435456 | bytes 3538950 | tf_op jit(solution)/shard_map/pallas_call | solution.py:41
  82.0 1.0 collective-permute-done.8.field_ref
  83.1 2.1 %shard_map.75.refs_0_ = f32[1024,64]{1,0:T(8,128)S(1)} custom-call(s32[1]{0:T(128)} %bitcast.h_ref, s32[1]{0:T(128)} %bitcast.1.zh_ref, s32[1]{0:T(128)} %bitcast.2.y_ref, bf16[4,32,512]{2,1,0:T(8,128)(2,1)} %collective-permute-done.8.field_ref, bf16[64,16384]{1,0:T(8,128)(2,1)S(1)} %copy-done.1, bf16[16,16384]{1,0:T(8,128)(2,1)S(1)} %copy-done.3, ...), custom_call_target="tpu_custom_call" | custom-call | flops 268435456 | bytes 3538950 | tf_op jit(solution)/shard_map/pallas_call | solution.py:41
  85.2 2.3 %shard_map.76 = (f32[1024,64]{1,0:T(8,128)S(1)}, bf16[1024,64]{1,0:T(8,128)(2,1)S(1)}) custom-call(s32[1]{0:T(128)} %bitcast.h_ref, s32[1]{0:T(128)} %bitcast.1.zh_ref, s32[1]{0:T(128)} %bitcast.2.y_ref, bf16[4,32,512]{2,1,0:T(8,128)(2,1)} %collective-permute-done.7.field_ref, bf16[64,16384]{1,0:T(8,128)(2,1)S(1)} %copy-done.1, ...), custom_call_target="tpu_custom_call" | custom-call | flops 268435456 | bytes 3670022 | tf_op jit(solution)/shard_map/pallas_call | solution.py:41
  87.5 4.9 %collective-permute-start.10 = (bf16[1024,64]{1,0:T(8,128)(2,1)S(1)}, bf16[1024,64]{1,0:T(8,128)(2,1)S(1)}, u32[]{:S(2)}, u32[]{:S(2)}) collective-permute-start(bf16[1024,64]{1,0:T(8,128)(2,1)S(1)} %get-tuple-element.14), channel_id=1, source_target_pairs={{0,1},{1,0},{2,3},{3,2},{4,5},{5,4},{6,7},{7,6},{8,9},{9,8},{10,11... | collective-permute-start | bytes 393224 | tf_op jit(solution)/shard_map/ppermute | solution.py:27
  92.3 1.2 collective-permute-done.10.recv_ref
  93.5 6.0 %shard_map.77 = (bf16[32,32,256]{2,1,0:T(8,128)(2,1)S(1)}, bf16[512,64]{1,0:T(8,128)(2,1)S(1)}, bf16[512,64]{1,0:T(8,128)(2,1)}) custom-call(s32[1]{0:T(128)} %bitcast.h_ref, f32[1024,64]{1,0:T(8,128)S(1)} %get-tuple-element.13.part_ref, bf16[1024,64]{1,0:T(8,128)(2,1)S(1)} %collective-permute-done.10.recv_ref, ...), custom_call_target="tpu_custom_call" | custom-call | flops 1073741824 | bytes 4198402 | tf_op jit(solution)/shard_map/pallas_call | solution.py:41
  99.5 14.2 %all_to_all.33.in_ref = bf16[32,32,256]{2,1,0:T(8,128)(2,1)S(1)} all-to-all(bf16[32,32,256]{2,1,0:T(8,128)(2,1)S(1)} %get-tuple-element.19), channel_id=1, replica_groups=mesh['x'=4,'zl'=2,'zh'=4,'y'=4,'core'=2] {'x','zl','y'}, dimensions={0} | all-to-all | bytes 1048576 | tf_op jit(solution)/shard_map/all_to_all | solution.py:31
  113.8 15.7 %all_to_all.34.own_ref = bf16[16,32,256]{2,1,0:T(8,128)(2,1)S(1)} all-to-all(bf16[16,32,256]{2,1,0:T(8,128)(2,1)S(1)} %shard_map.79), channel_id=1, replica_groups=mesh['x'=4,'zl'=2,'zh'=4,'y'=4,'core'=2] {'zh','y'}, dimensions={0} | all-to-all | bytes 524288 | tf_op jit(solution)/shard_map/all_to_all | solution.py:31
  129.5 3.3 %collective-permute-start.11 = (bf16[16,32,256]{2,1,0:T(8,128)(2,1)S(1)}, bf16[16,32,256]{2,1,0:T(8,128)(2,1)S(1)}, u32[]{:S(2)}, u32[]{:S(2)}) collective-permute-start(bf16[16,32,256]{2,1,0:T(8,128)(2,1)S(1)} %all_to_all.34.own_ref), channel_id=1, source_target_pairs={{0,1},{1,0},{2,3},{3,2},{4,5},{5,4},{6,7},{7,6},{8,9},{9,8},{10,11... | collective-permute-start | bytes 786440 | tf_op jit(solution)/shard_map/ppermute | solution.py:27
  132.8 1.2 collective-permute-done.11.other_ref
  134.0 0.7 shard_map.80
  134.7 9.2 %all_to_all.35.in_ref = bf16[8,32,512]{2,1,0:T(8,128)(2,1)S(1)} all-to-all(bf16[8,32,512]{2,1,0:T(8,128)(2,1)S(1)} %shard_map.80), channel_id=1, replica_groups=mesh['x'=4,'zl'=2,'zh'=4,'y'=4,'core'=2] {'x','zl'}, dimensions={0} | all-to-all | bytes 524288 | tf_op jit(solution)/shard_map/all_to_all | solution.py:31
  143.9 1.6 collective-permute-start.14
  145.5 0.8 collective-permute-start.13
  146.4 2.2 %collective-permute-start.12 = (bf16[1,32,512]{2,1,0:T(8,128)(2,1)S(1)}, bf16[1,32,512]{2,1,0:T(8,128)(2,1)S(1)}, u32[]{:S(2)}, u32[]{:S(2)}) collective-permute-start(bf16[1,32,512]{2,1,0:T(8,128)(2,1)S(1)} %shard_map.81.refs_0_), channel_id=1, source_target_pairs={{0,16},{8,24},{16,0},{24,8},{1,17},{9,25},{17,1},{25,9},{2,18},{10... | collective-permute-start | bytes 98312 | tf_op jit(solution)/shard_map/ppermute | solution.py:240
  148.6 1.8 %collective-permute-done.13.refs_2_ = bf16[1,32,512]{2,1,0:T(8,128)(2,1)S(1)} collective-permute-done((bf16[1,32,512]{2,1,0:T(8,128)(2,1)S(1)}, bf16[1,32,512]{2,1,0:T(8,128)(2,1)S(1)}, u32[]{:S(2)}, u32[]{:S(2)}) %collective-permute-start.13) | collective-permute-done | bytes 32800 | tf_op jit(solution)/shard_map/ppermute | solution.py:240
  150.4 2.6 %collective-permute-done.12.refs_1_ = bf16[1,32,512]{2,1,0:T(8,128)(2,1)S(1)} collective-permute-done((bf16[1,32,512]{2,1,0:T(8,128)(2,1)S(1)}, bf16[1,32,512]{2,1,0:T(8,128)(2,1)S(1)}, u32[]{:S(2)}, u32[]{:S(2)}) %collective-permute-start.12) | collective-permute-done | bytes 32800 | tf_op jit(solution)/shard_map/ppermute | solution.py:240
  153.1 0.9 collective-permute-start.17
  154.6 1.4 collective-permute-start.15
  156.0 1.2 shard_map.83.refs_0_
  157.3 1.3 shard_map.84.refs_0_
  158.5 1.8 %collective-permute-done.16.field_ref = bf16[4,32,512]{2,1,0:T(8,128)(2,1)S(1)} collective-permute-done((bf16[4,32,512]{2,1,0:T(8,128)(2,1)S(1)}, bf16[4,32,512]{2,1,0:T(8,128)(2,1)S(1)}, u32[]{:S(2)}, u32[]{:S(2)}) %collective-permute-start.16) | collective-permute-done | bytes 131104 | tf_op jit(solution)/shard_map/ppermute | solution.py:240
  160.4 1.2 shard_map.85.refs_0_
  161.7 1.3 shard_map.86
  163.0 3.6 %collective-permute-start.18 = (bf16[512,64]{1,0:T(8,128)(2,1)S(1)}, bf16[512,64]{1,0:T(8,128)(2,1)S(1)}, u32[]{:S(2)}, u32[]{:S(2)}) collective-permute-start(bf16[512,64]{1,0:T(8,128)(2,1)S(1)} %get-tuple-element.21), channel_id=1, source_target_pairs={{0,1},{1,0},{2,3},{3,2},{4,5},{5,4},{6,7},{7,6},{8,9},{9,8},{10,11... | collective-permute-start | bytes 196616 | tf_op jit(solution)/shard_map/ppermute | solution.py:27
  166.6 0.7 shard_map.78
  167.6 0.8 shard_map.87
  (34 shorter events, 3.1 us)
Async XLA Ops:
  0.6 5.1 %collective-permute-start.2 = (bf16[16,16384]{1,0:T(8,128)(2,1)}, bf16[16,16384]{1,0:T(8,128)(2,1)S(1)}, u32[]{:S(2)}, u32[]{:S(2)}) collective-permute-start(bf16[16,16384]{1,0:T(8,128)(2,1)} %cond_ref.19), channel_id=1, source_target_pairs={{0,1},{1,0},{2,3},{3,2},{4,5},{5,4},{6,7},{7,6},{8,9},{9,8},{10,11... | collective-permute-start | bytes 1572872 | tf_op jit(solution)/shard_map/ppermute | solution.py:27
  3.9 1.9 %collective-permute-start = (bf16[64,512]{1,0:T(8,128)(2,1)}, bf16[64,512]{1,0:T(8,128)(2,1)S(1)}, u32[]{:S(2)}, u32[]{:S(2)}) collective-permute-start(bf16[64,512]{1,0:T(8,128)(2,1)} %trial_ref.1), channel_id=1, source_target_pairs={{0,1},{1,0},{2,3},{3,2},{4,5},{5,4},{6,7},{7,6},{8,9},{9,8},{10,11... | collective-permute-start | bytes 196616 | tf_op jit(solution)/shard_map/ppermute | solution.py:27
  4.0 1.8 %collective-permute-start.1 = (f32[16,64]{1,0:T(8,128)}, f32[16,64]{1,0:T(8,128)S(1)}, u32[]{:S(2)}, u32[]{:S(2)}) collective-permute-start(f32[16,64]{1,0:T(8,128)} %bitcast.4), channel_id=1, source_target_pairs={{0,1},{1,0},{2,3},{3,2},{4,5},{5,4},{6,7},{7,6},{8,9},{9,8},{10,11... | collective-permute-start | bytes 12296 | tf_op jit(solution)/shard_map/ppermute | solution.py:27
  5.8 1.6 copy-start
  7.4 1.0 copy-start.2
  8.4 0.8 copy-start.6
  9.3 0.7 copy-start.8
  15.7 40.8 %copy-start.4 = (bf16[512,2048]{1,0:T(8,128)(2,1)S(1)}, bf16[512,2048]{1,0:T(8,128)(2,1)}, u32[]{:S(2)}) copy-start(bf16[512,2048]{1,0:T(8,128)(2,1)} %kernel_ref.3) | copy-start | bytes 6291460
  52.0 26.6 %copy-start.1 = (bf16[64,16384]{1,0:T(8,128)(2,1)S(1)}, bf16[64,16384]{1,0:T(8,128)(2,1)}, u32[]{:S(2)}) copy-start(bf16[64,16384]{1,0:T(8,128)(2,1)} %val_ref.19) | copy-start | bytes 6291460
  52.0 26.6 %copy-start.3 = (bf16[16,16384]{1,0:T(8,128)(2,1)S(1)}, bf16[16,16384]{1,0:T(8,128)(2,1)}, u32[]{:S(2)}) copy-start(bf16[16,16384]{1,0:T(8,128)(2,1)} %cond_ref.19) | copy-start | bytes 1572868
  52.0 4.5 %collective-permute-start.3 = (bf16[16,32,256]{2,1,0:T(8,128)(2,1)S(1)}, bf16[16,32,256]{2,1,0:T(8,128)(2,1)S(1)}, u32[]{:S(2)}, u32[]{:S(2)}) collective-permute-start(bf16[16,32,256]{2,1,0:T(8,128)(2,1)S(1)} %all_to_all.31.own_ref), channel_id=1, source_target_pairs={{0,1},{1,0},{2,3},{3,2},{4,5},{5,4},{6,7},{7,6},{8,9},{9,8},{10,11... | collective-permute-start | bytes 786440 | tf_op jit(solution)/shard_map/ppermute | solution.py:27
  66.5 4.7 %collective-permute-start.6 = (bf16[1,32,512]{2,1,0:T(8,128)(2,1)S(1)}, bf16[1,32,512]{2,1,0:T(8,128)(2,1)S(1)}, u32[]{:S(2)}, u32[]{:S(2)}) collective-permute-start(bf16[1,32,512]{2,1,0:T(8,128)(2,1)S(1)} %shard_map.71.refs_0_), channel_id=1, source_target_pairs={{0,24},{8,0},{16,8},{24,16},{1,25},{9,1},{17,9},{25,17},{2,26},{10... | collective-permute-start | bytes 98312 | tf_op jit(solution)/shard_map/ppermute | solution.py:240
  68.1 4.9 %collective-permute-start.5 = (bf16[1,32,512]{2,1,0:T(8,128)(2,1)S(1)}, bf16[1,32,512]{2,1,0:T(8,128)(2,1)S(1)}, u32[]{:S(2)}, u32[]{:S(2)}) collective-permute-start(bf16[1,32,512]{2,1,0:T(8,128)(2,1)S(1)} %shard_map.71.refs_0_), channel_id=1, source_target_pairs={{0,8},{8,16},{16,24},{24,0},{1,9},{9,17},{17,25},{25,1},{2,10},{10... | collective-permute-start | bytes 98312 | tf_op jit(solution)/shard_map/ppermute | solution.py:240
  68.9 6.7 %collective-permute-start.4 = (bf16[1,32,512]{2,1,0:T(8,128)(2,1)S(1)}, bf16[1,32,512]{2,1,0:T(8,128)(2,1)S(1)}, u32[]{:S(2)}, u32[]{:S(2)}) collective-permute-start(bf16[1,32,512]{2,1,0:T(8,128)(2,1)S(1)} %shard_map.71.refs_0_), channel_id=1, source_target_pairs={{0,16},{8,24},{16,0},{24,8},{1,17},{9,25},{17,1},{25,9},{2,18},{10... | collective-permute-start | bytes 98312 | tf_op jit(solution)/shard_map/ppermute | solution.py:240
  75.6 4.3 %collective-permute-start.9 = (bf16[4,32,512]{2,1,0:T(8,128)(2,1)S(1)}, bf16[4,32,512]{2,1,0:T(8,128)(2,1)}, u32[]{:S(2)}, u32[]{:S(2)}) collective-permute-start(bf16[4,32,512]{2,1,0:T(8,128)(2,1)S(1)} %shard_map.72.field_ref), channel_id=1, source_target_pairs={{0,6},{2,0},{4,2},{6,4},{1,7},{3,1},{5,3},{7,5},{8,14},{10,8},{12,... | collective-permute-start | bytes 393224 | tf_op jit(solution)/shard_map/ppermute | solution.py:240
  76.5 6.5 %collective-permute-start.8 = (bf16[4,32,512]{2,1,0:T(8,128)(2,1)S(1)}, bf16[4,32,512]{2,1,0:T(8,128)(2,1)}, u32[]{:S(2)}, u32[]{:S(2)}) collective-permute-start(bf16[4,32,512]{2,1,0:T(8,128)(2,1)S(1)} %shard_map.72.field_ref), channel_id=1, source_target_pairs={{0,2},{2,4},{4,6},{6,0},{1,3},{3,5},{5,7},{7,1},{8,10},{10,12},{12... | collective-permute-start | bytes 393224 | tf_op jit(solution)/shard_map/ppermute | solution.py:240
  77.1 8.1 %collective-permute-start.7 = (bf16[4,32,512]{2,1,0:T(8,128)(2,1)S(1)}, bf16[4,32,512]{2,1,0:T(8,128)(2,1)}, u32[]{:S(2)}, u32[]{:S(2)}) collective-permute-start(bf16[4,32,512]{2,1,0:T(8,128)(2,1)S(1)} %shard_map.72.field_ref), channel_id=1, source_target_pairs={{0,4},{2,6},{4,0},{6,2},{1,5},{3,7},{5,1},{7,3},{8,12},{10,14},{12... | collective-permute-start | bytes 393224 | tf_op jit(solution)/shard_map/ppermute | solution.py:240
  87.5 6.0 %collective-permute-start.10 = (bf16[1024,64]{1,0:T(8,128)(2,1)S(1)}, bf16[1024,64]{1,0:T(8,128)(2,1)S(1)}, u32[]{:S(2)}, u32[]{:S(2)}) collective-permute-start(bf16[1024,64]{1,0:T(8,128)(2,1)S(1)} %get-tuple-element.14), channel_id=1, source_target_pairs={{0,1},{1,0},{2,3},{3,2},{4,5},{5,4},{6,7},{7,6},{8,9},{9,8},{10,11... | collective-permute-start | bytes 393224 | tf_op jit(solution)/shard_map/ppermute | solution.py:27
  99.5 34.5 %copy-start.5 = (bf16[512,2048]{1,0:T(8,128)(2,1)S(1)}, bf16[512,2048]{1,0:T(8,128)(2,1)}, u32[]{:S(2)}) copy-start(bf16[512,2048]{1,0:T(8,128)(2,1)} %kernel_ref.3) | copy-start | bytes 6291460
  129.5 4.4 %collective-permute-start.11 = (bf16[16,32,256]{2,1,0:T(8,128)(2,1)S(1)}, bf16[16,32,256]{2,1,0:T(8,128)(2,1)S(1)}, u32[]{:S(2)}, u32[]{:S(2)}) collective-permute-start(bf16[16,32,256]{2,1,0:T(8,128)(2,1)S(1)} %all_to_all.34.own_ref), channel_id=1, source_target_pairs={{0,1},{1,0},{2,3},{3,2},{4,5},{5,4},{6,7},{7,6},{8,9},{9,8},{10,11... | collective-permute-start | bytes 786440 | tf_op jit(solution)/shard_map/ppermute | solution.py:27
  143.9 4.7 %collective-permute-start.14 = (bf16[1,32,512]{2,1,0:T(8,128)(2,1)S(1)}, bf16[1,32,512]{2,1,0:T(8,128)(2,1)S(1)}, u32[]{:S(2)}, u32[]{:S(2)}) collective-permute-start(bf16[1,32,512]{2,1,0:T(8,128)(2,1)S(1)} %shard_map.81.refs_0_), channel_id=1, source_target_pairs={{0,24},{8,0},{16,8},{24,16},{1,25},{9,1},{17,9},{25,17},{2,26},{10... | collective-permute-start | bytes 98312 | tf_op jit(solution)/shard_map/ppermute | solution.py:240
  145.5 4.9 %collective-permute-start.13 = (bf16[1,32,512]{2,1,0:T(8,128)(2,1)S(1)}, bf16[1,32,512]{2,1,0:T(8,128)(2,1)S(1)}, u32[]{:S(2)}, u32[]{:S(2)}) collective-permute-start(bf16[1,32,512]{2,1,0:T(8,128)(2,1)S(1)} %shard_map.81.refs_0_), channel_id=1, source_target_pairs={{0,8},{8,16},{16,24},{24,0},{1,9},{9,17},{17,25},{25,1},{2,10},{10... | collective-permute-start | bytes 98312 | tf_op jit(solution)/shard_map/ppermute | solution.py:240
  146.4 6.7 %collective-permute-start.12 = (bf16[1,32,512]{2,1,0:T(8,128)(2,1)S(1)}, bf16[1,32,512]{2,1,0:T(8,128)(2,1)S(1)}, u32[]{:S(2)}, u32[]{:S(2)}) collective-permute-start(bf16[1,32,512]{2,1,0:T(8,128)(2,1)S(1)} %shard_map.81.refs_0_), channel_id=1, source_target_pairs={{0,16},{8,24},{16,0},{24,8},{1,17},{9,25},{17,1},{25,9},{2,18},{10... | collective-permute-start | bytes 98312 | tf_op jit(solution)/shard_map/ppermute | solution.py:240
  153.1 4.2 %collective-permute-start.17 = (bf16[4,32,512]{2,1,0:T(8,128)(2,1)S(1)}, bf16[4,32,512]{2,1,0:T(8,128)(2,1)S(1)}, u32[]{:S(2)}, u32[]{:S(2)}) collective-permute-start(bf16[4,32,512]{2,1,0:T(8,128)(2,1)S(1)} %shard_map.82.field_ref), channel_id=1, source_target_pairs={{0,6},{2,0},{4,2},{6,4},{1,7},{3,1},{5,3},{7,5},{8,14},{10,8},{12,... | collective-permute-start | bytes 393224 | tf_op jit(solution)/shard_map/ppermute | solution.py:240
  154.0 6.4 %collective-permute-start.16 = (bf16[4,32,512]{2,1,0:T(8,128)(2,1)S(1)}, bf16[4,32,512]{2,1,0:T(8,128)(2,1)S(1)}, u32[]{:S(2)}, u32[]{:S(2)}) collective-permute-start(bf16[4,32,512]{2,1,0:T(8,128)(2,1)S(1)} %shard_map.82.field_ref), channel_id=1, source_target_pairs={{0,2},{2,4},{4,6},{6,0},{1,3},{3,5},{5,7},{7,1},{8,10},{10,12},{12... | collective-permute-start | bytes 393224 | tf_op jit(solution)/shard_map/ppermute | solution.py:240
  154.6 7.0 %collective-permute-start.15 = (bf16[4,32,512]{2,1,0:T(8,128)(2,1)S(1)}, bf16[4,32,512]{2,1,0:T(8,128)(2,1)S(1)}, u32[]{:S(2)}, u32[]{:S(2)}) collective-permute-start(bf16[4,32,512]{2,1,0:T(8,128)(2,1)S(1)} %shard_map.82.field_ref), channel_id=1, source_target_pairs={{0,4},{2,6},{4,0},{6,2},{1,5},{3,7},{5,1},{7,3},{8,12},{10,14},{12... | collective-permute-start | bytes 393224 | tf_op jit(solution)/shard_map/ppermute | solution.py:240
  161.6 5.9 %copy-start.7 = (bf16[64,512]{1,0:T(8,128)(2,1)S(1)}, bf16[64,512]{1,0:T(8,128)(2,1)}, u32[]{:S(2)}) copy-start(bf16[64,512]{1,0:T(8,128)(2,1)} %trial_ref.1) | copy-start | bytes 196612
  163.0 4.6 %collective-permute-start.18 = (bf16[512,64]{1,0:T(8,128)(2,1)S(1)}, bf16[512,64]{1,0:T(8,128)(2,1)S(1)}, u32[]{:S(2)}, u32[]{:S(2)}) collective-permute-start(bf16[512,64]{1,0:T(8,128)(2,1)S(1)} %get-tuple-element.21), channel_id=1, source_target_pairs={{0,1},{1,0},{2,3},{3,2},{4,5},{5,4},{6,7},{7,6},{8,9},{9,8},{10,11... | collective-permute-start | bytes 196616 | tf_op jit(solution)/shard_map/ppermute | solution.py:27

commit v2 on v1

--- a/solution.py
+++ b/solution.py
@@ -21,6 +21,7 @@
 VMEM = pl.BlockSpec(memory_space=pltpu.VMEM)
 VMEM_LIMIT = 16 << 20
 UNROLL = 2
+START_FLOPS = 4_000_000_000
 
 
 def swap_cores(array):
@@ -79,26 +80,7 @@
     lax.fori_loop(0, pieces // per_block, block, 0, unroll=UNROLL)
 
 
-def encode_first(
-    width,
-    h_ref,
-    own_ref,
-    other_ref,
-    gap_ref,
-    gap_other_ref,
-    val_ref,
-    cond_ref,
-    cond_other_ref,
-    out_ref,
-    xt_ref,
-    xt_other_ref,
-    scale_ref,
-):
-    conds = gap_ref.shape[0]
-    scale_ref[:conds] = (gap_ref[...] - CENTER) * (1.0 / HALF_WIDTH)
-    scale_ref[conds:] = (gap_other_ref[...] - CENTER) * (1.0 / HALF_WIDTH)
-    xt_ref[...] = own_ref[...].astype(F32).T.astype(BF16)
-    xt_other_ref[...] = other_ref[...].astype(F32).T.astype(BF16)
+def encode_first(width, h_ref, xt_ref, xt_other_ref, val_ref, cond_ref, cond_other_ref, out_ref):
     encode_points(h_ref, (xt_ref, xt_other_ref), val_ref, (cond_ref, cond_other_ref), out_ref, width)
 
 
@@ -115,6 +97,7 @@
     old_ref,
     old_other_ref,
     scale_ref,
+    scale_other_ref,
     val_ref,
     cond_ref,
     cond_other_ref,
@@ -123,13 +106,12 @@
     xt_other_ref,
 ):
     half = old_ref.shape[0]
-    conds = half // K
-    for side, (old, new) in enumerate(((old_ref, xt_ref), (old_other_ref, xt_other_ref))):
+    sides = ((old_ref, scale_ref, xt_ref), (old_other_ref, scale_other_ref, xt_other_ref))
+    for side, (old, scale, new) in enumerate(sides):
         here = slice(side * half, (side + 1) * half)
         there = slice((1 - side) * half, (2 - side) * half)
         coupled = part_ref[here] + recv_ref[there].astype(F32)
-        scale = scale_ref[side * conds : (side + 1) * conds]
-        new[...] = stepped(old[...], scale, coupled).astype(BF16)
+        new[...] = stepped(old[...], scale[...], coupled).astype(BF16)
     encode_points(h_ref, (xt_ref, xt_other_ref), val_ref, (cond_ref, cond_other_ref), out_ref, width)
 
 
@@ -139,7 +121,7 @@
     return call(
         functools.partial(kernel, width),
         (h, *whole, *orbitals),
-        (shape((pieces, K, piece)), shape((rows, val_count)), shape((rows, val_count)), *more),
+        (shape((pieces, K, piece)), *more),
         2 * rows * val_count * points,
         1,
     )
@@ -207,12 +189,11 @@
     return call(stack_kernel, arrays, (shape((len(arrays), *arrays[0].shape[1:])),), arrays[0].size)[0]
 
 
-def decode_kernel(steps, y_step, sizes, more, h_ref, zh_ref, y_ref, field_ref, val_ref, cond_ref, cond_other_ref, *refs):
-    part_ref = refs[1] if more else refs[0]
+def decode_kernel(steps, sizes, h_ref, zh_ref, y_ref, field_ref, val_ref, cond_ref, cond_other_ref, *refs):
+    *before, part_ref, send_ref = (*refs, None) if len(refs) == 1 else refs
     width = field_ref.shape[2]
-    y = lax.rem(y_ref[0] + sizes["y"] - y_step, sizes["y"])
     for index, z_step in enumerate(steps):
-        g = lax.rem(zh_ref[0] + sizes["zh"] - z_step, sizes["zh"]) * sizes["y"] + y
+        g = lax.rem(zh_ref[0] + sizes["zh"] - z_step, sizes["zh"]) * sizes["y"] + y_ref[0]
         field = field_ref[index].astype(F32)
         val = block_of(val_ref, g, h_ref, width)
         row = 0
@@ -223,12 +204,11 @@
                 rows = slice(row, row + 4 * K)
                 added = lax.dot_general(pairs, val, (((1,), (1,)), ((), ())), preferred_element_type=F32)
                 if index == 0:
-                    part_ref[rows, :] = refs[0][rows, :] + added if more else added
+                    part_ref[rows, :] = before[0][rows, :] + added if before else added
                 else:
                     part_ref[rows, :] += added
                 row += 4 * K
-    if len(refs) > more + 1:
-        send_ref = refs[-1]
+    if send_ref is not None:
         send_ref[...] = part_ref[part_ref.shape[0] - send_ref.shape[0] :].astype(BF16)
 
 
@@ -243,20 +223,21 @@
 def decode(field, place, orbitals, sizes, sent):
     val_count = orbitals[0].shape[0]
     rows = 2 * orbitals[1].shape[0] * K
-    steps = [0, *behind(sizes["zh"])]
+    steps = [0, *reversed(behind(sizes["zh"]))]
     field = stacked([field, *(shifted(field, "zh", sizes["zh"], step) for step in steps[1:])])
     far = behind(sizes["y"])
     fields = {step: shifted(field, "y", sizes["y"], step) for step in far}
     fields[0] = field
+    h, zh, y = place
     parts = ()
     for y_step in (0, *reversed(far)):
         here = fields[y_step]
         outputs = (shape((rows, val_count), F32),)
-        if y_step == far[0]:
+        if y_step:
             outputs += (shape((sent, val_count)),)
         parts = call(
-            functools.partial(decode_kernel, steps, y_step, sizes, len(parts)),
-            (*place, here, *orbitals, *parts),
+            functools.partial(decode_kernel, tuple(steps), sizes),
+            (h, zh, lax.rem(y + (sizes["y"] - y_step), sizes["y"]), here, *orbitals, *parts[:1]),
             outputs,
             2 * rows * val_count * here.shape[0] * here.shape[2],
             len(place),
@@ -264,6 +245,15 @@
     return parts
 
 
+def start_kernel(trial_ref, gap_ref, xt_ref, scale_ref):
+    xt_ref[...] = trial_ref[...].astype(F32).T.astype(BF16)
+    scale_ref[...] = (gap_ref[...] - CENTER) * (1.0 / HALF_WIDTH)
+
+
+def started(trial, gap):
+    return call(start_kernel, (trial, gap), (shape(trial.shape[::-1]), shape(gap.shape, F32)), START_FLOPS)
+
+
 def turn_kernel(xt_ref, out_ref):
     out_ref[...] = xt_ref[...].astype(F32).T.astype(BF16)
 
@@ -275,7 +265,7 @@
 def finish_kernel(part_ref, recv_ref, xt_ref, scale_ref, trial_ref, out_ref):
     rows = recv_ref.shape[0]
     coupled = part_ref[:rows] + recv_ref[...].astype(F32)
-    second = stepped(xt_ref[...], scale_ref[: rows // K], coupled)
+    second = stepped(xt_ref[...], scale_ref[...], coupled)
     out_ref[...] = (2.0 * second.T - trial_ref[...].astype(F32)).astype(BF16)
 
 
@@ -298,15 +288,15 @@
     place = [lax.axis_index(axis).astype(jnp.int32).reshape(1) for axis in ("core", "zh", "y")]
     h = place[0]
     orbitals = (orb_val, orb_cond, swap_cores(orb_cond))
-    gap = energy_gap.T
-    whole = (trial, swap_cores(trial), gap, swap_cores(gap))
-    scale = shape((2 * gap.shape[0], gap.shape[1]), F32)
-
-    encoded, xt, xt_other, scale = encode(encode_first, h, whole, orbitals, pieces, piece, width, scale)
+    xt, scale = started(trial, energy_gap.T)
+    xt_other, scale_other = swap_cores(xt), swap_cores(scale)
+
+    encoded = encode(encode_first, h, (xt, xt_other), orbitals, pieces, piece, width)[0]
     field = field_of(encoded, h, kernel, sizes)
     part, sent = decode(field, place, orbitals, sizes, 2 * xt.shape[0])
-    whole = (part, swap_cores(sent), xt, xt_other, scale)
-    encoded, xt, _ = encode(encode_next, h, whole, orbitals, pieces, piece, width)
+    whole = (part, swap_cores(sent), xt, xt_other, scale, scale_other)
+    states = (shape(xt.shape), shape(xt.shape))
+    encoded, xt, _ = encode(encode_next, h, whole, orbitals, pieces, piece, width, *states)
     first_step = turned(xt)
     field = field_of(encoded, h, kernel, sizes)
     part, sent = decode(field, place, orbitals, sizes, xt.shape[0])

time: 169 us -> 168 us (level)
  Pallas kernels: 27.8 us -> 30.8 us
  local copies, waits for them, and re-layouts: 4.19 us -> 1.67 us
    pallas_call x20 -> x21, Pallas kernels: 27.8 us -> 30.8 us  [call(): pl.pallas_call(kernel, in_specs=[smem] * scalars + [VMEM] * (len(inputs)...]
    unnamed x18 -> x14, local copies, waits for them, and re-layouts: 4.19 us -> 1.67 us
  transfers between devices with their start and end apart: 19 -> 19, of which waited for: 11 -> 11; matrix products, arithmetic and copies ran while one was open for 0% -> 0% of each run, Pallas kernels for 6% -> 8%
where the time goes in v2:
time: 168 us
  blocking collectives  85.4 us (51%)
  starting transfers between devices  33.5 us (20%)
  Pallas kernels  30.8 us (18%)
  waiting for transfers between devices  15.6 us (9%)
    all_to_all x6, blocking collectives, exchange(): return lax.all_to_all(array, axes, 0, 0, tiled=True)  85.4 us
    pallas_call x21, Pallas kernels, call(): pl.pallas_call(kernel, in_specs=[smem] * scalars + [VMEM] * (len(inputs)...  30.8 us
    ppermute x7, starting transfers between devices, swap_cores(): return lax.ppermute(array, 'core', [(0, 1), (1, 0)])  18.2 us
    ppermute x12, starting transfers between devices, shifted(): lax.ppermute(array, axis, [(i, (i + step) % count) for i in range(count)])  15.3 us
    ppermute x12, waiting for transfers between devices, shifted(): lax.ppermute(array, axis, [(i, (i + step) % count) for i in range(count)])  10.6 us
    ppermute x7, waiting for transfers between devices, swap_cores(): return lax.ppermute(array, 'core', [(0, 1), (1, 0)])  5 us
  transfers between devices with their start and end apart: 19, of which 11 were waited for; matrix products, arithmetic and copies ran while one was open for 0% of the time, Pallas kernels for 8%

profile of v2, /device:TPU:1, one launch (start us, length us, event | category | flops | bytes accessed | tf_op | source)
XLA Modules:
  0.0 167.6 jit_solution(4566157820019244855)
XLA Ops:
  0.6 3.3 %collective-permute-start.1 = (bf16[16,16384]{1,0:T(8,128)(2,1)}, bf16[16,16384]{1,0:T(8,128)(2,1)S(1)}, u32[]{:S(2)}, u32[]{:S(2)}) collective-permute-start(bf16[16,16384]{1,0:T(8,128)(2,1)} %cond_ref.19), channel_id=1, source_target_pairs={{0,1},{1,0},{2,3},{3,2},{4,5},{5,4},{6,7},{7,6},{8,9},{9,8},{10,11... | collective-permute-start | bytes 1572872 | tf_op jit(solution)/shard_map/ppermute | solution.py:28
  3.9 0.8 copy-done.4
  4.8 0.7 copy-done.6
  5.7 1.3 collective-permute-done.xt_other_ref.old_other_ref
  7.1 5.6 %shard_map.69 = bf16[32,32,256]{2,1,0:T(8,128)(2,1)S(1)} custom-call(s32[1]{0:T(128)} %bitcast.h_ref, bf16[512,64]{1,0:T(8,128)(2,1)S(1)} %get-tuple-element.14.xt_ref.old_ref, bf16[512,64]{1,0:T(8,128)(2,1)S(1)} %collective-permute-done.xt_other_ref.old_other_ref, bf16[64,16384]{1,0:T(8,128)(2,1)S(1)} %copy-done, bf16[16,16384]{1,0:T(8,128)(2,1)S(1)} %copy-done.1, ...), custom_call_target="tpu_custom_call" | custom-call | flops 1073741824 | bytes 3801090 | tf_op jit(solution)/shard_map/pallas_call | solution.py:42
  12.7 17.1 %all_to_all.30.in_ref = bf16[32,32,256]{2,1,0:T(8,128)(2,1)S(1)} all-to-all(bf16[32,32,256]{2,1,0:T(8,128)(2,1)S(1)} %shard_map.69), channel_id=1, replica_groups=mesh['x'=4,'zl'=2,'zh'=4,'y'=4,'core'=2] {'x','zl','y'}, dimensions={0} | all-to-all | bytes 1048576 | tf_op jit(solution)/shard_map/all_to_all | solution.py:32
  30.0 19.4 %all_to_all.31.own_ref = bf16[16,32,256]{2,1,0:T(8,128)(2,1)S(1)} all-to-all(bf16[16,32,256]{2,1,0:T(8,128)(2,1)S(1)} %shard_map.70), channel_id=1, replica_groups=mesh['x'=4,'zl'=2,'zh'=4,'y'=4,'core'=2] {'zh','y'}, dimensions={0} | all-to-all | bytes 524288 | tf_op jit(solution)/shard_map/all_to_all | solution.py:32
  49.3 3.4 %collective-permute-start.2 = (bf16[16,32,256]{2,1,0:T(8,128)(2,1)S(1)}, bf16[16,32,256]{2,1,0:T(8,128)(2,1)S(1)}, u32[]{:S(2)}, u32[]{:S(2)}) collective-permute-start(bf16[16,32,256]{2,1,0:T(8,128)(2,1)S(1)} %all_to_all.31.own_ref), channel_id=1, source_target_pairs={{0,1},{1,0},{2,3},{3,2},{4,5},{5,4},{6,7},{7,6},{8,9},{9,8},{10,11... | collective-permute-start | bytes 786440 | tf_op jit(solution)/shard_map/ppermute | solution.py:28
  52.7 1.2 collective-permute-done.2.other_ref
  53.9 0.7 shard_map.71
  54.6 9.4 %all_to_all.32.in_ref = bf16[8,32,512]{2,1,0:T(8,128)(2,1)S(1)} all-to-all(bf16[8,32,512]{2,1,0:T(8,128)(2,1)S(1)} %shard_map.71), channel_id=1, replica_groups=mesh['x'=4,'zl'=2,'zh'=4,'y'=4,'core'=2] {'x','zl'}, dimensions={0} | all-to-all | bytes 524288 | tf_op jit(solution)/shard_map/all_to_all | solution.py:32
  64.1 1.3 collective-permute-start.3
  65.4 1.1 collective-permute-start.4
  66.5 1.9 %collective-permute-start.5 = (bf16[1,32,512]{2,1,0:T(8,128)(2,1)S(1)}, bf16[1,32,512]{2,1,0:T(8,128)(2,1)S(1)}, u32[]{:S(2)}, u32[]{:S(2)}) collective-permute-start(bf16[1,32,512]{2,1,0:T(8,128)(2,1)S(1)} %shard_map.72.refs_0_), channel_id=1, source_target_pairs={{0,16},{8,24},{16,0},{24,8},{1,17},{9,25},{17,1},{25,9},{2,18},{10... | collective-permute-start | bytes 98312 | tf_op jit(solution)/shard_map/ppermute | solution.py:220
  68.5 1.8 %collective-permute-done.4.refs_2_ = bf16[1,32,512]{2,1,0:T(8,128)(2,1)S(1)} collective-permute-done((bf16[1,32,512]{2,1,0:T(8,128)(2,1)S(1)}, bf16[1,32,512]{2,1,0:T(8,128)(2,1)S(1)}, u32[]{:S(2)}, u32[]{:S(2)}) %collective-permute-start.4) | collective-permute-done | bytes 32800 | tf_op jit(solution)/shard_map/ppermute | solution.py:220
  70.3 2.9 %collective-permute-done.5.refs_3_ = bf16[1,32,512]{2,1,0:T(8,128)(2,1)S(1)} collective-permute-done((bf16[1,32,512]{2,1,0:T(8,128)(2,1)S(1)}, bf16[1,32,512]{2,1,0:T(8,128)(2,1)S(1)}, u32[]{:S(2)}, u32[]{:S(2)}) %collective-permute-start.5) | collective-permute-done | bytes 32800 | tf_op jit(solution)/shard_map/ppermute | solution.py:220
  73.2 1.2 collective-permute-start.8
  74.4 0.4 collective-permute-start.7
  74.8 1.7 %collective-permute-start.6 = (bf16[4,32,512]{2,1,0:T(8,128)(2,1)S(1)}, bf16[4,32,512]{2,1,0:T(8,128)(2,1)}, u32[]{:S(2)}, u32[]{:S(2)}) collective-permute-start(bf16[4,32,512]{2,1,0:T(8,128)(2,1)S(1)} %shard_map.73.field_ref), channel_id=1, source_target_pairs={{0,4},{2,6},{4,0},{6,2},{1,5},{3,7},{5,1},{7,3},{8,12},{10,14},{12... | collective-permute-start | bytes 393224 | tf_op jit(solution)/shard_map/ppermute | solution.py:220
  76.5 1.2 shard_map.74.refs_0_
  77.7 2.9 %shard_map.75 = (f32[1024,64]{1,0:T(8,128)S(1)}, bf16[1024,64]{1,0:T(8,128)(2,1)}) custom-call(s32[1]{0:T(128)} %bitcast.h_ref, s32[1]{0:T(128)} %bitcast.1.zh_ref, s32[1]{0:T(128)S(6)} %rem.73.y_ref, bf16[4,32,512]{2,1,0:T(8,128)(2,1)} %collective-permute-done.8.field_ref, bf16[64,16384]{1,0:T(8,128)(2,1)S(1)} %copy-done, bf16[16,16384]{1,0:T(8,128)(2,1)S(1)} %copy-done.1, ...), custom_call_target="tpu_custom_call" | custom-call | flops 268435456 | bytes 3670022 | tf_op jit(solution)/shard_map/pallas_call | solution.py:42
  81.0 2.9 %shard_map.76 = (f32[1024,64]{1,0:T(8,128)S(1)}, bf16[1024,64]{1,0:T(8,128)(2,1)}) custom-call(s32[1]{0:T(128)} %bitcast.h_ref, s32[1]{0:T(128)} %bitcast.1.zh_ref, s32[1]{0:T(128)S(6)} %rem.67.y_ref, bf16[4,32,512]{2,1,0:T(8,128)(2,1)} %collective-permute-done.7.field_ref, bf16[64,16384]{1,0:T(8,128)(2,1)S(1)} %copy-done, bf16[16,16384]{1,0:T(8,128)(2,1)S(1)} %copy-done.1, ...), custom_call_target="tpu_custom_call" | custom-call | flops 268435456 | bytes 3670022 | tf_op jit(solution)/shard_map/pallas_call | solution.py:42
  83.9 2.3 %shard_map.77 = (f32[1024,64]{1,0:T(8,128)S(1)}, bf16[1024,64]{1,0:T(8,128)(2,1)S(1)}) custom-call(s32[1]{0:T(128)} %bitcast.h_ref, s32[1]{0:T(128)} %bitcast.1.zh_ref, s32[1]{0:T(128)S(6)} %rem.61.y_ref, bf16[4,32,512]{2,1,0:T(8,128)(2,1)} %collective-permute-done.6.field_ref, bf16[64,16384]{1,0:T(8,128)(2,1)S(1)} %copy-done, ...), custom_call_target="tpu_custom_call" | custom-call | flops 268435456 | bytes 3670022 | tf_op jit(solution)/shard_map/pallas_call | solution.py:42
  86.2 4.6 %collective-permute-start.9 = (bf16[1024,64]{1,0:T(8,128)(2,1)S(1)}, bf16[1024,64]{1,0:T(8,128)(2,1)S(1)}, u32[]{:S(2)}, u32[]{:S(2)}) collective-permute-start(bf16[1024,64]{1,0:T(8,128)(2,1)S(1)} %get-tuple-element.18), channel_id=1, source_target_pairs={{0,1},{1,0},{2,3},{3,2},{4,5},{5,4},{6,7},{7,6},{8,9},{9,8},{10,11... | collective-permute-start | bytes 393224 | tf_op jit(solution)/shard_map/ppermute | solution.py:28
  90.8 1.1 collective-permute-done.10.scale_other_ref
  91.9 6.0 %shard_map.78 = (bf16[32,32,256]{2,1,0:T(8,128)(2,1)S(1)}, bf16[512,64]{1,0:T(8,128)(2,1)S(1)}, bf16[512,64]{1,0:T(8,128)(2,1)}) custom-call(s32[1]{0:T(128)} %bitcast.h_ref, f32[1024,64]{1,0:T(8,128)S(1)} %get-tuple-element.17.part_ref, bf16[1024,64]{1,0:T(8,128)(2,1)S(1)} %collective-permute-done.9.recv_ref, ...), custom_call_target="tpu_custom_call" | custom-call | flops 1073741824 | bytes 4198402 | tf_op jit(solution)/shard_map/pallas_call | solution.py:42
  97.9 14.8 %all_to_all.33.in_ref = bf16[32,32,256]{2,1,0:T(8,128)(2,1)S(1)} all-to-all(bf16[32,32,256]{2,1,0:T(8,128)(2,1)S(1)} %get-tuple-element.21), channel_id=1, replica_groups=mesh['x'=4,'zl'=2,'zh'=4,'y'=4,'core'=2] {'x','zl','y'}, dimensions={0} | all-to-all | bytes 1048576 | tf_op jit(solution)/shard_map/all_to_all | solution.py:32
  112.8 15.5 %all_to_all.34.own_ref = bf16[16,32,256]{2,1,0:T(8,128)(2,1)S(1)} all-to-all(bf16[16,32,256]{2,1,0:T(8,128)(2,1)S(1)} %shard_map.80), channel_id=1, replica_groups=mesh['x'=4,'zl'=2,'zh'=4,'y'=4,'core'=2] {'zh','y'}, dimensions={0} | all-to-all | bytes 524288 | tf_op jit(solution)/shard_map/all_to_all | solution.py:32
  128.3 3.3 %collective-permute-start.11 = (bf16[16,32,256]{2,1,0:T(8,128)(2,1)S(1)}, bf16[16,32,256]{2,1,0:T(8,128)(2,1)S(1)}, u32[]{:S(2)}, u32[]{:S(2)}) collective-permute-start(bf16[16,32,256]{2,1,0:T(8,128)(2,1)S(1)} %all_to_all.34.own_ref), channel_id=1, source_target_pairs={{0,1},{1,0},{2,3},{3,2},{4,5},{5,4},{6,7},{7,6},{8,9},{9,8},{10,11... | collective-permute-start | bytes 786440 | tf_op jit(solution)/shard_map/ppermute | solution.py:28
  131.6 1.2 collective-permute-done.11.other_ref
  132.7 0.7 shard_map.81
  133.5 9.2 %all_to_all.35.in_ref = bf16[8,32,512]{2,1,0:T(8,128)(2,1)S(1)} all-to-all(bf16[8,32,512]{2,1,0:T(8,128)(2,1)S(1)} %shard_map.81), channel_id=1, replica_groups=mesh['x'=4,'zl'=2,'zh'=4,'y'=4,'core'=2] {'x','zl'}, dimensions={0} | all-to-all | bytes 524288 | tf_op jit(solution)/shard_map/all_to_all | solution.py:32
  142.7 1.6 collective-permute-start.12
  144.3 0.8 collective-permute-start.13
  145.1 2.2 %collective-permute-start.14 = (bf16[1,32,512]{2,1,0:T(8,128)(2,1)S(1)}, bf16[1,32,512]{2,1,0:T(8,128)(2,1)S(1)}, u32[]{:S(2)}, u32[]{:S(2)}) collective-permute-start(bf16[1,32,512]{2,1,0:T(8,128)(2,1)S(1)} %shard_map.82.refs_0_), channel_id=1, source_target_pairs={{0,16},{8,24},{16,0},{24,8},{1,17},{9,25},{17,1},{25,9},{2,18},{10... | collective-permute-start | bytes 98312 | tf_op jit(solution)/shard_map/ppermute | solution.py:220
  147.4 1.8 %collective-permute-done.13.refs_2_ = bf16[1,32,512]{2,1,0:T(8,128)(2,1)S(1)} collective-permute-done((bf16[1,32,512]{2,1,0:T(8,128)(2,1)S(1)}, bf16[1,32,512]{2,1,0:T(8,128)(2,1)S(1)}, u32[]{:S(2)}, u32[]{:S(2)}) %collective-permute-start.13) | collective-permute-done | bytes 32800 | tf_op jit(solution)/shard_map/ppermute | solution.py:220
  149.2 2.6 %collective-permute-done.14.refs_3_ = bf16[1,32,512]{2,1,0:T(8,128)(2,1)S(1)} collective-permute-done((bf16[1,32,512]{2,1,0:T(8,128)(2,1)S(1)}, bf16[1,32,512]{2,1,0:T(8,128)(2,1)S(1)}, u32[]{:S(2)}, u32[]{:S(2)}) %collective-permute-start.14) | collective-permute-done | bytes 32800 | tf_op jit(solution)/shard_map/ppermute | solution.py:220
  151.8 0.9 collective-permute-start.17
  152.7 0.7 collective-permute-start.16
  153.4 1.4 collective-permute-start.15
  154.8 1.2 shard_map.84.refs_0_
  156.0 2.0 %shard_map.85 = (f32[1024,64]{1,0:T(8,128)S(1)}, bf16[512,64]{1,0:T(8,128)(2,1)}) custom-call(s32[1]{0:T(128)} %bitcast.h_ref, s32[1]{0:T(128)} %bitcast.1.zh_ref, s32[1]{0:T(128)S(6)} %rem.73.y_ref, bf16[4,32,512]{2,1,0:T(8,128)(2,1)S(1)} %collective-permute-done.17.field_ref, bf16[64,16384]{1,0:T(8,128)(2,1)S(1)} %copy-done, ...), custom_call_target="tpu_custom_call" | custom-call | flops 268435456 | bytes 3604486 | tf_op jit(solution)/shard_map/pallas_call | solution.py:42
  158.0 1.1 collective-permute-done.16.field_ref
  159.1 2.0 %shard_map.86 = (f32[1024,64]{1,0:T(8,128)S(1)}, bf16[512,64]{1,0:T(8,128)(2,1)}) custom-call(s32[1]{0:T(128)} %bitcast.h_ref, s32[1]{0:T(128)} %bitcast.1.zh_ref, s32[1]{0:T(128)S(6)} %rem.67.y_ref, bf16[4,32,512]{2,1,0:T(8,128)(2,1)S(1)} %collective-permute-done.16.field_ref, bf16[64,16384]{1,0:T(8,128)(2,1)S(1)} %copy-done, ...), custom_call_target="tpu_custom_call" | custom-call | flops 268435456 | bytes 3604486 | tf_op jit(solution)/shard_map/pallas_call | solution.py:42
  161.1 1.3 shard_map.87
  162.4 3.5 %collective-permute-start.18 = (bf16[512,64]{1,0:T(8,128)(2,1)S(1)}, bf16[512,64]{1,0:T(8,128)(2,1)S(1)}, u32[]{:S(2)}, u32[]{:S(2)}) collective-permute-start(bf16[512,64]{1,0:T(8,128)(2,1)S(1)} %get-tuple-element.25), channel_id=1, source_target_pairs={{0,1},{1,0},{2,3},{3,2},{4,5},{5,4},{6,7},{7,6},{8,9},{9,8},{10,11... | collective-permute-start | bytes 196616 | tf_op jit(solution)/shard_map/ppermute | solution.py:28
  165.9 0.7 shard_map.79
  166.9 0.8 shard_map.88
  (31 shorter events, 1.3 us)
Async XLA Ops:
  0.6 6.4 %collective-permute-start.1 = (bf16[16,16384]{1,0:T(8,128)(2,1)}, bf16[16,16384]{1,0:T(8,128)(2,1)S(1)}, u32[]{:S(2)}, u32[]{:S(2)}) collective-permute-start(bf16[16,16384]{1,0:T(8,128)(2,1)} %cond_ref.19), channel_id=1, source_target_pairs={{0,1},{1,0},{2,3},{3,2},{4,5},{5,4},{6,7},{7,6},{8,9},{9,8},{10,11... | collective-permute-start | bytes 1572872 | tf_op jit(solution)/shard_map/ppermute | solution.py:28
  3.9 0.8 copy-start.4
  4.8 0.7 copy-start.6
  5.5 1.6 copy-start
  5.5 1.7 copy-start.1
  5.6 1.4 collective-permute-start
  12.7 41.2 %copy-start.2 = (bf16[512,2048]{1,0:T(8,128)(2,1)S(1)}, bf16[512,2048]{1,0:T(8,128)(2,1)}, u32[]{:S(2)}) copy-start(bf16[512,2048]{1,0:T(8,128)(2,1)} %kernel_ref.3) | copy-start | bytes 6291460
  49.3 4.6 %collective-permute-start.2 = (bf16[16,32,256]{2,1,0:T(8,128)(2,1)S(1)}, bf16[16,32,256]{2,1,0:T(8,128)(2,1)S(1)}, u32[]{:S(2)}, u32[]{:S(2)}) collective-permute-start(bf16[16,32,256]{2,1,0:T(8,128)(2,1)S(1)} %all_to_all.31.own_ref), channel_id=1, source_target_pairs={{0,1},{1,0},{2,3},{3,2},{4,5},{5,4},{6,7},{7,6},{8,9},{9,8},{10,11... | collective-permute-start | bytes 786440 | tf_op jit(solution)/shard_map/ppermute | solution.py:28
  64.1 4.4 %collective-permute-start.3 = (bf16[1,32,512]{2,1,0:T(8,128)(2,1)S(1)}, bf16[1,32,512]{2,1,0:T(8,128)(2,1)S(1)}, u32[]{:S(2)}, u32[]{:S(2)}) collective-permute-start(bf16[1,32,512]{2,1,0:T(8,128)(2,1)S(1)} %shard_map.72.refs_0_), channel_id=1, source_target_pairs={{0,24},{8,0},{16,8},{24,16},{1,25},{9,1},{17,9},{25,17},{2,26},{10... | collective-permute-start | bytes 98312 | tf_op jit(solution)/shard_map/ppermute | solution.py:220
  65.4 4.9 %collective-permute-start.4 = (bf16[1,32,512]{2,1,0:T(8,128)(2,1)S(1)}, bf16[1,32,512]{2,1,0:T(8,128)(2,1)S(1)}, u32[]{:S(2)}, u32[]{:S(2)}) collective-permute-start(bf16[1,32,512]{2,1,0:T(8,128)(2,1)S(1)} %shard_map.72.refs_0_), channel_id=1, source_target_pairs={{0,8},{8,16},{16,24},{24,0},{1,9},{9,17},{17,25},{25,1},{2,10},{10... | collective-permute-start | bytes 98312 | tf_op jit(solution)/shard_map/ppermute | solution.py:220
  66.5 6.7 %collective-permute-start.5 = (bf16[1,32,512]{2,1,0:T(8,128)(2,1)S(1)}, bf16[1,32,512]{2,1,0:T(8,128)(2,1)S(1)}, u32[]{:S(2)}, u32[]{:S(2)}) collective-permute-start(bf16[1,32,512]{2,1,0:T(8,128)(2,1)S(1)} %shard_map.72.refs_0_), channel_id=1, source_target_pairs={{0,16},{8,24},{16,0},{24,8},{1,17},{9,25},{17,1},{25,9},{2,18},{10... | collective-permute-start | bytes 98312 | tf_op jit(solution)/shard_map/ppermute | solution.py:220
  73.2 4.5 %collective-permute-start.8 = (bf16[4,32,512]{2,1,0:T(8,128)(2,1)S(1)}, bf16[4,32,512]{2,1,0:T(8,128)(2,1)}, u32[]{:S(2)}, u32[]{:S(2)}) collective-permute-start(bf16[4,32,512]{2,1,0:T(8,128)(2,1)S(1)} %shard_map.73.field_ref), channel_id=1, source_target_pairs={{0,6},{2,0},{4,2},{6,4},{1,7},{3,1},{5,3},{7,5},{8,14},{10,8},{12,... | collective-permute-start | bytes 393224 | tf_op jit(solution)/shard_map/ppermute | solution.py:220
  74.4 6.5 %collective-permute-start.7 = (bf16[4,32,512]{2,1,0:T(8,128)(2,1)S(1)}, bf16[4,32,512]{2,1,0:T(8,128)(2,1)}, u32[]{:S(2)}, u32[]{:S(2)}) collective-permute-start(bf16[4,32,512]{2,1,0:T(8,128)(2,1)S(1)} %shard_map.73.field_ref), channel_id=1, source_target_pairs={{0,2},{2,4},{4,6},{6,0},{1,3},{3,5},{5,7},{7,1},{8,10},{10,12},{12... | collective-permute-start | bytes 393224 | tf_op jit(solution)/shard_map/ppermute | solution.py:220
  74.8 9.1 %collective-permute-start.6 = (bf16[4,32,512]{2,1,0:T(8,128)(2,1)S(1)}, bf16[4,32,512]{2,1,0:T(8,128)(2,1)}, u32[]{:S(2)}, u32[]{:S(2)}) collective-permute-start(bf16[4,32,512]{2,1,0:T(8,128)(2,1)S(1)} %shard_map.73.field_ref), channel_id=1, source_target_pairs={{0,4},{2,6},{4,0},{6,2},{1,5},{3,7},{5,1},{7,3},{8,12},{10,14},{12... | collective-permute-start | bytes 393224 | tf_op jit(solution)/shard_map/ppermute | solution.py:220
  86.2 5.7 %collective-permute-start.9 = (bf16[1024,64]{1,0:T(8,128)(2,1)S(1)}, bf16[1024,64]{1,0:T(8,128)(2,1)S(1)}, u32[]{:S(2)}, u32[]{:S(2)}) collective-permute-start(bf16[1024,64]{1,0:T(8,128)(2,1)S(1)} %get-tuple-element.18), channel_id=1, source_target_pairs={{0,1},{1,0},{2,3},{3,2},{4,5},{5,4},{6,7},{7,6},{8,9},{9,8},{10,11... | collective-permute-start | bytes 393224 | tf_op jit(solution)/shard_map/ppermute | solution.py:28
  90.7 1.2 collective-permute-start.10
  97.9 34.9 %copy-start.3 = (bf16[512,2048]{1,0:T(8,128)(2,1)S(1)}, bf16[512,2048]{1,0:T(8,128)(2,1)}, u32[]{:S(2)}) copy-start(bf16[512,2048]{1,0:T(8,128)(2,1)} %kernel_ref.3) | copy-start | bytes 6291460
  128.3 4.4 %collective-permute-start.11 = (bf16[16,32,256]{2,1,0:T(8,128)(2,1)S(1)}, bf16[16,32,256]{2,1,0:T(8,128)(2,1)S(1)}, u32[]{:S(2)}, u32[]{:S(2)}) collective-permute-start(bf16[16,32,256]{2,1,0:T(8,128)(2,1)S(1)} %all_to_all.34.own_ref), channel_id=1, source_target_pairs={{0,1},{1,0},{2,3},{3,2},{4,5},{5,4},{6,7},{7,6},{8,9},{9,8},{10,11... | collective-permute-start | bytes 786440 | tf_op jit(solution)/shard_map/ppermute | solution.py:28
  142.7 4.7 %collective-permute-start.12 = (bf16[1,32,512]{2,1,0:T(8,128)(2,1)S(1)}, bf16[1,32,512]{2,1,0:T(8,128)(2,1)S(1)}, u32[]{:S(2)}, u32[]{:S(2)}) collective-permute-start(bf16[1,32,512]{2,1,0:T(8,128)(2,1)S(1)} %shard_map.82.refs_0_), channel_id=1, source_target_pairs={{0,24},{8,0},{16,8},{24,16},{1,25},{9,1},{17,9},{25,17},{2,26},{10... | collective-permute-start | bytes 98312 | tf_op jit(solution)/shard_map/ppermute | solution.py:220
  144.3 4.9 %collective-permute-start.13 = (bf16[1,32,512]{2,1,0:T(8,128)(2,1)S(1)}, bf16[1,32,512]{2,1,0:T(8,128)(2,1)S(1)}, u32[]{:S(2)}, u32[]{:S(2)}) collective-permute-start(bf16[1,32,512]{2,1,0:T(8,128)(2,1)S(1)} %shard_map.82.refs_0_), channel_id=1, source_target_pairs={{0,8},{8,16},{16,24},{24,0},{1,9},{9,17},{17,25},{25,1},{2,10},{10... | collective-permute-start | bytes 98312 | tf_op jit(solution)/shard_map/ppermute | solution.py:220
  145.1 6.7 %collective-permute-start.14 = (bf16[1,32,512]{2,1,0:T(8,128)(2,1)S(1)}, bf16[1,32,512]{2,1,0:T(8,128)(2,1)S(1)}, u32[]{:S(2)}, u32[]{:S(2)}) collective-permute-start(bf16[1,32,512]{2,1,0:T(8,128)(2,1)S(1)} %shard_map.82.refs_0_), channel_id=1, source_target_pairs={{0,16},{8,24},{16,0},{24,8},{1,17},{9,25},{17,1},{25,9},{2,18},{10... | collective-permute-start | bytes 98312 | tf_op jit(solution)/shard_map/ppermute | solution.py:220
  151.8 4.2 %collective-permute-start.17 = (bf16[4,32,512]{2,1,0:T(8,128)(2,1)S(1)}, bf16[4,32,512]{2,1,0:T(8,128)(2,1)S(1)}, u32[]{:S(2)}, u32[]{:S(2)}) collective-permute-start(bf16[4,32,512]{2,1,0:T(8,128)(2,1)S(1)} %shard_map.83.field_ref), channel_id=1, source_target_pairs={{0,6},{2,0},{4,2},{6,4},{1,7},{3,1},{5,3},{7,5},{8,14},{10,8},{12,... | collective-permute-start | bytes 393224 | tf_op jit(solution)/shard_map/ppermute | solution.py:220
  152.7 6.4 %collective-permute-start.16 = (bf16[4,32,512]{2,1,0:T(8,128)(2,1)S(1)}, bf16[4,32,512]{2,1,0:T(8,128)(2,1)S(1)}, u32[]{:S(2)}, u32[]{:S(2)}) collective-permute-start(bf16[4,32,512]{2,1,0:T(8,128)(2,1)S(1)} %shard_map.83.field_ref), channel_id=1, source_target_pairs={{0,2},{2,4},{4,6},{6,0},{1,3},{3,5},{5,7},{7,1},{8,10},{10,12},{12... | collective-permute-start | bytes 393224 | tf_op jit(solution)/shard_map/ppermute | solution.py:220
  153.4 7.7 %collective-permute-start.15 = (bf16[4,32,512]{2,1,0:T(8,128)(2,1)S(1)}, bf16[4,32,512]{2,1,0:T(8,128)(2,1)S(1)}, u32[]{:S(2)}, u32[]{:S(2)}) collective-permute-start(bf16[4,32,512]{2,1,0:T(8,128)(2,1)S(1)} %shard_map.83.field_ref), channel_id=1, source_target_pairs={{0,4},{2,6},{4,0},{6,2},{1,5},{3,7},{5,1},{7,3},{8,12},{10,14},{12... | collective-permute-start | bytes 393224 | tf_op jit(solution)/shard_map/ppermute | solution.py:220
  161.1 5.8 %copy-start.5 = (bf16[64,512]{1,0:T(8,128)(2,1)S(1)}, bf16[64,512]{1,0:T(8,128)(2,1)}, u32[]{:S(2)}) copy-start(bf16[64,512]{1,0:T(8,128)(2,1)} %trial_ref.3) | copy-start | bytes 196612
  162.4 4.5 %collective-permute-start.18 = (bf16[512,64]{1,0:T(8,128)(2,1)S(1)}, bf16[512,64]{1,0:T(8,128)(2,1)S(1)}, u32[]{:S(2)}, u32[]{:S(2)}) collective-permute-start(bf16[512,64]{1,0:T(8,128)(2,1)S(1)} %get-tuple-element.25), channel_id=1, source_target_pairs={{0,1},{1,0},{2,3},{3,2},{4,5},{5,4},{6,7},{7,6},{8,9},{9,8},{10,11... | collective-permute-start | bytes 196616 | tf_op jit(solution)/shard_map/ppermute | solution.py:28

commit v3 on v2

--- a/solution.py
+++ b/solution.py
@@ -6,6 +6,7 @@
 from jax.experimental import pallas as pl
 from jax.experimental.pallas import tpu as pltpu
 from jax.sharding import Mesh, PartitionSpec as P
+
 
 K = 32
 CENTER = 2.0
@@ -84,7 +85,8 @@
     encode_points(h_ref, (xt_ref, xt_other_ref), val_ref, (cond_ref, cond_other_ref), out_ref, width)
 
 
-def stepped(xt, scale, coupled):
+def stepped(xt, gap, coupled):
+    scale = (gap - CENTER) * (1.0 / HALF_WIDTH)
     scale = jnp.broadcast_to(scale[:, None, :], (scale.shape[0], K, scale.shape[1])).reshape(xt.shape)
     return xt.astype(F32) * scale + coupled * (2.0 / HALF_WIDTH)
 
@@ -96,8 +98,8 @@
     recv_ref,
     old_ref,
     old_other_ref,
-    scale_ref,
-    scale_other_ref,
+    gap_ref,
+    gap_other_ref,
     val_ref,
     cond_ref,
     cond_other_ref,
@@ -106,12 +108,12 @@
     xt_other_ref,
 ):
     half = old_ref.shape[0]
-    sides = ((old_ref, scale_ref, xt_ref), (old_other_ref, scale_other_ref, xt_other_ref))
-    for side, (old, scale, new) in enumerate(sides):
+    sides = ((old_ref, gap_ref, xt_ref), (old_other_ref, gap_other_ref, xt_other_ref))
+    for side, (old, gap, new) in enumerate(sides):
         here = slice(side * half, (side + 1) * half)
         there = slice((1 - side) * half, (2 - side) * half)
         coupled = part_ref[here] + recv_ref[there].astype(F32)
-        new[...] = stepped(old[...], scale[...], coupled).astype(BF16)
+        new[...] = stepped(old[...], gap[...], coupled).astype(BF16)
     encode_points(h_ref, (xt_ref, xt_other_ref), val_ref, (cond_ref, cond_other_ref), out_ref, width)
 
 
@@ -189,8 +191,9 @@
     return call(stack_kernel, arrays, (shape((len(arrays), *arrays[0].shape[1:])),), arrays[0].size)[0]
 
 
-def decode_kernel(steps, sizes, h_ref, zh_ref, y_ref, field_ref, val_ref, cond_ref, cond_other_ref, *refs):
-    *before, part_ref, send_ref = (*refs, None) if len(refs) == 1 else refs
+def decode_kernel(steps, sizes, more, h_ref, zh_ref, y_ref, field_ref, val_ref, cond_ref, cond_other_ref, *refs):
+    before = refs[:more]
+    part_ref, send_ref = (*refs[more:], None)[:2]
     width = field_ref.shape[2]
     for index, z_step in enumerate(steps):
         g = lax.rem(zh_ref[0] + sizes["zh"] - z_step, sizes["zh"]) * sizes["y"] + y_ref[0]
@@ -223,8 +226,11 @@
 def decode(field, place, orbitals, sizes, sent):
     val_count = orbitals[0].shape[0]
     rows = 2 * orbitals[1].shape[0] * K
-    steps = [0, *reversed(behind(sizes["zh"]))]
-    field = stacked([field, *(shifted(field, "zh", sizes["zh"], step) for step in steps[1:])])
+    steps = [0, *behind(sizes["zh"])]
+    fields = [field]
+    for step in steps[1:]:
+        fields.append(shifted(field, "zh", sizes["zh"], step))
+    field = stacked(fields)
     far = behind(sizes["y"])
     fields = {step: shifted(field, "y", sizes["y"], step) for step in far}
     fields[0] = field
@@ -233,11 +239,11 @@
     for y_step in (0, *reversed(far)):
         here = fields[y_step]
         outputs = (shape((rows, val_count), F32),)
-        if y_step:
+        if y_step == far[0]:
             outputs += (shape((sent, val_count)),)
         parts = call(
-            functools.partial(decode_kernel, tuple(steps), sizes),
-            (h, zh, lax.rem(y + (sizes["y"] - y_step), sizes["y"]), here, *orbitals, *parts[:1]),
+            functools.partial(decode_kernel, tuple(steps), sizes, len(parts)),
+            (h, zh, lax.rem(y + (sizes["y"] - y_step), sizes["y"]), here, *orbitals, *parts),
             outputs,
             2 * rows * val_count * here.shape[0] * here.shape[2],
             len(place),
@@ -245,32 +251,23 @@
     return parts
 
 
-def start_kernel(trial_ref, gap_ref, xt_ref, scale_ref):
-    xt_ref[...] = trial_ref[...].astype(F32).T.astype(BF16)
-    scale_ref[...] = (gap_ref[...] - CENTER) * (1.0 / HALF_WIDTH)
-
-
-def started(trial, gap):
-    return call(start_kernel, (trial, gap), (shape(trial.shape[::-1]), shape(gap.shape, F32)), START_FLOPS)
-
-
 def turn_kernel(xt_ref, out_ref):
     out_ref[...] = xt_ref[...].astype(F32).T.astype(BF16)
 
 
-def turned(xt):
-    return call(turn_kernel, (xt,), (shape(xt.shape[::-1]),), xt.size)[0]
-
-
-def finish_kernel(part_ref, recv_ref, xt_ref, scale_ref, trial_ref, out_ref):
+def turned(xt, flops):
+    return call(turn_kernel, (xt,), (shape(xt.shape[::-1]),), flops)[0]
+
+
+def finish_kernel(part_ref, recv_ref, xt_ref, gap_ref, trial_ref, out_ref):
     rows = recv_ref.shape[0]
     coupled = part_ref[:rows] + recv_ref[...].astype(F32)
-    second = stepped(xt_ref[...], scale_ref[...], coupled)
+    second = stepped(xt_ref[...], gap_ref[...], coupled)
     out_ref[...] = (2.0 * second.T - trial_ref[...].astype(F32)).astype(BF16)
 
 
-def finish(part, recv, xt, scale, trial):
-    return call(finish_kernel, (part, recv, xt, scale, trial), (shape(trial.shape),), 8 * trial.size)[0]
+def finish(part, recv, xt, gap, trial):
+    return call(finish_kernel, (part, recv, xt, gap, trial), (shape(trial.shape),), 8 * trial.size)[0]
 
 
 def field_of(encoded, h, kernel, sizes):
@@ -288,19 +285,20 @@
     place = [lax.axis_index(axis).astype(jnp.int32).reshape(1) for axis in ("core", "zh", "y")]
     h = place[0]
     orbitals = (orb_val, orb_cond, swap_cores(orb_cond))
-    xt, scale = started(trial, energy_gap.T)
-    xt_other, scale_other = swap_cores(xt), swap_cores(scale)
+    gap = energy_gap.T
+    xt = turned(trial, START_FLOPS)
+    xt_other = swap_cores(xt)
 
     encoded = encode(encode_first, h, (xt, xt_other), orbitals, pieces, piece, width)[0]
     field = field_of(encoded, h, kernel, sizes)
     part, sent = decode(field, place, orbitals, sizes, 2 * xt.shape[0])
-    whole = (part, swap_cores(sent), xt, xt_other, scale, scale_other)
+    whole = (part, swap_cores(sent), xt, xt_other, gap, swap_cores(gap))
     states = (shape(xt.shape), shape(xt.shape))
     encoded, xt, _ = encode(encode_next, h, whole, orbitals, pieces, piece, width, *states)
-    first_step = turned(xt)
+    first_step = turned(xt, xt.size)
     field = field_of(encoded, h, kernel, sizes)
     part, sent = decode(field, place, orbitals, sizes, xt.shape[0])
-    filtered = finish(part, swap_cores(sent), xt, scale, trial)
+    filtered = finish(part, swap_cores(sent), xt, gap, trial)
     return first_step, filtered
 
 

time: 168 us -> 165 us (0.982)
  Pallas kernels: 30.8 us -> 27.8 us
    pallas_call x21, Pallas kernels: 30.8 us -> 27.8 us  [call(): pl.pallas_call(kernel, in_specs=[smem] * scalars + [VMEM] * (len(inputs)...]
  transfers between devices with their start and end apart: 19 -> 19, of which waited for: 11 -> 11; matrix products, arithmetic and copies ran while one was open for 0% -> 0% of each run, Pallas kernels for 8% -> 6%
where the time goes in v3:
time: 165 us
  blocking collectives  85.9 us (52%)
  starting transfers between devices  32.2 us (20%)
  Pallas kernels  27.8 us (17%)
  waiting for transfers between devices  17.1 us (10%)
    all_to_all x6, blocking collectives, exchange(): return lax.all_to_all(array, axes, 0, 0, tiled=True)  85.9 us
    pallas_call x21, Pallas kernels, call(): pl.pallas_call(kernel, in_specs=[smem] * scalars + [VMEM] * (len(inputs)...  27.8 us
    ppermute x7, starting transfers between devices, swap_cores(): return lax.ppermute(array, 'core', [(0, 1), (1, 0)])  17.5 us
    ppermute x12, starting transfers between devices, shifted(): lax.ppermute(array, axis, [(i, (i + step) % count) for i in range(count)])  14.7 us
    ppermute x12, waiting for transfers between devices, shifted(): lax.ppermute(array, axis, [(i, (i + step) % count) for i in range(count)])  12.2 us
    ppermute x7, waiting for transfers between devices, swap_cores(): return lax.ppermute(array, 'core', [(0, 1), (1, 0)])  4.84 us
  transfers between devices with their start and end apart: 19, of which 11 were waited for; matrix products, arithmetic and copies ran while one was open for 0% of the time, Pallas kernels for 6%

profile of v3, /device:TPU:1, one launch (start us, length us, event | category | flops | bytes accessed | tf_op | source)
XLA Modules:
  0.0 164.7 jit_solution(10081983101300826206)
XLA Ops:
  0.6 3.3 %collective-permute-start.1 = (bf16[16,16384]{1,0:T(8,128)(2,1)}, bf16[16,16384]{1,0:T(8,128)(2,1)S(1)}, u32[]{:S(2)}, u32[]{:S(2)}) collective-permute-start(bf16[16,16384]{1,0:T(8,128)(2,1)} %cond_ref.19), channel_id=1, source_target_pairs={{0,1},{1,0},{2,3},{3,2},{4,5},{5,4},{6,7},{7,6},{8,9},{9,8},{10,11... | collective-permute-start | bytes 1572872 | tf_op jit(solution)/shard_map/ppermute | solution.py:29
  3.9 0.8 copy-done.4
  5.1 1.2 collective-permute-done.xt_other_ref.old_other_ref
  6.3 5.6 %shard_map.69 = bf16[32,32,256]{2,1,0:T(8,128)(2,1)S(1)} custom-call(s32[1]{0:T(128)} %bitcast.h_ref, bf16[512,64]{1,0:T(8,128)(2,1)S(1)} %shard_map.68.xt_ref.old_ref, bf16[512,64]{1,0:T(8,128)(2,1)S(1)} %collective-permute-done.xt_other_ref.old_other_ref, bf16[64,16384]{1,0:T(8,128)(2,1)S(1)} %copy-done, bf16[16,16384]{1,0:T(8,128)(2,1)S(1)} %copy-done.1, ...), custom_call_target="tpu_custom_call" | custom-call | flops 1073741824 | bytes 3801090 | tf_op jit(solution)/shard_map/pallas_call | solution.py:43
  12.0 17.0 %all_to_all.30.in_ref = bf16[32,32,256]{2,1,0:T(8,128)(2,1)S(1)} all-to-all(bf16[32,32,256]{2,1,0:T(8,128)(2,1)S(1)} %shard_map.69), channel_id=1, replica_groups=mesh['x'=4,'zl'=2,'zh'=4,'y'=4,'core'=2] {'x','zl','y'}, dimensions={0} | all-to-all | bytes 1048576 | tf_op jit(solution)/shard_map/all_to_all | solution.py:33
  29.1 19.4 %all_to_all.31.own_ref = bf16[16,32,256]{2,1,0:T(8,128)(2,1)S(1)} all-to-all(bf16[16,32,256]{2,1,0:T(8,128)(2,1)S(1)} %shard_map.70), channel_id=1, replica_groups=mesh['x'=4,'zl'=2,'zh'=4,'y'=4,'core'=2] {'zh','y'}, dimensions={0} | all-to-all | bytes 524288 | tf_op jit(solution)/shard_map/all_to_all | solution.py:33
  48.4 3.4 %collective-permute-start.2 = (bf16[16,32,256]{2,1,0:T(8,128)(2,1)S(1)}, bf16[16,32,256]{2,1,0:T(8,128)(2,1)S(1)}, u32[]{:S(2)}, u32[]{:S(2)}) collective-permute-start(bf16[16,32,256]{2,1,0:T(8,128)(2,1)S(1)} %all_to_all.31.own_ref), channel_id=1, source_target_pairs={{0,1},{1,0},{2,3},{3,2},{4,5},{5,4},{6,7},{7,6},{8,9},{9,8},{10,11... | collective-permute-start | bytes 786440 | tf_op jit(solution)/shard_map/ppermute | solution.py:29
  51.9 1.2 collective-permute-done.2.other_ref
  53.0 0.7 shard_map.71
  53.8 9.4 %all_to_all.32.in_ref = bf16[8,32,512]{2,1,0:T(8,128)(2,1)S(1)} all-to-all(bf16[8,32,512]{2,1,0:T(8,128)(2,1)S(1)} %shard_map.71), channel_id=1, replica_groups=mesh['x'=4,'zl'=2,'zh'=4,'y'=4,'core'=2] {'x','zl'}, dimensions={0} | all-to-all | bytes 524288 | tf_op jit(solution)/shard_map/all_to_all | solution.py:33
  63.2 1.3 collective-permute-start.5
  64.6 1.1 collective-permute-start.4
  65.7 1.8 %collective-permute-start.3 = (bf16[1,32,512]{2,1,0:T(8,128)(2,1)S(1)}, bf16[1,32,512]{2,1,0:T(8,128)(2,1)S(1)}, u32[]{:S(2)}, u32[]{:S(2)}) collective-permute-start(bf16[1,32,512]{2,1,0:T(8,128)(2,1)S(1)} %shard_map.72.refs_0_), channel_id=1, source_target_pairs={{0,16},{8,24},{16,0},{24,8},{1,17},{9,25},{17,1},{25,9},{2,18},{10... | collective-permute-start | bytes 98312 | tf_op jit(solution)/shard_map/ppermute | solution.py:223
  67.5 2.0 %collective-permute-done.4.refs_2_ = bf16[1,32,512]{2,1,0:T(8,128)(2,1)S(1)} collective-permute-done((bf16[1,32,512]{2,1,0:T(8,128)(2,1)S(1)}, bf16[1,32,512]{2,1,0:T(8,128)(2,1)S(1)}, u32[]{:S(2)}, u32[]{:S(2)}) %collective-permute-start.4) | collective-permute-done | bytes 32800 | tf_op jit(solution)/shard_map/ppermute | solution.py:223
  69.5 2.9 %collective-permute-done.3.refs_1_ = bf16[1,32,512]{2,1,0:T(8,128)(2,1)S(1)} collective-permute-done((bf16[1,32,512]{2,1,0:T(8,128)(2,1)S(1)}, bf16[1,32,512]{2,1,0:T(8,128)(2,1)S(1)}, u32[]{:S(2)}, u32[]{:S(2)}) %collective-permute-start.3) | collective-permute-done | bytes 32800 | tf_op jit(solution)/shard_map/ppermute | solution.py:223
  72.4 0.8 collective-permute-start.8
  73.2 0.8 collective-permute-start.7
  73.9 1.3 collective-permute-start.6
  75.2 1.2 shard_map.74.refs_0_
  76.5 2.2 %shard_map.75.refs_0_ = f32[1024,64]{1,0:T(8,128)S(1)} custom-call(s32[1]{0:T(128)} %bitcast.h_ref, s32[1]{0:T(128)} %bitcast.1.zh_ref, s32[1]{0:T(128)S(6)} %rem.73.y_ref, bf16[4,32,512]{2,1,0:T(8,128)(2,1)} %collective-permute-done.8.field_ref, bf16[64,16384]{1,0:T(8,128)(2,1)S(1)} %copy-done, bf16[16,16384]{1,0:T(8,128)(2,1)S(1)} %copy-done.1, ...), custom_call_target="tpu_custom_call" | custom-call | flops 268435456 | bytes 3538950 | tf_op jit(solution)/shard_map/pallas_call | solution.py:43
  78.6 1.1 collective-permute-done.7.field_ref
  79.7 2.1 %shard_map.76.refs_0_ = f32[1024,64]{1,0:T(8,128)S(1)} custom-call(s32[1]{0:T(128)} %bitcast.h_ref, s32[1]{0:T(128)} %bitcast.1.zh_ref, s32[1]{0:T(128)S(6)} %rem.67.y_ref, bf16[4,32,512]{2,1,0:T(8,128)(2,1)} %collective-permute-done.7.field_ref, bf16[64,16384]{1,0:T(8,128)(2,1)S(1)} %copy-done, bf16[16,16384]{1,0:T(8,128)(2,1)S(1)} %copy-done.1, ...), custom_call_target="tpu_custom_call" | custom-call | flops 268435456 | bytes 3538950 | tf_op jit(solution)/shard_map/pallas_call | solution.py:43
  81.9 2.3 %shard_map.77 = (f32[1024,64]{1,0:T(8,128)S(1)}, bf16[1024,64]{1,0:T(8,128)(2,1)S(1)}) custom-call(s32[1]{0:T(128)} %bitcast.h_ref, s32[1]{0:T(128)} %bitcast.1.zh_ref, s32[1]{0:T(128)S(6)} %rem.61.y_ref, bf16[4,32,512]{2,1,0:T(8,128)(2,1)} %collective-permute-done.6.field_ref, bf16[64,16384]{1,0:T(8,128)(2,1)S(1)} %copy-done, ...), custom_call_target="tpu_custom_call" | custom-call | flops 268435456 | bytes 3670022 | tf_op jit(solution)/shard_map/pallas_call | solution.py:43
  84.1 3.5 %collective-permute-start.9 = (bf16[1024,64]{1,0:T(8,128)(2,1)S(1)}, bf16[1024,64]{1,0:T(8,128)(2,1)S(1)}, u32[]{:S(2)}, u32[]{:S(2)}) collective-permute-start(bf16[1024,64]{1,0:T(8,128)(2,1)S(1)} %get-tuple-element.9), channel_id=1, source_target_pairs={{0,1},{1,0},{2,3},{3,2},{4,5},{5,4},{6,7},{7,6},{8,9},{9,8},{10,11... | collective-permute-start | bytes 393224 | tf_op jit(solution)/shard_map/ppermute | solution.py:29
  87.8 1.1 collective-permute-done.10.gap_other_ref
  88.8 6.0 %shard_map.78 = (bf16[32,32,256]{2,1,0:T(8,128)(2,1)S(1)}, bf16[512,64]{1,0:T(8,128)(2,1)S(1)}, bf16[512,64]{1,0:T(8,128)(2,1)}) custom-call(s32[1]{0:T(128)} %bitcast.h_ref, f32[1024,64]{1,0:T(8,128)S(1)} %get-tuple-element.8.part_ref, bf16[1024,64]{1,0:T(8,128)(2,1)S(1)} %collective-permute-done.9.recv_ref, bf16[512,64]{1,0:T(8,128)(2,1)S(1)} %shard_map.68.xt_ref.old_ref, ...), custom_call_target="tpu_custom_call" | custom-call | flops 1073741824 | bytes 4198402 | tf_op jit(solution)/shard_map/pallas_call | solution.py:43
  94.8 15.2 %all_to_all.33.in_ref = bf16[32,32,256]{2,1,0:T(8,128)(2,1)S(1)} all-to-all(bf16[32,32,256]{2,1,0:T(8,128)(2,1)S(1)} %get-tuple-element.11), channel_id=1, replica_groups=mesh['x'=4,'zl'=2,'zh'=4,'y'=4,'core'=2] {'x','zl','y'}, dimensions={0} | all-to-all | bytes 1048576 | tf_op jit(solution)/shard_map/all_to_all | solution.py:33
  110.1 15.8 %all_to_all.34.own_ref = bf16[16,32,256]{2,1,0:T(8,128)(2,1)S(1)} all-to-all(bf16[16,32,256]{2,1,0:T(8,128)(2,1)S(1)} %shard_map.80), channel_id=1, replica_groups=mesh['x'=4,'zl'=2,'zh'=4,'y'=4,'core'=2] {'zh','y'}, dimensions={0} | all-to-all | bytes 524288 | tf_op jit(solution)/shard_map/all_to_all | solution.py:33
  125.9 3.3 %collective-permute-start.11 = (bf16[16,32,256]{2,1,0:T(8,128)(2,1)S(1)}, bf16[16,32,256]{2,1,0:T(8,128)(2,1)S(1)}, u32[]{:S(2)}, u32[]{:S(2)}) collective-permute-start(bf16[16,32,256]{2,1,0:T(8,128)(2,1)S(1)} %all_to_all.34.own_ref), channel_id=1, source_target_pairs={{0,1},{1,0},{2,3},{3,2},{4,5},{5,4},{6,7},{7,6},{8,9},{9,8},{10,11... | collective-permute-start | bytes 786440 | tf_op jit(solution)/shard_map/ppermute | solution.py:29
  129.2 1.2 collective-permute-done.11.other_ref
  130.4 0.7 shard_map.81
  131.1 9.2 %all_to_all.35.in_ref = bf16[8,32,512]{2,1,0:T(8,128)(2,1)S(1)} all-to-all(bf16[8,32,512]{2,1,0:T(8,128)(2,1)S(1)} %shard_map.81), channel_id=1, replica_groups=mesh['x'=4,'zl'=2,'zh'=4,'y'=4,'core'=2] {'x','zl'}, dimensions={0} | all-to-all | bytes 524288 | tf_op jit(solution)/shard_map/all_to_all | solution.py:33
  140.3 1.6 collective-permute-start.14
  141.9 0.8 collective-permute-start.13
  142.8 2.3 %collective-permute-start.12 = (bf16[1,32,512]{2,1,0:T(8,128)(2,1)S(1)}, bf16[1,32,512]{2,1,0:T(8,128)(2,1)S(1)}, u32[]{:S(2)}, u32[]{:S(2)}) collective-permute-start(bf16[1,32,512]{2,1,0:T(8,128)(2,1)S(1)} %shard_map.82.refs_0_), channel_id=1, source_target_pairs={{0,16},{8,24},{16,0},{24,8},{1,17},{9,25},{17,1},{25,9},{2,18},{10... | collective-permute-start | bytes 98312 | tf_op jit(solution)/shard_map/ppermute | solution.py:223
  145.0 1.8 %collective-permute-done.13.refs_2_ = bf16[1,32,512]{2,1,0:T(8,128)(2,1)S(1)} collective-permute-done((bf16[1,32,512]{2,1,0:T(8,128)(2,1)S(1)}, bf16[1,32,512]{2,1,0:T(8,128)(2,1)S(1)}, u32[]{:S(2)}, u32[]{:S(2)}) %collective-permute-start.13) | collective-permute-done | bytes 32800 | tf_op jit(solution)/shard_map/ppermute | solution.py:223
  146.8 2.6 %collective-permute-done.12.refs_1_ = bf16[1,32,512]{2,1,0:T(8,128)(2,1)S(1)} collective-permute-done((bf16[1,32,512]{2,1,0:T(8,128)(2,1)S(1)}, bf16[1,32,512]{2,1,0:T(8,128)(2,1)S(1)}, u32[]{:S(2)}, u32[]{:S(2)}) %collective-permute-start.12) | collective-permute-done | bytes 32800 | tf_op jit(solution)/shard_map/ppermute | solution.py:223
  149.4 0.9 collective-permute-start.17
  150.4 0.6 collective-permute-start.16
  151.0 1.4 collective-permute-start.15
  152.4 1.2 shard_map.84.refs_0_
  153.7 1.3 shard_map.85.refs_0_
  154.9 1.9 %collective-permute-done.16.field_ref = bf16[4,32,512]{2,1,0:T(8,128)(2,1)S(1)} collective-permute-done((bf16[4,32,512]{2,1,0:T(8,128)(2,1)S(1)}, bf16[4,32,512]{2,1,0:T(8,128)(2,1)S(1)}, u32[]{:S(2)}, u32[]{:S(2)}) %collective-permute-start.16) | collective-permute-done | bytes 131104 | tf_op jit(solution)/shard_map/ppermute | solution.py:223
  156.8 1.2 shard_map.86.refs_0_
  158.1 1.3 shard_map.87
  159.4 3.6 %collective-permute-start.18 = (bf16[512,64]{1,0:T(8,128)(2,1)S(1)}, bf16[512,64]{1,0:T(8,128)(2,1)S(1)}, u32[]{:S(2)}, u32[]{:S(2)}) collective-permute-start(bf16[512,64]{1,0:T(8,128)(2,1)S(1)} %get-tuple-element.13), channel_id=1, source_target_pairs={{0,1},{1,0},{2,3},{3,2},{4,5},{5,4},{6,7},{7,6},{8,9},{9,8},{10,11... | collective-permute-start | bytes 196616 | tf_op jit(solution)/shard_map/ppermute | solution.py:29
  163.0 0.7 shard_map.79
  164.0 0.8 shard_map.88
  (31 shorter events, 1.1 us)
Async XLA Ops:
  0.6 5.7 %copy-start.1 = (bf16[16,16384]{1,0:T(8,128)(2,1)S(1)}, bf16[16,16384]{1,0:T(8,128)(2,1)}, u32[]{:S(2)}) copy-start(bf16[16,16384]{1,0:T(8,128)(2,1)} %cond_ref.19) | copy-start | bytes 1572868
  0.6 5.7 %copy-start = (bf16[64,16384]{1,0:T(8,128)(2,1)S(1)}, bf16[64,16384]{1,0:T(8,128)(2,1)}, u32[]{:S(2)}) copy-start(bf16[64,16384]{1,0:T(8,128)(2,1)} %val_ref.19) | copy-start | bytes 6291460
  0.6 5.7 %collective-permute-start.1 = (bf16[16,16384]{1,0:T(8,128)(2,1)}, bf16[16,16384]{1,0:T(8,128)(2,1)S(1)}, u32[]{:S(2)}, u32[]{:S(2)}) collective-permute-start(bf16[16,16384]{1,0:T(8,128)(2,1)} %cond_ref.19), channel_id=1, source_target_pairs={{0,1},{1,0},{2,3},{3,2},{4,5},{5,4},{6,7},{7,6},{8,9},{9,8},{10,11... | collective-permute-start | bytes 1572872 | tf_op jit(solution)/shard_map/ppermute | solution.py:29
  3.9 0.8 copy-start.4
  4.9 1.4 collective-permute-start
  11.9 41.1 %copy-start.2 = (bf16[512,2048]{1,0:T(8,128)(2,1)S(1)}, bf16[512,2048]{1,0:T(8,128)(2,1)}, u32[]{:S(2)}) copy-start(bf16[512,2048]{1,0:T(8,128)(2,1)} %kernel_ref.3) | copy-start | bytes 6291460
  48.4 4.6 %collective-permute-start.2 = (bf16[16,32,256]{2,1,0:T(8,128)(2,1)S(1)}, bf16[16,32,256]{2,1,0:T(8,128)(2,1)S(1)}, u32[]{:S(2)}, u32[]{:S(2)}) collective-permute-start(bf16[16,32,256]{2,1,0:T(8,128)(2,1)S(1)} %all_to_all.31.own_ref), channel_id=1, source_target_pairs={{0,1},{1,0},{2,3},{3,2},{4,5},{5,4},{6,7},{7,6},{8,9},{9,8},{10,11... | collective-permute-start | bytes 786440 | tf_op jit(solution)/shard_map/ppermute | solution.py:29
  63.2 4.3 %collective-permute-start.5 = (bf16[1,32,512]{2,1,0:T(8,128)(2,1)S(1)}, bf16[1,32,512]{2,1,0:T(8,128)(2,1)S(1)}, u32[]{:S(2)}, u32[]{:S(2)}) collective-permute-start(bf16[1,32,512]{2,1,0:T(8,128)(2,1)S(1)} %shard_map.72.refs_0_), channel_id=1, source_target_pairs={{0,24},{8,0},{16,8},{24,16},{1,25},{9,1},{17,9},{25,17},{2,26},{10... | collective-permute-start | bytes 98312 | tf_op jit(solution)/shard_map/ppermute | solution.py:223
  64.6 4.9 %collective-permute-start.4 = (bf16[1,32,512]{2,1,0:T(8,128)(2,1)S(1)}, bf16[1,32,512]{2,1,0:T(8,128)(2,1)S(1)}, u32[]{:S(2)}, u32[]{:S(2)}) collective-permute-start(bf16[1,32,512]{2,1,0:T(8,128)(2,1)S(1)} %shard_map.72.refs_0_), channel_id=1, source_target_pairs={{0,8},{8,16},{16,24},{24,0},{1,9},{9,17},{17,25},{25,1},{2,10},{10... | collective-permute-start | bytes 98312 | tf_op jit(solution)/shard_map/ppermute | solution.py:223
  65.7 6.7 %collective-permute-start.3 = (bf16[1,32,512]{2,1,0:T(8,128)(2,1)S(1)}, bf16[1,32,512]{2,1,0:T(8,128)(2,1)S(1)}, u32[]{:S(2)}, u32[]{:S(2)}) collective-permute-start(bf16[1,32,512]{2,1,0:T(8,128)(2,1)S(1)} %shard_map.72.refs_0_), channel_id=1, source_target_pairs={{0,16},{8,24},{16,0},{24,8},{1,17},{9,25},{17,1},{25,9},{2,18},{10... | collective-permute-start | bytes 98312 | tf_op jit(solution)/shard_map/ppermute | solution.py:223
  72.4 4.1 %collective-permute-start.8 = (bf16[4,32,512]{2,1,0:T(8,128)(2,1)S(1)}, bf16[4,32,512]{2,1,0:T(8,128)(2,1)}, u32[]{:S(2)}, u32[]{:S(2)}) collective-permute-start(bf16[4,32,512]{2,1,0:T(8,128)(2,1)S(1)} %shard_map.73.field_ref), channel_id=1, source_target_pairs={{0,6},{2,0},{4,2},{6,4},{1,7},{3,1},{5,3},{7,5},{8,14},{10,8},{12,... | collective-permute-start | bytes 393224 | tf_op jit(solution)/shard_map/ppermute | solution.py:223
  73.2 6.5 %collective-permute-start.7 = (bf16[4,32,512]{2,1,0:T(8,128)(2,1)S(1)}, bf16[4,32,512]{2,1,0:T(8,128)(2,1)}, u32[]{:S(2)}, u32[]{:S(2)}) collective-permute-start(bf16[4,32,512]{2,1,0:T(8,128)(2,1)S(1)} %shard_map.73.field_ref), channel_id=1, source_target_pairs={{0,2},{2,4},{4,6},{6,0},{1,3},{3,5},{5,7},{7,1},{8,10},{10,12},{12... | collective-permute-start | bytes 393224 | tf_op jit(solution)/shard_map/ppermute | solution.py:223
  73.9 7.9 %collective-permute-start.6 = (bf16[4,32,512]{2,1,0:T(8,128)(2,1)S(1)}, bf16[4,32,512]{2,1,0:T(8,128)(2,1)}, u32[]{:S(2)}, u32[]{:S(2)}) collective-permute-start(bf16[4,32,512]{2,1,0:T(8,128)(2,1)S(1)} %shard_map.73.field_ref), channel_id=1, source_target_pairs={{0,4},{2,6},{4,0},{6,2},{1,5},{3,7},{5,1},{7,3},{8,12},{10,14},{12... | collective-permute-start | bytes 393224 | tf_op jit(solution)/shard_map/ppermute | solution.py:223
  81.8 5.8 %copy-start.6 = (f32[64,16]{0,1:T(8,128)S(1)}, f32[64,16]{0,1:T(8,128)}, u32[]{:S(2)}) copy-start(f32[64,16]{0,1:T(8,128)} %param.6) | copy-start | bytes 12292
  84.1 4.7 %collective-permute-start.9 = (bf16[1024,64]{1,0:T(8,128)(2,1)S(1)}, bf16[1024,64]{1,0:T(8,128)(2,1)S(1)}, u32[]{:S(2)}, u32[]{:S(2)}) collective-permute-start(bf16[1024,64]{1,0:T(8,128)(2,1)S(1)} %get-tuple-element.9), channel_id=1, source_target_pairs={{0,1},{1,0},{2,3},{3,2},{4,5},{5,4},{6,7},{7,6},{8,9},{9,8},{10,11... | collective-permute-start | bytes 393224 | tf_op jit(solution)/shard_map/ppermute | solution.py:29
  87.6 1.2 collective-permute-start.10
  94.8 35.5 %copy-start.3 = (bf16[512,2048]{1,0:T(8,128)(2,1)S(1)}, bf16[512,2048]{1,0:T(8,128)(2,1)}, u32[]{:S(2)}) copy-start(bf16[512,2048]{1,0:T(8,128)(2,1)} %kernel_ref.3) | copy-start | bytes 6291460
  125.9 4.5 %collective-permute-start.11 = (bf16[16,32,256]{2,1,0:T(8,128)(2,1)S(1)}, bf16[16,32,256]{2,1,0:T(8,128)(2,1)S(1)}, u32[]{:S(2)}, u32[]{:S(2)}) collective-permute-start(bf16[16,32,256]{2,1,0:T(8,128)(2,1)S(1)} %all_to_all.34.own_ref), channel_id=1, source_target_pairs={{0,1},{1,0},{2,3},{3,2},{4,5},{5,4},{6,7},{7,6},{8,9},{9,8},{10,11... | collective-permute-start | bytes 786440 | tf_op jit(solution)/shard_map/ppermute | solution.py:29
  140.3 4.7 %collective-permute-start.14 = (bf16[1,32,512]{2,1,0:T(8,128)(2,1)S(1)}, bf16[1,32,512]{2,1,0:T(8,128)(2,1)S(1)}, u32[]{:S(2)}, u32[]{:S(2)}) collective-permute-start(bf16[1,32,512]{2,1,0:T(8,128)(2,1)S(1)} %shard_map.82.refs_0_), channel_id=1, source_target_pairs={{0,24},{8,0},{16,8},{24,16},{1,25},{9,1},{17,9},{25,17},{2,26},{10... | collective-permute-start | bytes 98312 | tf_op jit(solution)/shard_map/ppermute | solution.py:223
  141.9 4.9 %collective-permute-start.13 = (bf16[1,32,512]{2,1,0:T(8,128)(2,1)S(1)}, bf16[1,32,512]{2,1,0:T(8,128)(2,1)S(1)}, u32[]{:S(2)}, u32[]{:S(2)}) collective-permute-start(bf16[1,32,512]{2,1,0:T(8,128)(2,1)S(1)} %shard_map.82.refs_0_), channel_id=1, source_target_pairs={{0,8},{8,16},{16,24},{24,0},{1,9},{9,17},{17,25},{25,1},{2,10},{10... | collective-permute-start | bytes 98312 | tf_op jit(solution)/shard_map/ppermute | solution.py:223
  142.8 6.7 %collective-permute-start.12 = (bf16[1,32,512]{2,1,0:T(8,128)(2,1)S(1)}, bf16[1,32,512]{2,1,0:T(8,128)(2,1)S(1)}, u32[]{:S(2)}, u32[]{:S(2)}) collective-permute-start(bf16[1,32,512]{2,1,0:T(8,128)(2,1)S(1)} %shard_map.82.refs_0_), channel_id=1, source_target_pairs={{0,16},{8,24},{16,0},{24,8},{1,17},{9,25},{17,1},{25,9},{2,18},{10... | collective-permute-start | bytes 98312 | tf_op jit(solution)/shard_map/ppermute | solution.py:223
  149.4 4.2 %collective-permute-start.17 = (bf16[4,32,512]{2,1,0:T(8,128)(2,1)S(1)}, bf16[4,32,512]{2,1,0:T(8,128)(2,1)S(1)}, u32[]{:S(2)}, u32[]{:S(2)}) collective-permute-start(bf16[4,32,512]{2,1,0:T(8,128)(2,1)S(1)} %shard_map.83.field_ref), channel_id=1, source_target_pairs={{0,6},{2,0},{4,2},{6,4},{1,7},{3,1},{5,3},{7,5},{8,14},{10,8},{12,... | collective-permute-start | bytes 393224 | tf_op jit(solution)/shard_map/ppermute | solution.py:223
  150.4 6.4 %collective-permute-start.16 = (bf16[4,32,512]{2,1,0:T(8,128)(2,1)S(1)}, bf16[4,32,512]{2,1,0:T(8,128)(2,1)S(1)}, u32[]{:S(2)}, u32[]{:S(2)}) collective-permute-start(bf16[4,32,512]{2,1,0:T(8,128)(2,1)S(1)} %shard_map.83.field_ref), channel_id=1, source_target_pairs={{0,2},{2,4},{4,6},{6,0},{1,3},{3,5},{5,7},{7,1},{8,10},{10,12},{12... | collective-permute-start | bytes 393224 | tf_op jit(solution)/shard_map/ppermute | solution.py:223
  151.0 7.1 %collective-permute-start.15 = (bf16[4,32,512]{2,1,0:T(8,128)(2,1)S(1)}, bf16[4,32,512]{2,1,0:T(8,128)(2,1)S(1)}, u32[]{:S(2)}, u32[]{:S(2)}) collective-permute-start(bf16[4,32,512]{2,1,0:T(8,128)(2,1)S(1)} %shard_map.83.field_ref), channel_id=1, source_target_pairs={{0,4},{2,6},{4,0},{6,2},{1,5},{3,7},{5,1},{7,3},{8,12},{10,14},{12... | collective-permute-start | bytes 393224 | tf_op jit(solution)/shard_map/ppermute | solution.py:223
  158.0 5.9 %copy-start.5 = (bf16[64,512]{1,0:T(8,128)(2,1)S(1)}, bf16[64,512]{1,0:T(8,128)(2,1)}, u32[]{:S(2)}) copy-start(bf16[64,512]{1,0:T(8,128)(2,1)} %trial_ref.1) | copy-start | bytes 196612
  159.4 4.6 %collective-permute-start.18 = (bf16[512,64]{1,0:T(8,128)(2,1)S(1)}, bf16[512,64]{1,0:T(8,128)(2,1)S(1)}, u32[]{:S(2)}, u32[]{:S(2)}) collective-permute-start(bf16[512,64]{1,0:T(8,128)(2,1)S(1)} %get-tuple-element.13), channel_id=1, source_target_pairs={{0,1},{1,0},{2,3},{3,2},{4,5},{5,4},{6,7},{7,6},{8,9},{9,8},{10,11... | collective-permute-start | bytes 196616 | tf_op jit(solution)/shard_map/ppermute | solution.py:29

commit v4 on v3

--- a/solution.py
+++ b/solution.py
@@ -14,7 +14,6 @@
 
 FINE = (("x", 4), ("zl", 2), ("zh", 4), ("y", 4), ("core", 2))
 VAL = ("x", "zl")
-RING = ("zh", "y")
 PTS = ("zh", "y", "core")
 
 BF16 = jnp.bfloat16
@@ -142,42 +141,46 @@
     return call(total_kernel, (array,), (shape((copies, *array.shape[1:])),), array.size)[0]
 
 
-def apply_kernel(pieces, width, h_ref, own_ref, other_ref, kernel_ref, out_ref):
-    piece = own_ref.shape[2]
+def add_kernel(*refs):
+    *parts, out_ref = refs
+    total = parts[0][...].astype(F32)
+    for part in parts[1:]:
+        total = total + part[...].astype(F32)
+    out_ref[...] = total.astype(BF16)
+
+
+def added(arrays):
+    return call(add_kernel, arrays, (shape(arrays[0].shape),), START_FLOPS)[0]
+
+
+def apply_kernel(steps, pieces, width, h_ref, y_ref, *refs):
+    *fit_refs, kernel_ref, out_ref = refs
+    piece = fit_refs[0].shape[2]
     even = h_ref[0] == 0
-
-    def added(ref, q):
-        total = ref[q].astype(F32)
-        for index in range(q + pieces, ref.shape[0], pieces):
-            total = total + ref[index].astype(F32)
-        return total
-
     total = jnp.zeros((K, kernel_ref.shape[0]), F32)
-    for q in range(pieces):
-        own, other = added(own_ref, q), added(other_ref, q)
+    for step, ref in zip(steps, fit_refs):
+        at = lax.rem(y_ref[0] + pieces - step, pieces) * piece
+        first = 2 * width * lax.div(at, width) + lax.rem(at, width)
+        own, other = ref[0].astype(F32), ref[1].astype(F32)
         for side in range(2):
             fit = jnp.where(even, own, other) if side == 0 else jnp.where(even, other, own)
-            at = q * piece
-            first = width * (2 * (at // width) + side) + at % width
+            cols = pl.ds(pl.multiple_of(first + side * width, piece), piece)
             total = total + lax.dot_general(
-                fit.astype(BF16),
-                kernel_ref[:, first : first + piece],
-                (((1,), (1,)), ((), ())),
-                preferred_element_type=F32,
+                fit.astype(BF16), kernel_ref[:, cols], (((1,), (1,)), ((), ())), preferred_element_type=F32
             )
     total = total.astype(BF16)
     for copy in range(out_ref.shape[0]):
         out_ref[copy] = total
 
 
-def applied(h, own, other, kernel, pieces, copies):
+def applied(h, y, fits, steps, kernel, copies):
     rows = kernel.shape[0]
     return call(
-        functools.partial(apply_kernel, pieces, rows),
-        (h, own, other, kernel),
+        functools.partial(apply_kernel, tuple(steps), len(steps), rows),
+        (h, y, *fits, kernel),
         (shape((copies, K, rows)),),
         2 * K * kernel.size,
-        1,
+        2,
     )[0]
 
 
@@ -188,7 +191,22 @@
 
 
 def stacked(arrays):
-    return call(stack_kernel, arrays, (shape((len(arrays), *arrays[0].shape[1:])),), arrays[0].size)[0]
+    return call(stack_kernel, arrays, (shape((len(arrays), *arrays[0].shape[1:])),), START_FLOPS)[0]
+
+
+def behind(count):
+    return sorted(range(1, count), key=lambda step: -min(step, count - step))
+
+
+def shifted(array, axis, count, step):
+    return lax.ppermute(array, axis, [(i, (i + step) % count) for i in range(count)])
+
+
+def along_zh(array, sizes):
+    arrays = [array]
+    for step in behind(sizes["zh"]):
+        arrays.append(shifted(array, "zh", sizes["zh"], step))
+    return arrays
 
 
 def decode_kernel(steps, sizes, more, h_ref, zh_ref, y_ref, field_ref, val_ref, cond_ref, cond_other_ref, *refs):
@@ -215,22 +233,11 @@
         send_ref[...] = part_ref[part_ref.shape[0] - send_ref.shape[0] :].astype(BF16)
 
 
-def behind(count):
-    return sorted(range(1, count), key=lambda step: -min(step, count - step))
-
-
-def shifted(array, axis, count, step):
-    return lax.ppermute(array, axis, [(i, (i + step) % count) for i in range(count)])
-
-
 def decode(field, place, orbitals, sizes, sent):
     val_count = orbitals[0].shape[0]
     rows = 2 * orbitals[1].shape[0] * K
     steps = [0, *behind(sizes["zh"])]
-    fields = [field]
-    for step in steps[1:]:
-        fields.append(shifted(field, "zh", sizes["zh"], step))
-    field = stacked(fields)
+    field = stacked(along_zh(field, sizes))
     far = behind(sizes["y"])
     fields = {step: shifted(field, "y", sizes["y"], step) for step in far}
     fields[0] = field
@@ -270,11 +277,13 @@
     return call(finish_kernel, (part, recv, xt, gap, trial), (shape(trial.shape),), 8 * trial.size)[0]
 
 
-def field_of(encoded, h, kernel, sizes):
-    ring = sizes["zh"] * sizes["y"]
-    shares = exchange(encoded, (*VAL, "y"))
-    shares = exchange(summed(shares, ring), RING)
-    image = applied(h, shares, swap_cores(shares), kernel, sizes["y"], sizes["x"] * sizes["zl"])
+def field_of(encoded, place, kernel, sizes):
+    h, _, y = place
+    fit = added(along_zh(summed(exchange(encoded, (*VAL, "y")), 1), sizes))
+    fit = stacked([fit, swap_cores(fit)])
+    steps = [0, *behind(sizes["y"])]
+    fits = [fit, *(shifted(fit, "y", sizes["y"], step) for step in steps[1:])]
+    image = applied(h, y, fits, steps, kernel, sizes["x"] * sizes["zl"])
     return summed(exchange(image, VAL), 1)
 
 
@@ -290,13 +299,13 @@
     xt_other = swap_cores(xt)
 
     encoded = encode(encode_first, h, (xt, xt_other), orbitals, pieces, piece, width)[0]
-    field = field_of(encoded, h, kernel, sizes)
+    field = field_of(encoded, place, kernel, sizes)
     part, sent = decode(field, place, orbitals, sizes, 2 * xt.shape[0])
     whole = (part, swap_cores(sent), xt, xt_other, gap, swap_cores(gap))
     states = (shape(xt.shape), shape(xt.shape))
     encoded, xt, _ = encode(encode_next, h, whole, orbitals, pieces, piece, width, *states)
     first_step = turned(xt, xt.size)
-    field = field_of(encoded, h, kernel, sizes)
+    field = field_of(encoded, place, kernel, sizes)
     part, sent = decode(field, place, orbitals, sizes, xt.shape[0])
     filtered = finish(part, swap_cores(sent), xt, gap, trial)
     return first_step, filtered

time: 165 us -> 174 us (1.055)
  blocking collectives: 85.9 us -> 47.7 us
  starting transfers between devices: 32.2 us -> 63.9 us
  waiting for transfers between devices: 17.1 us -> 30.8 us
    all_to_all x6 -> x4, blocking collectives: 85.9 us -> 47.7 us  [exchange(): return lax.all_to_all(array, axes, 0, 0, tiled=True)]
    ppermute x12 -> x24, starting transfers between devices: 14.7 us -> 40.2 us  [shifted(): lax.ppermute(array, axis, [(i, (i + step) % count) for i in range(count)])]
    ppermute x12 -> x24, waiting for transfers between devices: 12.2 us -> 26.6 us  [shifted(): lax.ppermute(array, axis, [(i, (i + step) % count) for i in range(count)])]
    ppermute x7, starting transfers between devices: 17.5 us -> 23.6 us  [swap_cores(): return lax.ppermute(array, 'core', [(0, 1), (1, 0)])]
    pallas_call x21 -> x25, Pallas kernels: 27.8 us -> 27.8 us  [call(): pl.pallas_call(kernel, in_specs=[smem] * scalars + [VMEM] * (len(inputs)...]
  transfers between devices with their start and end apart: 19 -> 31, of which waited for: 11 -> 19; matrix products, arithmetic and copies ran while one was open for 0% -> 0% of each run, Pallas kernels for 6% -> 6%
where the time goes in v4:
time: 174 us; the launch traced here: 173 us
  starting transfers between devices  63.9 us (37%)
  blocking collectives  47.7 us (27%)
  waiting for transfers between devices  30.8 us (18%)
  Pallas kernels  27.8 us (16%)
  local copies, waits for them, and re-layouts  2.46 us (1%)
    all_to_all x4, blocking collectives, exchange(): return lax.all_to_all(array, axes, 0, 0, tiled=True)  47.7 us
    ppermute x24, starting transfers between devices, shifted(): lax.ppermute(array, axis, [(i, (i + step) % count) for i in range(count)])  40.2 us
    pallas_call x25, Pallas kernels, call(): pl.pallas_call(kernel, in_specs=[smem] * scalars + [VMEM] * (len(inputs)...  27.8 us
    ppermute x24, waiting for transfers between devices, shifted(): lax.ppermute(array, axis, [(i, (i + step) % count) for i in range(count)])  26.6 us
    ppermute x7, starting transfers between devices, swap_cores(): return lax.ppermute(array, 'core', [(0, 1), (1, 0)])  23.6 us
    ppermute x7, waiting for transfers between devices, swap_cores(): return lax.ppermute(array, 'core', [(0, 1), (1, 0)])  4.2 us
  transfers between devices with their start and end apart: 31, of which 19 were waited for; matrix products, arithmetic and copies ran while one was open for 0% of the time, Pallas kernels for 6%

profile of v4, /device:TPU:1, one launch (start us, length us, event | category | flops | bytes accessed | tf_op | source)
XLA Modules:
  0.0 173.4 jit_solution(3596948223314517348)
XLA Ops:
  0.6 3.3 %collective-permute-start.1 = (bf16[16,16384]{1,0:T(8,128)(2,1)}, bf16[16,16384]{1,0:T(8,128)(2,1)S(1)}, u32[]{:S(2)}, u32[]{:S(2)}) collective-permute-start(bf16[16,16384]{1,0:T(8,128)(2,1)} %cond_ref.19), channel_id=1, source_target_pairs={{0,1},{1,0},{2,3},{3,2},{4,5},{5,4},{6,7},{7,6},{8,9},{9,8},{10,11... | collective-permute-start | bytes 1572872 | tf_op jit(solution)/shard_map/ppermute | solution.py:28
  5.1 1.2 collective-permute-done.xt_other_ref.old_other_ref
  6.3 5.6 %shard_map.69 = bf16[32,32,256]{2,1,0:T(8,128)(2,1)S(1)} custom-call(s32[1]{0:T(128)} %bitcast.h_ref, bf16[512,64]{1,0:T(8,128)(2,1)S(1)} %shard_map.68.xt_ref.old_ref, bf16[512,64]{1,0:T(8,128)(2,1)S(1)} %collective-permute-done.xt_other_ref.old_other_ref, bf16[64,16384]{1,0:T(8,128)(2,1)S(1)} %copy-done, bf16[16,16384]{1,0:T(8,128)(2,1)S(1)} %copy-done.1, ...), custom_call_target="tpu_custom_call" | custom-call | flops 1073741824 | bytes 3801090 | tf_op jit(solution)/shard_map/pallas_call | solution.py:42
  11.9 16.9 %all_to_all.20.in_ref = bf16[32,32,256]{2,1,0:T(8,128)(2,1)S(1)} all-to-all(bf16[32,32,256]{2,1,0:T(8,128)(2,1)S(1)} %shard_map.69), channel_id=1, replica_groups=mesh['x'=4,'zl'=2,'zh'=4,'y'=4,'core'=2] {'x','zl','y'}, dimensions={0} | all-to-all | bytes 1048576 | tf_op jit(solution)/shard_map/all_to_all | solution.py:32
  28.9 5.2 %collective-permute-start.4 = (bf16[1,32,256]{2,1,0:T(8,128)(2,1)S(1)}, bf16[1,32,256]{2,1,0:T(8,128)(2,1)S(1)}, u32[]{:S(2)}, u32[]{:S(2)}) collective-permute-start(bf16[1,32,256]{2,1,0:T(8,128)(2,1)S(1)} %shard_map.70.refs_0_), channel_id=1, source_target_pairs={{0,24},{8,0},{16,8},{24,16},{1,25},{9,1},{17,9},{25,17},{2,26},{10... | collective-permute-start | bytes 49160 | tf_op jit(solution)/shard_map/ppermute | solution.py:202
  34.1 3.3 %collective-permute-start.2 = (bf16[1,32,256]{2,1,0:T(8,128)(2,1)S(1)}, bf16[1,32,256]{2,1,0:T(8,128)(2,1)S(1)}, u32[]{:S(2)}, u32[]{:S(2)}) collective-permute-start(bf16[1,32,256]{2,1,0:T(8,128)(2,1)S(1)} %shard_map.70.refs_0_), channel_id=1, source_target_pairs={{0,16},{8,24},{16,0},{24,8},{1,17},{9,25},{17,1},{25,9},{2,18},{10... | collective-permute-start | bytes 49160 | tf_op jit(solution)/shard_map/ppermute | solution.py:202
  37.4 1.4 collective-permute-done.3.refs_2_
  38.8 1.8 %collective-permute-done.2.refs_1_ = bf16[1,32,256]{2,1,0:T(8,128)(2,1)S(1)} collective-permute-done((bf16[1,32,256]{2,1,0:T(8,128)(2,1)S(1)}, bf16[1,32,256]{2,1,0:T(8,128)(2,1)S(1)}, u32[]{:S(2)}, u32[]{:S(2)}) %collective-permute-start.2) | collective-permute-done | bytes 16416 | tf_op jit(solution)/shard_map/ppermute | solution.py:202
  40.6 3.4 %collective-permute-start.5 = (bf16[1,32,256]{2,1,0:T(8,128)(2,1)S(1)}, bf16[1,32,256]{2,1,0:T(8,128)(2,1)S(1)}, u32[]{:S(2)}, u32[]{:S(2)}) collective-permute-start(bf16[1,32,256]{2,1,0:T(8,128)(2,1)S(1)} %shard_map.71.refs_0_), channel_id=1, source_target_pairs={{0,1},{1,0},{2,3},{3,2},{4,5},{5,4},{6,7},{7,6},{8,9},{9,8},{10,11... | collective-permute-start | bytes 49160 | tf_op jit(solution)/shard_map/ppermute | solution.py:28
  46.4 1.8 %collective-permute-start.6 = (bf16[2,32,256]{2,1,0:T(8,128)(2,1)S(1)}, bf16[2,32,256]{2,1,0:T(8,128)(2,1)S(1)}, u32[]{:S(2)}, u32[]{:S(2)}) collective-permute-start(bf16[2,32,256]{2,1,0:T(8,128)(2,1)S(1)} %shard_map.72.refs_0_), channel_id=1, source_target_pairs={{0,4},{2,6},{4,0},{6,2},{1,5},{3,7},{5,1},{7,3},{8,12},{10,14},{12... | collective-permute-start | bytes 98312 | tf_op jit(solution)/shard_map/ppermute | solution.py:202
  48.2 1.6 collective-permute-done.7.refs_2_
  49.8 1.2 collective-permute-done.6.refs_1_
  51.0 1.6 copy-done.2
  53.3 8.6 %all_to_all.21.in_ref = bf16[8,32,512]{2,1,0:T(8,128)(2,1)S(1)} all-to-all(bf16[8,32,512]{2,1,0:T(8,128)(2,1)S(1)} %shard_map.73), channel_id=1, replica_groups=mesh['x'=4,'zl'=2,'zh'=4,'y'=4,'core'=2] {'x','zl'}, dimensions={0} | all-to-all | bytes 524288 | tf_op jit(solution)/shard_map/all_to_all | solution.py:32
  62.0 3.9 %collective-permute-start.11 = (bf16[1,32,512]{2,1,0:T(8,128)(2,1)S(1)}, bf16[1,32,512]{2,1,0:T(8,128)(2,1)S(1)}, u32[]{:S(2)}, u32[]{:S(2)}) collective-permute-start(bf16[1,32,512]{2,1,0:T(8,128)(2,1)S(1)} %shard_map.74.refs_0_), channel_id=1, source_target_pairs={{0,24},{8,0},{16,8},{24,16},{1,25},{9,1},{17,9},{25,17},{2,26},{10... | collective-permute-start | bytes 98312 | tf_op jit(solution)/shard_map/ppermute | solution.py:202
  65.9 2.2 %collective-permute-start.9 = (bf16[1,32,512]{2,1,0:T(8,128)(2,1)S(1)}, bf16[1,32,512]{2,1,0:T(8,128)(2,1)S(1)}, u32[]{:S(2)}, u32[]{:S(2)}) collective-permute-start(bf16[1,32,512]{2,1,0:T(8,128)(2,1)S(1)} %shard_map.74.refs_0_), channel_id=1, source_target_pairs={{0,16},{8,24},{16,0},{24,8},{1,17},{9,25},{17,1},{25,9},{2,18},{10... | collective-permute-start | bytes 98312 | tf_op jit(solution)/shard_map/ppermute | solution.py:202
  68.1 2.7 %collective-permute-done.10.refs_2_ = bf16[1,32,512]{2,1,0:T(8,128)(2,1)S(1)} collective-permute-done((bf16[1,32,512]{2,1,0:T(8,128)(2,1)S(1)}, bf16[1,32,512]{2,1,0:T(8,128)(2,1)S(1)}, u32[]{:S(2)}, u32[]{:S(2)}) %collective-permute-start.10) | collective-permute-done | bytes 32800 | tf_op jit(solution)/shard_map/ppermute | solution.py:202
  70.8 1.8 %collective-permute-done.9.refs_1_ = bf16[1,32,512]{2,1,0:T(8,128)(2,1)S(1)} collective-permute-done((bf16[1,32,512]{2,1,0:T(8,128)(2,1)S(1)}, bf16[1,32,512]{2,1,0:T(8,128)(2,1)S(1)}, u32[]{:S(2)}, u32[]{:S(2)}) %collective-permute-start.9) | collective-permute-done | bytes 32800 | tf_op jit(solution)/shard_map/ppermute | solution.py:202
  72.6 2.1 %collective-permute-start.14 = (bf16[4,32,512]{2,1,0:T(8,128)(2,1)S(1)}, bf16[4,32,512]{2,1,0:T(8,128)(2,1)}, u32[]{:S(2)}, u32[]{:S(2)}) collective-permute-start(bf16[4,32,512]{2,1,0:T(8,128)(2,1)S(1)} %shard_map.75.field_ref), channel_id=1, source_target_pairs={{0,6},{2,0},{4,2},{6,4},{1,7},{3,1},{5,3},{7,5},{8,14},{10,8},{12,... | collective-permute-start | bytes 393224 | tf_op jit(solution)/shard_map/ppermute | solution.py:202
  74.7 1.3 collective-permute-start.12
  76.0 1.2 shard_map.76.refs_0_
  77.2 2.2 %shard_map.77.refs_0_ = f32[1024,64]{1,0:T(8,128)S(1)} custom-call(s32[1]{0:T(128)} %bitcast.h_ref, s32[1]{0:T(128)} %bitcast.1.zh_ref, s32[1]{0:T(128)S(6)} %rem.73.y_ref, bf16[4,32,512]{2,1,0:T(8,128)(2,1)} %collective-permute-done.14.field_ref, bf16[64,16384]{1,0:T(8,128)(2,1)S(1)} %copy-done, bf16[16,16384]{1,0:T(8,128)(2,1)S(1)} %copy-done.1, ...), custom_call_target="tpu_custom_call" | custom-call | flops 268435456 | bytes 3538950 | tf_op jit(solution)/shard_map/pallas_call | solution.py:42
  79.4 1.9 %collective-permute-done.13.field_ref = bf16[4,32,512]{2,1,0:T(8,128)(2,1)} collective-permute-done((bf16[4,32,512]{2,1,0:T(8,128)(2,1)S(1)}, bf16[4,32,512]{2,1,0:T(8,128)(2,1)}, u32[]{:S(2)}, u32[]{:S(2)}) %collective-permute-start.13) | collective-permute-done | bytes 131104 | tf_op jit(solution)/shard_map/ppermute | solution.py:202
  81.2 2.1 %shard_map.78.refs_0_ = f32[1024,64]{1,0:T(8,128)S(1)} custom-call(s32[1]{0:T(128)} %bitcast.h_ref, s32[1]{0:T(128)} %bitcast.1.zh_ref, s32[1]{0:T(128)S(6)} %rem.67.y_ref, bf16[4,32,512]{2,1,0:T(8,128)(2,1)} %collective-permute-done.13.field_ref, bf16[64,16384]{1,0:T(8,128)(2,1)S(1)} %copy-done, bf16[16,16384]{1,0:T(8,128)(2,1)S(1)} %copy-done.1, ...), custom_call_target="tpu_custom_call" | custom-call | flops 268435456 | bytes 3538950 | tf_op jit(solution)/shard_map/pallas_call | solution.py:42
  83.4 2.3 %shard_map.79 = (f32[1024,64]{1,0:T(8,128)S(1)}, bf16[1024,64]{1,0:T(8,128)(2,1)S(1)}) custom-call(s32[1]{0:T(128)} %bitcast.h_ref, s32[1]{0:T(128)} %bitcast.1.zh_ref, s32[1]{0:T(128)S(6)} %rem.61.y_ref, bf16[4,32,512]{2,1,0:T(8,128)(2,1)} %collective-permute-done.12.field_ref, bf16[64,16384]{1,0:T(8,128)(2,1)S(1)} %copy-done, ...), custom_call_target="tpu_custom_call" | custom-call | flops 268435456 | bytes 3670022 | tf_op jit(solution)/shard_map/pallas_call | solution.py:42
  85.7 6.7 %collective-permute-start.15 = (bf16[1024,64]{1,0:T(8,128)(2,1)S(1)}, bf16[1024,64]{1,0:T(8,128)(2,1)S(1)}, u32[]{:S(2)}, u32[]{:S(2)}) collective-permute-start(bf16[1024,64]{1,0:T(8,128)(2,1)S(1)} %get-tuple-element.9), channel_id=1, source_target_pairs={{0,1},{1,0},{2,3},{3,2},{4,5},{5,4},{6,7},{7,6},{8,9},{9,8},{10,11... | collective-permute-start | bytes 393224 | tf_op jit(solution)/shard_map/ppermute | solution.py:28
  93.5 6.0 %shard_map.80 = (bf16[32,32,256]{2,1,0:T(8,128)(2,1)S(1)}, bf16[512,64]{1,0:T(8,128)(2,1)S(1)}, bf16[512,64]{1,0:T(8,128)(2,1)}) custom-call(s32[1]{0:T(128)} %bitcast.h_ref, f32[1024,64]{1,0:T(8,128)S(1)} %get-tuple-element.8.part_ref, bf16[1024,64]{1,0:T(8,128)(2,1)S(1)} %collective-permute-done.15.recv_ref, bf16[512,64]{1,0:T(8,128)(2,1)S(1)} %shard_map.68.xt_ref.old_ref, ...), custom_call_target="tpu_custom_call" | custom-call | flops 1073741824 | bytes 4198402 | tf_op jit(solution)/shard_map/pallas_call | solution.py:42
  99.5 13.4 %all_to_all.22.in_ref = bf16[32,32,256]{2,1,0:T(8,128)(2,1)S(1)} all-to-all(bf16[32,32,256]{2,1,0:T(8,128)(2,1)S(1)} %get-tuple-element.11), channel_id=1, replica_groups=mesh['x'=4,'zl'=2,'zh'=4,'y'=4,'core'=2] {'x','zl','y'}, dimensions={0} | all-to-all | bytes 1048576 | tf_op jit(solution)/shard_map/all_to_all | solution.py:32
  113.0 4.0 %collective-permute-start.19 = (bf16[1,32,256]{2,1,0:T(8,128)(2,1)S(1)}, bf16[1,32,256]{2,1,0:T(8,128)(2,1)S(1)}, u32[]{:S(2)}, u32[]{:S(2)}) collective-permute-start(bf16[1,32,256]{2,1,0:T(8,128)(2,1)S(1)} %shard_map.82.refs_0_), channel_id=1, source_target_pairs={{0,24},{8,0},{16,8},{24,16},{1,25},{9,1},{17,9},{25,17},{2,26},{10... | collective-permute-start | bytes 49160 | tf_op jit(solution)/shard_map/ppermute | solution.py:202
  117.0 2.2 %collective-permute-start.17 = (bf16[1,32,256]{2,1,0:T(8,128)(2,1)S(1)}, bf16[1,32,256]{2,1,0:T(8,128)(2,1)S(1)}, u32[]{:S(2)}, u32[]{:S(2)}) collective-permute-start(bf16[1,32,256]{2,1,0:T(8,128)(2,1)S(1)} %shard_map.82.refs_0_), channel_id=1, source_target_pairs={{0,16},{8,24},{16,0},{24,8},{1,17},{9,25},{17,1},{25,9},{2,18},{10... | collective-permute-start | bytes 49160 | tf_op jit(solution)/shard_map/ppermute | solution.py:202
  119.2 2.5 %collective-permute-done.18.refs_2_ = bf16[1,32,256]{2,1,0:T(8,128)(2,1)S(1)} collective-permute-done((bf16[1,32,256]{2,1,0:T(8,128)(2,1)S(1)}, bf16[1,32,256]{2,1,0:T(8,128)(2,1)S(1)}, u32[]{:S(2)}, u32[]{:S(2)}) %collective-permute-start.18) | collective-permute-done | bytes 16416 | tf_op jit(solution)/shard_map/ppermute | solution.py:202
  121.7 1.8 %collective-permute-done.17.refs_1_ = bf16[1,32,256]{2,1,0:T(8,128)(2,1)S(1)} collective-permute-done((bf16[1,32,256]{2,1,0:T(8,128)(2,1)S(1)}, bf16[1,32,256]{2,1,0:T(8,128)(2,1)S(1)}, u32[]{:S(2)}, u32[]{:S(2)}) %collective-permute-start.17) | collective-permute-done | bytes 16416 | tf_op jit(solution)/shard_map/ppermute | solution.py:202
  123.5 3.2 %collective-permute-start.20 = (bf16[1,32,256]{2,1,0:T(8,128)(2,1)S(1)}, bf16[1,32,256]{2,1,0:T(8,128)(2,1)S(1)}, u32[]{:S(2)}, u32[]{:S(2)}) collective-permute-start(bf16[1,32,256]{2,1,0:T(8,128)(2,1)S(1)} %shard_map.83.refs_0_), channel_id=1, source_target_pairs={{0,1},{1,0},{2,3},{3,2},{4,5},{5,4},{6,7},{7,6},{8,9},{9,8},{10,11... | collective-permute-start | bytes 49160 | tf_op jit(solution)/shard_map/ppermute | solution.py:28
  129.0 1.9 %collective-permute-start.21 = (bf16[2,32,256]{2,1,0:T(8,128)(2,1)S(1)}, bf16[2,32,256]{2,1,0:T(8,128)(2,1)S(1)}, u32[]{:S(2)}, u32[]{:S(2)}) collective-permute-start(bf16[2,32,256]{2,1,0:T(8,128)(2,1)S(1)} %shard_map.84.refs_0_), channel_id=1, source_target_pairs={{0,4},{2,6},{4,0},{6,2},{1,5},{3,7},{5,1},{7,3},{8,12},{10,14},{12... | collective-permute-start | bytes 98312 | tf_op jit(solution)/shard_map/ppermute | solution.py:202
  131.0 1.6 collective-permute-done.22.refs_2_
  134.4 8.8 %all_to_all.23.in_ref = bf16[8,32,512]{2,1,0:T(8,128)(2,1)S(1)} all-to-all(bf16[8,32,512]{2,1,0:T(8,128)(2,1)S(1)} %shard_map.85), channel_id=1, replica_groups=mesh['x'=4,'zl'=2,'zh'=4,'y'=4,'core'=2] {'x','zl'}, dimensions={0} | all-to-all | bytes 524288 | tf_op jit(solution)/shard_map/all_to_all | solution.py:32
  143.2 3.9 %collective-permute-start.26 = (bf16[1,32,512]{2,1,0:T(8,128)(2,1)S(1)}, bf16[1,32,512]{2,1,0:T(8,128)(2,1)S(1)}, u32[]{:S(2)}, u32[]{:S(2)}) collective-permute-start(bf16[1,32,512]{2,1,0:T(8,128)(2,1)S(1)} %shard_map.86.refs_0_), channel_id=1, source_target_pairs={{0,24},{8,0},{16,8},{24,16},{1,25},{9,1},{17,9},{25,17},{2,26},{10... | collective-permute-start | bytes 98312 | tf_op jit(solution)/shard_map/ppermute | solution.py:202
  147.1 2.2 %collective-permute-start.24 = (bf16[1,32,512]{2,1,0:T(8,128)(2,1)S(1)}, bf16[1,32,512]{2,1,0:T(8,128)(2,1)S(1)}, u32[]{:S(2)}, u32[]{:S(2)}) collective-permute-start(bf16[1,32,512]{2,1,0:T(8,128)(2,1)S(1)} %shard_map.86.refs_0_), channel_id=1, source_target_pairs={{0,16},{8,24},{16,0},{24,8},{1,17},{9,25},{17,1},{25,9},{2,18},{10... | collective-permute-start | bytes 98312 | tf_op jit(solution)/shard_map/ppermute | solution.py:202
  149.3 2.7 %collective-permute-done.25.refs_2_ = bf16[1,32,512]{2,1,0:T(8,128)(2,1)S(1)} collective-permute-done((bf16[1,32,512]{2,1,0:T(8,128)(2,1)S(1)}, bf16[1,32,512]{2,1,0:T(8,128)(2,1)S(1)}, u32[]{:S(2)}, u32[]{:S(2)}) %collective-permute-start.25) | collective-permute-done | bytes 32800 | tf_op jit(solution)/shard_map/ppermute | solution.py:202
  152.0 1.8 %collective-permute-done.24.refs_1_ = bf16[1,32,512]{2,1,0:T(8,128)(2,1)S(1)} collective-permute-done((bf16[1,32,512]{2,1,0:T(8,128)(2,1)S(1)}, bf16[1,32,512]{2,1,0:T(8,128)(2,1)S(1)}, u32[]{:S(2)}, u32[]{:S(2)}) %collective-permute-start.24) | collective-permute-done | bytes 32800 | tf_op jit(solution)/shard_map/ppermute | solution.py:202
  153.8 2.1 %collective-permute-start.29 = (bf16[4,32,512]{2,1,0:T(8,128)(2,1)S(1)}, bf16[4,32,512]{2,1,0:T(8,128)(2,1)S(1)}, u32[]{:S(2)}, u32[]{:S(2)}) collective-permute-start(bf16[4,32,512]{2,1,0:T(8,128)(2,1)S(1)} %shard_map.87.field_ref), channel_id=1, source_target_pairs={{0,6},{2,0},{4,2},{6,4},{1,7},{3,1},{5,3},{7,5},{8,14},{10,8},{12,... | collective-permute-start | bytes 393224 | tf_op jit(solution)/shard_map/ppermute | solution.py:202
  155.9 1.3 collective-permute-start.27
  157.2 1.2 shard_map.88.refs_0_
  158.5 1.3 shard_map.89.refs_0_
  159.7 2.6 %collective-permute-done.28.field_ref = bf16[4,32,512]{2,1,0:T(8,128)(2,1)S(1)} collective-permute-done((bf16[4,32,512]{2,1,0:T(8,128)(2,1)S(1)}, bf16[4,32,512]{2,1,0:T(8,128)(2,1)S(1)}, u32[]{:S(2)}, u32[]{:S(2)}) %collective-permute-start.28) | collective-permute-done | bytes 131104 | tf_op jit(solution)/shard_map/ppermute | solution.py:202
  162.4 1.2 shard_map.90.refs_0_
  163.6 1.3 shard_map.91
  165.0 6.7 %collective-permute-start.30 = (bf16[512,64]{1,0:T(8,128)(2,1)S(1)}, bf16[512,64]{1,0:T(8,128)(2,1)S(1)}, u32[]{:S(2)}, u32[]{:S(2)}) collective-permute-start(bf16[512,64]{1,0:T(8,128)(2,1)S(1)} %get-tuple-element.13), channel_id=1, source_target_pairs={{0,1},{1,0},{2,3},{3,2},{4,5},{5,4},{6,7},{7,6},{8,9},{9,8},{10,11... | collective-permute-start | bytes 196616 | tf_op jit(solution)/shard_map/ppermute | solution.py:28
  (57 shorter events, 11.6 us)
Async XLA Ops:
  0.6 5.7 %copy-start.1 = (bf16[16,16384]{1,0:T(8,128)(2,1)S(1)}, bf16[16,16384]{1,0:T(8,128)(2,1)}, u32[]{:S(2)}) copy-start(bf16[16,16384]{1,0:T(8,128)(2,1)} %cond_ref.19) | copy-start | bytes 1572868
  0.6 5.7 %copy-start = (bf16[64,16384]{1,0:T(8,128)(2,1)S(1)}, bf16[64,16384]{1,0:T(8,128)(2,1)}, u32[]{:S(2)}) copy-start(bf16[64,16384]{1,0:T(8,128)(2,1)} %val_ref.19) | copy-start | bytes 6291460
  0.6 5.7 %collective-permute-start.1 = (bf16[16,16384]{1,0:T(8,128)(2,1)}, bf16[16,16384]{1,0:T(8,128)(2,1)S(1)}, u32[]{:S(2)}, u32[]{:S(2)}) collective-permute-start(bf16[16,16384]{1,0:T(8,128)(2,1)} %cond_ref.19), channel_id=1, source_target_pairs={{0,1},{1,0},{2,3},{3,2},{4,5},{5,4},{6,7},{7,6},{8,9},{9,8},{10,11... | collective-permute-start | bytes 1572872 | tf_op jit(solution)/shard_map/ppermute | solution.py:28
  3.9 0.8 copy-start.4
  4.9 1.4 collective-permute-start
  28.9 8.5 %collective-permute-start.4 = (bf16[1,32,256]{2,1,0:T(8,128)(2,1)S(1)}, bf16[1,32,256]{2,1,0:T(8,128)(2,1)S(1)}, u32[]{:S(2)}, u32[]{:S(2)}) collective-permute-start(bf16[1,32,256]{2,1,0:T(8,128)(2,1)S(1)} %shard_map.70.refs_0_), channel_id=1, source_target_pairs={{0,24},{8,0},{16,8},{24,16},{1,25},{9,1},{17,9},{25,17},{2,26},{10... | collective-permute-start | bytes 49160 | tf_op jit(solution)/shard_map/ppermute | solution.py:202
  34.1 4.7 %collective-permute-start.3 = (bf16[1,32,256]{2,1,0:T(8,128)(2,1)S(1)}, bf16[1,32,256]{2,1,0:T(8,128)(2,1)S(1)}, u32[]{:S(2)}, u32[]{:S(2)}) collective-permute-start(bf16[1,32,256]{2,1,0:T(8,128)(2,1)S(1)} %shard_map.70.refs_0_), channel_id=1, source_target_pairs={{0,8},{8,16},{16,24},{24,0},{1,9},{9,17},{17,25},{25,1},{2,10},{10... | collective-permute-start | bytes 49160 | tf_op jit(solution)/shard_map/ppermute | solution.py:202
  34.1 6.5 %collective-permute-start.2 = (bf16[1,32,256]{2,1,0:T(8,128)(2,1)S(1)}, bf16[1,32,256]{2,1,0:T(8,128)(2,1)S(1)}, u32[]{:S(2)}, u32[]{:S(2)}) collective-permute-start(bf16[1,32,256]{2,1,0:T(8,128)(2,1)S(1)} %shard_map.70.refs_0_), channel_id=1, source_target_pairs={{0,16},{8,24},{16,0},{24,8},{1,17},{9,25},{17,1},{25,9},{2,18},{10... | collective-permute-start | bytes 49160 | tf_op jit(solution)/shard_map/ppermute | solution.py:202
  40.6 4.3 %collective-permute-start.5 = (bf16[1,32,256]{2,1,0:T(8,128)(2,1)S(1)}, bf16[1,32,256]{2,1,0:T(8,128)(2,1)S(1)}, u32[]{:S(2)}, u32[]{:S(2)}) collective-permute-start(bf16[1,32,256]{2,1,0:T(8,128)(2,1)S(1)} %shard_map.71.refs_0_), channel_id=1, source_target_pairs={{0,1},{1,0},{2,3},{3,2},{4,5},{5,4},{6,7},{7,6},{8,9},{9,8},{10,11... | collective-permute-start | bytes 49160 | tf_op jit(solution)/shard_map/ppermute | solution.py:28
  44.9 3.2 %collective-permute-start.8 = (bf16[2,32,256]{2,1,0:T(8,128)(2,1)S(1)}, bf16[2,32,256]{2,1,0:T(8,128)(2,1)S(1)}, u32[]{:S(2)}, u32[]{:S(2)}) collective-permute-start(bf16[2,32,256]{2,1,0:T(8,128)(2,1)S(1)} %shard_map.72.refs_0_), channel_id=1, source_target_pairs={{0,6},{2,0},{4,2},{6,4},{1,7},{3,1},{5,3},{7,5},{8,14},{10,8},{12,... | collective-permute-start | bytes 98312 | tf_op jit(solution)/shard_map/ppermute | solution.py:202
  45.8 4.0 %collective-permute-start.7 = (bf16[2,32,256]{2,1,0:T(8,128)(2,1)S(1)}, bf16[2,32,256]{2,1,0:T(8,128)(2,1)S(1)}, u32[]{:S(2)}, u32[]{:S(2)}) collective-permute-start(bf16[2,32,256]{2,1,0:T(8,128)(2,1)S(1)} %shard_map.72.refs_0_), channel_id=1, source_target_pairs={{0,2},{2,4},{4,6},{6,0},{1,3},{3,5},{5,7},{7,1},{8,10},{10,12},{12... | collective-permute-start | bytes 98312 | tf_op jit(solution)/shard_map/ppermute | solution.py:202
  46.4 4.6 %collective-permute-start.6 = (bf16[2,32,256]{2,1,0:T(8,128)(2,1)S(1)}, bf16[2,32,256]{2,1,0:T(8,128)(2,1)S(1)}, u32[]{:S(2)}, u32[]{:S(2)}) collective-permute-start(bf16[2,32,256]{2,1,0:T(8,128)(2,1)S(1)} %shard_map.72.refs_0_), channel_id=1, source_target_pairs={{0,4},{2,6},{4,0},{6,2},{1,5},{3,7},{5,1},{7,3},{8,12},{10,14},{12... | collective-permute-start | bytes 98312 | tf_op jit(solution)/shard_map/ppermute | solution.py:202
  51.0 1.6 copy-start.2
  62.0 6.1 %collective-permute-start.11 = (bf16[1,32,512]{2,1,0:T(8,128)(2,1)S(1)}, bf16[1,32,512]{2,1,0:T(8,128)(2,1)S(1)}, u32[]{:S(2)}, u32[]{:S(2)}) collective-permute-start(bf16[1,32,512]{2,1,0:T(8,128)(2,1)S(1)} %shard_map.74.refs_0_), channel_id=1, source_target_pairs={{0,24},{8,0},{16,8},{24,16},{1,25},{9,1},{17,9},{25,17},{2,26},{10... | collective-permute-start | bytes 98312 | tf_op jit(solution)/shard_map/ppermute | solution.py:202
  65.9 4.9 %collective-permute-start.10 = (bf16[1,32,512]{2,1,0:T(8,128)(2,1)S(1)}, bf16[1,32,512]{2,1,0:T(8,128)(2,1)S(1)}, u32[]{:S(2)}, u32[]{:S(2)}) collective-permute-start(bf16[1,32,512]{2,1,0:T(8,128)(2,1)S(1)} %shard_map.74.refs_0_), channel_id=1, source_target_pairs={{0,8},{8,16},{16,24},{24,0},{1,9},{9,17},{17,25},{25,1},{2,10},{10... | collective-permute-start | bytes 98312 | tf_op jit(solution)/shard_map/ppermute | solution.py:202
  65.9 6.7 %collective-permute-start.9 = (bf16[1,32,512]{2,1,0:T(8,128)(2,1)S(1)}, bf16[1,32,512]{2,1,0:T(8,128)(2,1)S(1)}, u32[]{:S(2)}, u32[]{:S(2)}) collective-permute-start(bf16[1,32,512]{2,1,0:T(8,128)(2,1)S(1)} %shard_map.74.refs_0_), channel_id=1, source_target_pairs={{0,16},{8,24},{16,0},{24,8},{1,17},{9,25},{17,1},{25,9},{2,18},{10... | collective-permute-start | bytes 98312 | tf_op jit(solution)/shard_map/ppermute | solution.py:202
  72.6 4.6 %collective-permute-start.14 = (bf16[4,32,512]{2,1,0:T(8,128)(2,1)S(1)}, bf16[4,32,512]{2,1,0:T(8,128)(2,1)}, u32[]{:S(2)}, u32[]{:S(2)}) collective-permute-start(bf16[4,32,512]{2,1,0:T(8,128)(2,1)S(1)} %shard_map.75.field_ref), channel_id=1, source_target_pairs={{0,6},{2,0},{4,2},{6,4},{1,7},{3,1},{5,3},{7,5},{8,14},{10,8},{12,... | collective-permute-start | bytes 393224 | tf_op jit(solution)/shard_map/ppermute | solution.py:202
  74.7 6.5 %collective-permute-start.13 = (bf16[4,32,512]{2,1,0:T(8,128)(2,1)S(1)}, bf16[4,32,512]{2,1,0:T(8,128)(2,1)}, u32[]{:S(2)}, u32[]{:S(2)}) collective-permute-start(bf16[4,32,512]{2,1,0:T(8,128)(2,1)S(1)} %shard_map.75.field_ref), channel_id=1, source_target_pairs={{0,2},{2,4},{4,6},{6,0},{1,3},{3,5},{5,7},{7,1},{8,10},{10,12},{12... | collective-permute-start | bytes 393224 | tf_op jit(solution)/shard_map/ppermute | solution.py:202
  74.7 8.7 %collective-permute-start.12 = (bf16[4,32,512]{2,1,0:T(8,128)(2,1)S(1)}, bf16[4,32,512]{2,1,0:T(8,128)(2,1)}, u32[]{:S(2)}, u32[]{:S(2)}) collective-permute-start(bf16[4,32,512]{2,1,0:T(8,128)(2,1)S(1)} %shard_map.75.field_ref), channel_id=1, source_target_pairs={{0,4},{2,6},{4,0},{6,2},{1,5},{3,7},{5,1},{7,3},{8,12},{10,14},{12... | collective-permute-start | bytes 393224 | tf_op jit(solution)/shard_map/ppermute | solution.py:202
  83.4 9.0 %copy-start.6 = (f32[64,16]{0,1:T(8,128)S(1)}, f32[64,16]{0,1:T(8,128)}, u32[]{:S(2)}) copy-start(f32[64,16]{0,1:T(8,128)} %param.6) | copy-start | bytes 12292
  85.7 7.9 %collective-permute-start.15 = (bf16[1024,64]{1,0:T(8,128)(2,1)S(1)}, bf16[1024,64]{1,0:T(8,128)(2,1)S(1)}, u32[]{:S(2)}, u32[]{:S(2)}) collective-permute-start(bf16[1024,64]{1,0:T(8,128)(2,1)S(1)} %get-tuple-element.9), channel_id=1, source_target_pairs={{0,1},{1,0},{2,3},{3,2},{4,5},{5,4},{6,7},{7,6},{8,9},{9,8},{10,11... | collective-permute-start | bytes 393224 | tf_op jit(solution)/shard_map/ppermute | solution.py:28
  92.4 1.2 collective-permute-start.16
  113.0 6.1 %collective-permute-start.19 = (bf16[1,32,256]{2,1,0:T(8,128)(2,1)S(1)}, bf16[1,32,256]{2,1,0:T(8,128)(2,1)S(1)}, u32[]{:S(2)}, u32[]{:S(2)}) collective-permute-start(bf16[1,32,256]{2,1,0:T(8,128)(2,1)S(1)} %shard_map.82.refs_0_), channel_id=1, source_target_pairs={{0,24},{8,0},{16,8},{24,16},{1,25},{9,1},{17,9},{25,17},{2,26},{10... | collective-permute-start | bytes 49160 | tf_op jit(solution)/shard_map/ppermute | solution.py:202
  117.0 4.7 %collective-permute-start.18 = (bf16[1,32,256]{2,1,0:T(8,128)(2,1)S(1)}, bf16[1,32,256]{2,1,0:T(8,128)(2,1)S(1)}, u32[]{:S(2)}, u32[]{:S(2)}) collective-permute-start(bf16[1,32,256]{2,1,0:T(8,128)(2,1)S(1)} %shard_map.82.refs_0_), channel_id=1, source_target_pairs={{0,8},{8,16},{16,24},{24,0},{1,9},{9,17},{17,25},{25,1},{2,10},{10... | collective-permute-start | bytes 49160 | tf_op jit(solution)/shard_map/ppermute | solution.py:202
  117.0 6.5 %collective-permute-start.17 = (bf16[1,32,256]{2,1,0:T(8,128)(2,1)S(1)}, bf16[1,32,256]{2,1,0:T(8,128)(2,1)S(1)}, u32[]{:S(2)}, u32[]{:S(2)}) collective-permute-start(bf16[1,32,256]{2,1,0:T(8,128)(2,1)S(1)} %shard_map.82.refs_0_), channel_id=1, source_target_pairs={{0,16},{8,24},{16,0},{24,8},{1,17},{9,25},{17,1},{25,9},{2,18},{10... | collective-permute-start | bytes 49160 | tf_op jit(solution)/shard_map/ppermute | solution.py:202
  123.5 10.1 %copy-start.3 = (bf16[512,2048]{1,0:T(8,128)(2,1)S(1)}, bf16[512,2048]{1,0:T(8,128)(2,1)}, u32[]{:S(2)}) copy-start(bf16[512,2048]{1,0:T(8,128)(2,1)} %refs_4_.3) | copy-start | bytes 6291460
  123.5 4.0 %collective-permute-start.20 = (bf16[1,32,256]{2,1,0:T(8,128)(2,1)S(1)}, bf16[1,32,256]{2,1,0:T(8,128)(2,1)S(1)}, u32[]{:S(2)}, u32[]{:S(2)}) collective-permute-start(bf16[1,32,256]{2,1,0:T(8,128)(2,1)S(1)} %shard_map.83.refs_0_), channel_id=1, source_target_pairs={{0,1},{1,0},{2,3},{3,2},{4,5},{5,4},{6,7},{7,6},{8,9},{9,8},{10,11... | collective-permute-start | bytes 49160 | tf_op jit(solution)/shard_map/ppermute | solution.py:28
  127.6 3.4 %collective-permute-start.23 = (bf16[2,32,256]{2,1,0:T(8,128)(2,1)S(1)}, bf16[2,32,256]{2,1,0:T(8,128)(2,1)S(1)}, u32[]{:S(2)}, u32[]{:S(2)}) collective-permute-start(bf16[2,32,256]{2,1,0:T(8,128)(2,1)S(1)} %shard_map.84.refs_0_), channel_id=1, source_target_pairs={{0,6},{2,0},{4,2},{6,4},{1,7},{3,1},{5,3},{7,5},{8,14},{10,8},{12,... | collective-permute-start | bytes 98312 | tf_op jit(solution)/shard_map/ppermute | solution.py:202
  128.6 4.0 %collective-permute-start.22 = (bf16[2,32,256]{2,1,0:T(8,128)(2,1)S(1)}, bf16[2,32,256]{2,1,0:T(8,128)(2,1)S(1)}, u32[]{:S(2)}, u32[]{:S(2)}) collective-permute-start(bf16[2,32,256]{2,1,0:T(8,128)(2,1)S(1)} %shard_map.84.refs_0_), channel_id=1, source_target_pairs={{0,2},{2,4},{4,6},{6,0},{1,3},{3,5},{5,7},{7,1},{8,10},{10,12},{12... | collective-permute-start | bytes 98312 | tf_op jit(solution)/shard_map/ppermute | solution.py:202
  129.0 4.6 %collective-permute-start.21 = (bf16[2,32,256]{2,1,0:T(8,128)(2,1)S(1)}, bf16[2,32,256]{2,1,0:T(8,128)(2,1)S(1)}, u32[]{:S(2)}, u32[]{:S(2)}) collective-permute-start(bf16[2,32,256]{2,1,0:T(8,128)(2,1)S(1)} %shard_map.84.refs_0_), channel_id=1, source_target_pairs={{0,4},{2,6},{4,0},{6,2},{1,5},{3,7},{5,1},{7,3},{8,12},{10,14},{12... | collective-permute-start | bytes 98312 | tf_op jit(solution)/shard_map/ppermute | solution.py:202
  143.2 6.1 %collective-permute-start.26 = (bf16[1,32,512]{2,1,0:T(8,128)(2,1)S(1)}, bf16[1,32,512]{2,1,0:T(8,128)(2,1)S(1)}, u32[]{:S(2)}, u32[]{:S(2)}) collective-permute-start(bf16[1,32,512]{2,1,0:T(8,128)(2,1)S(1)} %shard_map.86.refs_0_), channel_id=1, source_target_pairs={{0,24},{8,0},{16,8},{24,16},{1,25},{9,1},{17,9},{25,17},{2,26},{10... | collective-permute-start | bytes 98312 | tf_op jit(solution)/shard_map/ppermute | solution.py:202
  147.1 4.9 %collective-permute-start.25 = (bf16[1,32,512]{2,1,0:T(8,128)(2,1)S(1)}, bf16[1,32,512]{2,1,0:T(8,128)(2,1)S(1)}, u32[]{:S(2)}, u32[]{:S(2)}) collective-permute-start(bf16[1,32,512]{2,1,0:T(8,128)(2,1)S(1)} %shard_map.86.refs_0_), channel_id=1, source_target_pairs={{0,8},{8,16},{16,24},{24,0},{1,9},{9,17},{17,25},{25,1},{2,10},{10... | collective-permute-start | bytes 98312 | tf_op jit(solution)/shard_map/ppermute | solution.py:202
  147.1 6.7 %collective-permute-start.24 = (bf16[1,32,512]{2,1,0:T(8,128)(2,1)S(1)}, bf16[1,32,512]{2,1,0:T(8,128)(2,1)S(1)}, u32[]{:S(2)}, u32[]{:S(2)}) collective-permute-start(bf16[1,32,512]{2,1,0:T(8,128)(2,1)S(1)} %shard_map.86.refs_0_), channel_id=1, source_target_pairs={{0,16},{8,24},{16,0},{24,8},{1,17},{9,25},{17,1},{25,9},{2,18},{10... | collective-permute-start | bytes 98312 | tf_op jit(solution)/shard_map/ppermute | solution.py:202
  153.8 4.7 %collective-permute-start.29 = (bf16[4,32,512]{2,1,0:T(8,128)(2,1)S(1)}, bf16[4,32,512]{2,1,0:T(8,128)(2,1)S(1)}, u32[]{:S(2)}, u32[]{:S(2)}) collective-permute-start(bf16[4,32,512]{2,1,0:T(8,128)(2,1)S(1)} %shard_map.87.field_ref), channel_id=1, source_target_pairs={{0,6},{2,0},{4,2},{6,4},{1,7},{3,1},{5,3},{7,5},{8,14},{10,8},{12,... | collective-permute-start | bytes 393224 | tf_op jit(solution)/shard_map/ppermute | solution.py:202
  155.9 6.4 %collective-permute-start.28 = (bf16[4,32,512]{2,1,0:T(8,128)(2,1)S(1)}, bf16[4,32,512]{2,1,0:T(8,128)(2,1)S(1)}, u32[]{:S(2)}, u32[]{:S(2)}) collective-permute-start(bf16[4,32,512]{2,1,0:T(8,128)(2,1)S(1)} %shard_map.87.field_ref), channel_id=1, source_target_pairs={{0,2},{2,4},{4,6},{6,0},{1,3},{3,5},{5,7},{7,1},{8,10},{10,12},{12... | collective-permute-start | bytes 393224 | tf_op jit(solution)/shard_map/ppermute | solution.py:202
  155.9 7.7 %collective-permute-start.27 = (bf16[4,32,512]{2,1,0:T(8,128)(2,1)S(1)}, bf16[4,32,512]{2,1,0:T(8,128)(2,1)S(1)}, u32[]{:S(2)}, u32[]{:S(2)}) collective-permute-start(bf16[4,32,512]{2,1,0:T(8,128)(2,1)S(1)} %shard_map.87.field_ref), channel_id=1, source_target_pairs={{0,4},{2,6},{4,0},{6,2},{1,5},{3,7},{5,1},{7,3},{8,12},{10,14},{12... | collective-permute-start | bytes 393224 | tf_op jit(solution)/shard_map/ppermute | solution.py:202
  163.6 9.0 %copy-start.5 = (bf16[64,512]{1,0:T(8,128)(2,1)S(1)}, bf16[64,512]{1,0:T(8,128)(2,1)}, u32[]{:S(2)}) copy-start(bf16[64,512]{1,0:T(8,128)(2,1)} %trial_ref.1) | copy-start | bytes 196612
  165.0 7.7 %collective-permute-start.30 = (bf16[512,64]{1,0:T(8,128)(2,1)S(1)}, bf16[512,64]{1,0:T(8,128)(2,1)S(1)}, u32[]{:S(2)}, u32[]{:S(2)}) collective-permute-start(bf16[512,64]{1,0:T(8,128)(2,1)S(1)} %get-tuple-element.13), channel_id=1, source_target_pairs={{0,1},{1,0},{2,3},{3,2},{4,5},{5,4},{6,7},{7,6},{8,9},{9,8},{10,11... | collective-permute-start | bytes 196616 | tf_op jit(solution)/shard_map/ppermute | solution.py:28

commit v5 on v3

--- a/solution.py
+++ b/solution.py
@@ -14,14 +14,14 @@
 
 FINE = (("x", 4), ("zl", 2), ("zh", 4), ("y", 4), ("core", 2))
 VAL = ("x", "zl")
-RING = ("zh", "y")
+RING = ("y", "zh")
 PTS = ("zh", "y", "core")
 
 BF16 = jnp.bfloat16
 F32 = jnp.float32
 VMEM = pl.BlockSpec(memory_space=pltpu.VMEM)
 VMEM_LIMIT = 16 << 20
-UNROLL = 2
+UNROLL = 4
 START_FLOPS = 4_000_000_000
 
 
@@ -147,8 +147,9 @@
     even = h_ref[0] == 0
 
     def added(ref, q):
-        total = ref[q].astype(F32)
-        for index in range(q + pieces, ref.shape[0], pieces):
+        shares = ref.shape[0] // pieces
+        total = ref[q * shares].astype(F32)
+        for index in range(q * shares + 1, (q + 1) * shares):
             total = total + ref[index].astype(F32)
         return total
 

time: 165 us -> 165 us (level)
  blocking collectives: 85.9 us -> 89.5 us
  starting transfers between devices: 32.2 us -> 28.7 us
    all_to_all x6, blocking collectives: 85.9 us -> 89.5 us  [exchange(): return lax.all_to_all(array, axes, 0, 0, tiled=True)]
    ppermute x7, starting transfers between devices: 17.5 us -> 15.2 us  [swap_cores(): return lax.ppermute(array, 'core', [(0, 1), (1, 0)])]
  transfers between devices with their start and end apart: 19 -> 19, of which waited for: 11 -> 13; matrix products, arithmetic and copies ran while one was open for 0% -> 0% of each run, Pallas kernels for 6% -> 6%
where the time goes in v5:
time: 165 us; the launch traced here: 164 us
  blocking collectives  89.5 us (54%)
  starting transfers between devices  28.7 us (17%)
  Pallas kernels  26.4 us (16%)
  waiting for transfers between devices  17.9 us (11%)
    all_to_all x6, blocking collectives, exchange(): return lax.all_to_all(array, axes, 0, 0, tiled=True)  89.5 us
    pallas_call x21, Pallas kernels, call(): pl.pallas_call(kernel, in_specs=[smem] * scalars + [VMEM] * (len(inputs)...  26.4 us
    ppermute x7, starting transfers between devices, swap_cores(): return lax.ppermute(array, 'core', [(0, 1), (1, 0)])  15.2 us
    ppermute x12, starting transfers between devices, shifted(): lax.ppermute(array, axis, [(i, (i + step) % count) for i in range(count)])  13.5 us
    ppermute x12, waiting for transfers between devices, shifted(): lax.ppermute(array, axis, [(i, (i + step) % count) for i in range(count)])  13.1 us
    ppermute x7, waiting for transfers between devices, swap_cores(): return lax.ppermute(array, 'core', [(0, 1), (1, 0)])  4.84 us
  transfers between devices with their start and end apart: 19, of which 13 were waited for; matrix products, arithmetic and copies ran while one was open for 0% of the time, Pallas kernels for 6%

profile of v5, /device:TPU:1, one launch (start us, length us, event | category | flops | bytes accessed | tf_op | source)
XLA Modules:
  0.0 164.2 jit_solution(12649823744615893760)
XLA Ops:
  0.6 3.3 %collective-permute-start.1 = (bf16[16,16384]{1,0:T(8,128)(2,1)}, bf16[16,16384]{1,0:T(8,128)(2,1)S(1)}, u32[]{:S(2)}, u32[]{:S(2)}) collective-permute-start(bf16[16,16384]{1,0:T(8,128)(2,1)} %cond_ref.19), channel_id=1, source_target_pairs={{0,1},{1,0},{2,3},{3,2},{4,5},{5,4},{6,7},{7,6},{8,9},{9,8},{10,11... | collective-permute-start | bytes 1572872 | tf_op jit(solution)/shard_map/ppermute | solution.py:29
  3.9 0.8 copy-done.4
  5.1 1.2 collective-permute-done.xt_other_ref.old_other_ref
  6.3 5.0 %shard_map.69 = bf16[32,32,256]{2,1,0:T(8,128)(2,1)S(1)} custom-call(s32[1]{0:T(128)} %bitcast.h_ref, bf16[512,64]{1,0:T(8,128)(2,1)S(1)} %shard_map.68.xt_ref.old_ref, bf16[512,64]{1,0:T(8,128)(2,1)S(1)} %collective-permute-done.xt_other_ref.old_other_ref, bf16[64,16384]{1,0:T(8,128)(2,1)S(1)} %copy-done, bf16[16,16384]{1,0:T(8,128)(2,1)S(1)} %copy-done.1, ...), custom_call_target="tpu_custom_call" | custom-call | flops 1073741824 | bytes 3801090 | tf_op jit(solution)/shard_map/pallas_call | solution.py:43
  11.4 17.0 %all_to_all.30.in_ref = bf16[32,32,256]{2,1,0:T(8,128)(2,1)S(1)} all-to-all(bf16[32,32,256]{2,1,0:T(8,128)(2,1)S(1)} %shard_map.69), channel_id=1, replica_groups=mesh['x'=4,'zl'=2,'zh'=4,'y'=4,'core'=2] {'x','zl','y'}, dimensions={0} | all-to-all | bytes 1048576 | tf_op jit(solution)/shard_map/all_to_all | solution.py:33
  28.5 21.6 %all_to_all.31.own_ref = bf16[16,32,256]{2,1,0:T(8,128)(2,1)S(1)} all-to-all(bf16[16,32,256]{2,1,0:T(8,128)(2,1)S(1)} %shard_map.70), channel_id=1, replica_groups=mesh['x'=4,'zl'=2,'zh'=4,'y'=4,'core'=2] {'y','zh'}, dimensions={0} | all-to-all | bytes 524288 | tf_op jit(solution)/shard_map/all_to_all | solution.py:33
  50.1 1.9 %collective-permute-start.2 = (bf16[16,32,256]{2,1,0:T(8,128)(2,1)S(1)}, bf16[16,32,256]{2,1,0:T(8,128)(2,1)S(1)}, u32[]{:S(2)}, u32[]{:S(2)}) collective-permute-start(bf16[16,32,256]{2,1,0:T(8,128)(2,1)S(1)} %all_to_all.31.own_ref), channel_id=1, source_target_pairs={{0,1},{1,0},{2,3},{3,2},{4,5},{5,4},{6,7},{7,6},{8,9},{9,8},{10,11... | collective-permute-start | bytes 786440 | tf_op jit(solution)/shard_map/ppermute | solution.py:29
  51.9 1.2 collective-permute-done.2.other_ref
  53.1 0.7 shard_map.71
  53.8 9.0 %all_to_all.32.in_ref = bf16[8,32,512]{2,1,0:T(8,128)(2,1)S(1)} all-to-all(bf16[8,32,512]{2,1,0:T(8,128)(2,1)S(1)} %shard_map.71), channel_id=1, replica_groups=mesh['x'=4,'zl'=2,'zh'=4,'y'=4,'core'=2] {'x','zl'}, dimensions={0} | all-to-all | bytes 524288 | tf_op jit(solution)/shard_map/all_to_all | solution.py:33
  62.9 0.6 collective-permute-start.5
  63.5 1.9 %collective-permute-start.4 = (bf16[1,32,512]{2,1,0:T(8,128)(2,1)S(1)}, bf16[1,32,512]{2,1,0:T(8,128)(2,1)S(1)}, u32[]{:S(2)}, u32[]{:S(2)}) collective-permute-start(bf16[1,32,512]{2,1,0:T(8,128)(2,1)S(1)} %shard_map.72.refs_0_), channel_id=1, source_target_pairs={{0,8},{8,16},{16,24},{24,0},{1,9},{9,17},{17,25},{25,1},{2,10},{10... | collective-permute-start | bytes 98312 | tf_op jit(solution)/shard_map/ppermute | solution.py:224
  65.3 2.2 %collective-permute-start.3 = (bf16[1,32,512]{2,1,0:T(8,128)(2,1)S(1)}, bf16[1,32,512]{2,1,0:T(8,128)(2,1)S(1)}, u32[]{:S(2)}, u32[]{:S(2)}) collective-permute-start(bf16[1,32,512]{2,1,0:T(8,128)(2,1)S(1)} %shard_map.72.refs_0_), channel_id=1, source_target_pairs={{0,16},{8,24},{16,0},{24,8},{1,17},{9,25},{17,1},{25,9},{2,18},{10... | collective-permute-start | bytes 98312 | tf_op jit(solution)/shard_map/ppermute | solution.py:224
  67.6 0.8 collective-permute-done.4.refs_2_
  68.4 3.6 %collective-permute-done.3.refs_1_ = bf16[1,32,512]{2,1,0:T(8,128)(2,1)S(1)} collective-permute-done((bf16[1,32,512]{2,1,0:T(8,128)(2,1)S(1)}, bf16[1,32,512]{2,1,0:T(8,128)(2,1)S(1)}, u32[]{:S(2)}, u32[]{:S(2)}) %collective-permute-start.3) | collective-permute-done | bytes 32800 | tf_op jit(solution)/shard_map/ppermute | solution.py:224
  72.0 0.7 collective-permute-start.8
  72.7 0.9 collective-permute-start.7
  73.6 0.6 collective-permute-start.6
  74.1 1.2 shard_map.74.refs_0_
  75.4 0.6 collective-permute-done.8.field_ref
  76.0 2.1 %shard_map.75.refs_0_ = f32[1024,64]{1,0:T(8,128)S(1)} custom-call(s32[1]{0:T(128)} %bitcast.h_ref, s32[1]{0:T(128)} %bitcast.1.zh_ref, s32[1]{0:T(128)S(6)} %rem.73.y_ref, bf16[4,32,512]{2,1,0:T(8,128)(2,1)} %collective-permute-done.8.field_ref, bf16[64,16384]{1,0:T(8,128)(2,1)S(1)} %copy-done, bf16[16,16384]{1,0:T(8,128)(2,1)S(1)} %copy-done.1, ...), custom_call_target="tpu_custom_call" | custom-call | flops 268435456 | bytes 3538950 | tf_op jit(solution)/shard_map/pallas_call | solution.py:43
  78.2 1.0 collective-permute-done.7.field_ref
  79.2 2.1 %shard_map.76.refs_0_ = f32[1024,64]{1,0:T(8,128)S(1)} custom-call(s32[1]{0:T(128)} %bitcast.h_ref, s32[1]{0:T(128)} %bitcast.1.zh_ref, s32[1]{0:T(128)S(6)} %rem.67.y_ref, bf16[4,32,512]{2,1,0:T(8,128)(2,1)} %collective-permute-done.7.field_ref, bf16[64,16384]{1,0:T(8,128)(2,1)S(1)} %copy-done, bf16[16,16384]{1,0:T(8,128)(2,1)S(1)} %copy-done.1, ...), custom_call_target="tpu_custom_call" | custom-call | flops 268435456 | bytes 3538950 | tf_op jit(solution)/shard_map/pallas_call | solution.py:43
  81.4 2.3 %shard_map.77 = (f32[1024,64]{1,0:T(8,128)S(1)}, bf16[1024,64]{1,0:T(8,128)(2,1)S(1)}) custom-call(s32[1]{0:T(128)} %bitcast.h_ref, s32[1]{0:T(128)} %bitcast.1.zh_ref, s32[1]{0:T(128)S(6)} %rem.61.y_ref, bf16[4,32,512]{2,1,0:T(8,128)(2,1)} %collective-permute-done.6.field_ref, bf16[64,16384]{1,0:T(8,128)(2,1)S(1)} %copy-done, ...), custom_call_target="tpu_custom_call" | custom-call | flops 268435456 | bytes 3670022 | tf_op jit(solution)/shard_map/pallas_call | solution.py:43
  83.6 3.6 %collective-permute-start.9 = (bf16[1024,64]{1,0:T(8,128)(2,1)S(1)}, bf16[1024,64]{1,0:T(8,128)(2,1)S(1)}, u32[]{:S(2)}, u32[]{:S(2)}) collective-permute-start(bf16[1024,64]{1,0:T(8,128)(2,1)S(1)} %get-tuple-element.9), channel_id=1, source_target_pairs={{0,1},{1,0},{2,3},{3,2},{4,5},{5,4},{6,7},{7,6},{8,9},{9,8},{10,11... | collective-permute-start | bytes 393224 | tf_op jit(solution)/shard_map/ppermute | solution.py:29
  87.4 1.1 collective-permute-done.10.gap_other_ref
  88.4 5.3 %shard_map.78 = (bf16[32,32,256]{2,1,0:T(8,128)(2,1)S(1)}, bf16[512,64]{1,0:T(8,128)(2,1)S(1)}, bf16[512,64]{1,0:T(8,128)(2,1)}) custom-call(s32[1]{0:T(128)} %bitcast.h_ref, f32[1024,64]{1,0:T(8,128)S(1)} %get-tuple-element.8.part_ref, bf16[1024,64]{1,0:T(8,128)(2,1)S(1)} %collective-permute-done.9.recv_ref, bf16[512,64]{1,0:T(8,128)(2,1)S(1)} %shard_map.68.xt_ref.old_ref, ...), custom_call_target="tpu_custom_call" | custom-call | flops 1073741824 | bytes 4198402 | tf_op jit(solution)/shard_map/pallas_call | solution.py:43
  93.7 15.4 %all_to_all.33.in_ref = bf16[32,32,256]{2,1,0:T(8,128)(2,1)S(1)} all-to-all(bf16[32,32,256]{2,1,0:T(8,128)(2,1)S(1)} %get-tuple-element.11), channel_id=1, replica_groups=mesh['x'=4,'zl'=2,'zh'=4,'y'=4,'core'=2] {'x','zl','y'}, dimensions={0} | all-to-all | bytes 1048576 | tf_op jit(solution)/shard_map/all_to_all | solution.py:33
  109.3 17.4 %all_to_all.34.own_ref = bf16[16,32,256]{2,1,0:T(8,128)(2,1)S(1)} all-to-all(bf16[16,32,256]{2,1,0:T(8,128)(2,1)S(1)} %shard_map.80), channel_id=1, replica_groups=mesh['x'=4,'zl'=2,'zh'=4,'y'=4,'core'=2] {'y','zh'}, dimensions={0} | all-to-all | bytes 524288 | tf_op jit(solution)/shard_map/all_to_all | solution.py:33
  126.6 2.3 %collective-permute-start.11 = (bf16[16,32,256]{2,1,0:T(8,128)(2,1)S(1)}, bf16[16,32,256]{2,1,0:T(8,128)(2,1)S(1)}, u32[]{:S(2)}, u32[]{:S(2)}) collective-permute-start(bf16[16,32,256]{2,1,0:T(8,128)(2,1)S(1)} %all_to_all.34.own_ref), channel_id=1, source_target_pairs={{0,1},{1,0},{2,3},{3,2},{4,5},{5,4},{6,7},{7,6},{8,9},{9,8},{10,11... | collective-permute-start | bytes 786440 | tf_op jit(solution)/shard_map/ppermute | solution.py:29
  128.9 1.2 collective-permute-done.11.other_ref
  130.1 0.7 shard_map.81
  130.8 9.0 %all_to_all.35.in_ref = bf16[8,32,512]{2,1,0:T(8,128)(2,1)S(1)} all-to-all(bf16[8,32,512]{2,1,0:T(8,128)(2,1)S(1)} %shard_map.81), channel_id=1, replica_groups=mesh['x'=4,'zl'=2,'zh'=4,'y'=4,'core'=2] {'x','zl'}, dimensions={0} | all-to-all | bytes 524288 | tf_op jit(solution)/shard_map/all_to_all | solution.py:33
  140.4 1.9 %collective-permute-start.13 = (bf16[1,32,512]{2,1,0:T(8,128)(2,1)S(1)}, bf16[1,32,512]{2,1,0:T(8,128)(2,1)S(1)}, u32[]{:S(2)}, u32[]{:S(2)}) collective-permute-start(bf16[1,32,512]{2,1,0:T(8,128)(2,1)S(1)} %shard_map.82.refs_0_), channel_id=1, source_target_pairs={{0,8},{8,16},{16,24},{24,0},{1,9},{9,17},{17,25},{25,1},{2,10},{10... | collective-permute-start | bytes 98312 | tf_op jit(solution)/shard_map/ppermute | solution.py:224
  142.3 2.2 %collective-permute-start.12 = (bf16[1,32,512]{2,1,0:T(8,128)(2,1)S(1)}, bf16[1,32,512]{2,1,0:T(8,128)(2,1)S(1)}, u32[]{:S(2)}, u32[]{:S(2)}) collective-permute-start(bf16[1,32,512]{2,1,0:T(8,128)(2,1)S(1)} %shard_map.82.refs_0_), channel_id=1, source_target_pairs={{0,16},{8,24},{16,0},{24,8},{1,17},{9,25},{17,1},{25,9},{2,18},{10... | collective-permute-start | bytes 98312 | tf_op jit(solution)/shard_map/ppermute | solution.py:224
  144.5 0.8 collective-permute-done.13.refs_2_
  145.4 3.7 %collective-permute-done.12.refs_1_ = bf16[1,32,512]{2,1,0:T(8,128)(2,1)S(1)} collective-permute-done((bf16[1,32,512]{2,1,0:T(8,128)(2,1)S(1)}, bf16[1,32,512]{2,1,0:T(8,128)(2,1)S(1)}, u32[]{:S(2)}, u32[]{:S(2)}) %collective-permute-start.12) | collective-permute-done | bytes 32800 | tf_op jit(solution)/shard_map/ppermute | solution.py:224
  149.0 0.6 collective-permute-start.17
  149.7 0.9 collective-permute-start.16
  150.6 0.6 collective-permute-start.15
  151.2 1.2 shard_map.84.refs_0_
  152.9 1.2 shard_map.85.refs_0_
  154.2 1.9 %collective-permute-done.16.field_ref = bf16[4,32,512]{2,1,0:T(8,128)(2,1)S(1)} collective-permute-done((bf16[4,32,512]{2,1,0:T(8,128)(2,1)S(1)}, bf16[4,32,512]{2,1,0:T(8,128)(2,1)S(1)}, u32[]{:S(2)}, u32[]{:S(2)}) %collective-permute-start.16) | collective-permute-done | bytes 131104 | tf_op jit(solution)/shard_map/ppermute | solution.py:224
  156.1 1.2 shard_map.86.refs_0_
  157.4 1.3 shard_map.87
  158.7 3.7 %collective-permute-start.18 = (bf16[512,64]{1,0:T(8,128)(2,1)S(1)}, bf16[512,64]{1,0:T(8,128)(2,1)S(1)}, u32[]{:S(2)}, u32[]{:S(2)}) collective-permute-start(bf16[512,64]{1,0:T(8,128)(2,1)S(1)} %get-tuple-element.13), channel_id=1, source_target_pairs={{0,1},{1,0},{2,3},{3,2},{4,5},{5,4},{6,7},{7,6},{8,9},{9,8},{10,11... | collective-permute-start | bytes 196616 | tf_op jit(solution)/shard_map/ppermute | solution.py:29
  162.4 0.7 shard_map.79
  163.4 0.8 shard_map.88
  (31 shorter events, 2.1 us)
Async XLA Ops:
  0.6 5.7 %copy-start.1 = (bf16[16,16384]{1,0:T(8,128)(2,1)S(1)}, bf16[16,16384]{1,0:T(8,128)(2,1)}, u32[]{:S(2)}) copy-start(bf16[16,16384]{1,0:T(8,128)(2,1)} %cond_ref.19) | copy-start | bytes 1572868
  0.6 5.7 %copy-start = (bf16[64,16384]{1,0:T(8,128)(2,1)S(1)}, bf16[64,16384]{1,0:T(8,128)(2,1)}, u32[]{:S(2)}) copy-start(bf16[64,16384]{1,0:T(8,128)(2,1)} %val_ref.19) | copy-start | bytes 6291460
  0.6 5.7 %collective-permute-start.1 = (bf16[16,16384]{1,0:T(8,128)(2,1)}, bf16[16,16384]{1,0:T(8,128)(2,1)S(1)}, u32[]{:S(2)}, u32[]{:S(2)}) collective-permute-start(bf16[16,16384]{1,0:T(8,128)(2,1)} %cond_ref.19), channel_id=1, source_target_pairs={{0,1},{1,0},{2,3},{3,2},{4,5},{5,4},{6,7},{7,6},{8,9},{9,8},{10,11... | collective-permute-start | bytes 1572872 | tf_op jit(solution)/shard_map/ppermute | solution.py:29
  3.9 0.8 copy-start.4
  4.9 1.4 collective-permute-start
  11.3 41.7 %copy-start.2 = (bf16[512,2048]{1,0:T(8,128)(2,1)S(1)}, bf16[512,2048]{1,0:T(8,128)(2,1)}, u32[]{:S(2)}) copy-start(bf16[512,2048]{1,0:T(8,128)(2,1)} %kernel_ref.3) | copy-start | bytes 6291460
  50.1 3.0 %collective-permute-start.2 = (bf16[16,32,256]{2,1,0:T(8,128)(2,1)S(1)}, bf16[16,32,256]{2,1,0:T(8,128)(2,1)S(1)}, u32[]{:S(2)}, u32[]{:S(2)}) collective-permute-start(bf16[16,32,256]{2,1,0:T(8,128)(2,1)S(1)} %all_to_all.31.own_ref), channel_id=1, source_target_pairs={{0,1},{1,0},{2,3},{3,2},{4,5},{5,4},{6,7},{7,6},{8,9},{9,8},{10,11... | collective-permute-start | bytes 786440 | tf_op jit(solution)/shard_map/ppermute | solution.py:29
  62.9 4.7 %collective-permute-start.5 = (bf16[1,32,512]{2,1,0:T(8,128)(2,1)S(1)}, bf16[1,32,512]{2,1,0:T(8,128)(2,1)S(1)}, u32[]{:S(2)}, u32[]{:S(2)}) collective-permute-start(bf16[1,32,512]{2,1,0:T(8,128)(2,1)S(1)} %shard_map.72.refs_0_), channel_id=1, source_target_pairs={{0,24},{8,0},{16,8},{24,16},{1,25},{9,1},{17,9},{25,17},{2,26},{10... | collective-permute-start | bytes 98312 | tf_op jit(solution)/shard_map/ppermute | solution.py:224
  63.5 4.9 %collective-permute-start.4 = (bf16[1,32,512]{2,1,0:T(8,128)(2,1)S(1)}, bf16[1,32,512]{2,1,0:T(8,128)(2,1)S(1)}, u32[]{:S(2)}, u32[]{:S(2)}) collective-permute-start(bf16[1,32,512]{2,1,0:T(8,128)(2,1)S(1)} %shard_map.72.refs_0_), channel_id=1, source_target_pairs={{0,8},{8,16},{16,24},{24,0},{1,9},{9,17},{17,25},{25,1},{2,10},{10... | collective-permute-start | bytes 98312 | tf_op jit(solution)/shard_map/ppermute | solution.py:224
  65.3 6.7 %collective-permute-start.3 = (bf16[1,32,512]{2,1,0:T(8,128)(2,1)S(1)}, bf16[1,32,512]{2,1,0:T(8,128)(2,1)S(1)}, u32[]{:S(2)}, u32[]{:S(2)}) collective-permute-start(bf16[1,32,512]{2,1,0:T(8,128)(2,1)S(1)} %shard_map.72.refs_0_), channel_id=1, source_target_pairs={{0,16},{8,24},{16,0},{24,8},{1,17},{9,25},{17,1},{25,9},{2,18},{10... | collective-permute-start | bytes 98312 | tf_op jit(solution)/shard_map/ppermute | solution.py:224
  72.0 4.0 %collective-permute-start.8 = (bf16[4,32,512]{2,1,0:T(8,128)(2,1)S(1)}, bf16[4,32,512]{2,1,0:T(8,128)(2,1)}, u32[]{:S(2)}, u32[]{:S(2)}) collective-permute-start(bf16[4,32,512]{2,1,0:T(8,128)(2,1)S(1)} %shard_map.73.field_ref), channel_id=1, source_target_pairs={{0,6},{2,0},{4,2},{6,4},{1,7},{3,1},{5,3},{7,5},{8,14},{10,8},{12,... | collective-permute-start | bytes 393224 | tf_op jit(solution)/shard_map/ppermute | solution.py:224
  72.7 6.5 %collective-permute-start.7 = (bf16[4,32,512]{2,1,0:T(8,128)(2,1)S(1)}, bf16[4,32,512]{2,1,0:T(8,128)(2,1)}, u32[]{:S(2)}, u32[]{:S(2)}) collective-permute-start(bf16[4,32,512]{2,1,0:T(8,128)(2,1)S(1)} %shard_map.73.field_ref), channel_id=1, source_target_pairs={{0,2},{2,4},{4,6},{6,0},{1,3},{3,5},{5,7},{7,1},{8,10},{10,12},{12... | collective-permute-start | bytes 393224 | tf_op jit(solution)/shard_map/ppermute | solution.py:224
  73.6 7.8 %collective-permute-start.6 = (bf16[4,32,512]{2,1,0:T(8,128)(2,1)S(1)}, bf16[4,32,512]{2,1,0:T(8,128)(2,1)}, u32[]{:S(2)}, u32[]{:S(2)}) collective-permute-start(bf16[4,32,512]{2,1,0:T(8,128)(2,1)S(1)} %shard_map.73.field_ref), channel_id=1, source_target_pairs={{0,4},{2,6},{4,0},{6,2},{1,5},{3,7},{5,1},{7,3},{8,12},{10,14},{12... | collective-permute-start | bytes 393224 | tf_op jit(solution)/shard_map/ppermute | solution.py:224
  81.4 5.9 %copy-start.6 = (f32[64,16]{0,1:T(8,128)S(1)}, f32[64,16]{0,1:T(8,128)}, u32[]{:S(2)}) copy-start(f32[64,16]{0,1:T(8,128)} %param.6) | copy-start | bytes 12292
  83.6 4.8 %collective-permute-start.9 = (bf16[1024,64]{1,0:T(8,128)(2,1)S(1)}, bf16[1024,64]{1,0:T(8,128)(2,1)S(1)}, u32[]{:S(2)}, u32[]{:S(2)}) collective-permute-start(bf16[1024,64]{1,0:T(8,128)(2,1)S(1)} %get-tuple-element.9), channel_id=1, source_target_pairs={{0,1},{1,0},{2,3},{3,2},{4,5},{5,4},{6,7},{7,6},{8,9},{9,8},{10,11... | collective-permute-start | bytes 393224 | tf_op jit(solution)/shard_map/ppermute | solution.py:29
  87.3 1.2 collective-permute-start.10
  93.7 36.4 %copy-start.3 = (bf16[512,2048]{1,0:T(8,128)(2,1)S(1)}, bf16[512,2048]{1,0:T(8,128)(2,1)}, u32[]{:S(2)}) copy-start(bf16[512,2048]{1,0:T(8,128)(2,1)} %kernel_ref.3) | copy-start | bytes 6291460
  126.6 3.5 %collective-permute-start.11 = (bf16[16,32,256]{2,1,0:T(8,128)(2,1)S(1)}, bf16[16,32,256]{2,1,0:T(8,128)(2,1)S(1)}, u32[]{:S(2)}, u32[]{:S(2)}) collective-permute-start(bf16[16,32,256]{2,1,0:T(8,128)(2,1)S(1)} %all_to_all.34.own_ref), channel_id=1, source_target_pairs={{0,1},{1,0},{2,3},{3,2},{4,5},{5,4},{6,7},{7,6},{8,9},{9,8},{10,11... | collective-permute-start | bytes 786440 | tf_op jit(solution)/shard_map/ppermute | solution.py:29
  139.9 4.6 %collective-permute-start.14 = (bf16[1,32,512]{2,1,0:T(8,128)(2,1)S(1)}, bf16[1,32,512]{2,1,0:T(8,128)(2,1)S(1)}, u32[]{:S(2)}, u32[]{:S(2)}) collective-permute-start(bf16[1,32,512]{2,1,0:T(8,128)(2,1)S(1)} %shard_map.82.refs_0_), channel_id=1, source_target_pairs={{0,24},{8,0},{16,8},{24,16},{1,25},{9,1},{17,9},{25,17},{2,26},{10... | collective-permute-start | bytes 98312 | tf_op jit(solution)/shard_map/ppermute | solution.py:224
  140.4 4.9 %collective-permute-start.13 = (bf16[1,32,512]{2,1,0:T(8,128)(2,1)S(1)}, bf16[1,32,512]{2,1,0:T(8,128)(2,1)S(1)}, u32[]{:S(2)}, u32[]{:S(2)}) collective-permute-start(bf16[1,32,512]{2,1,0:T(8,128)(2,1)S(1)} %shard_map.82.refs_0_), channel_id=1, source_target_pairs={{0,8},{8,16},{16,24},{24,0},{1,9},{9,17},{17,25},{25,1},{2,10},{10... | collective-permute-start | bytes 98312 | tf_op jit(solution)/shard_map/ppermute | solution.py:224
  142.3 6.7 %collective-permute-start.12 = (bf16[1,32,512]{2,1,0:T(8,128)(2,1)S(1)}, bf16[1,32,512]{2,1,0:T(8,128)(2,1)S(1)}, u32[]{:S(2)}, u32[]{:S(2)}) collective-permute-start(bf16[1,32,512]{2,1,0:T(8,128)(2,1)S(1)} %shard_map.82.refs_0_), channel_id=1, source_target_pairs={{0,16},{8,24},{16,0},{24,8},{1,17},{9,25},{17,1},{25,9},{2,18},{10... | collective-permute-start | bytes 98312 | tf_op jit(solution)/shard_map/ppermute | solution.py:224
  149.0 3.9 %collective-permute-start.17 = (bf16[4,32,512]{2,1,0:T(8,128)(2,1)S(1)}, bf16[4,32,512]{2,1,0:T(8,128)(2,1)S(1)}, u32[]{:S(2)}, u32[]{:S(2)}) collective-permute-start(bf16[4,32,512]{2,1,0:T(8,128)(2,1)S(1)} %shard_map.83.field_ref), channel_id=1, source_target_pairs={{0,6},{2,0},{4,2},{6,4},{1,7},{3,1},{5,3},{7,5},{8,14},{10,8},{12,... | collective-permute-start | bytes 393224 | tf_op jit(solution)/shard_map/ppermute | solution.py:224
  149.7 6.4 %collective-permute-start.16 = (bf16[4,32,512]{2,1,0:T(8,128)(2,1)S(1)}, bf16[4,32,512]{2,1,0:T(8,128)(2,1)S(1)}, u32[]{:S(2)}, u32[]{:S(2)}) collective-permute-start(bf16[4,32,512]{2,1,0:T(8,128)(2,1)S(1)} %shard_map.83.field_ref), channel_id=1, source_target_pairs={{0,2},{2,4},{4,6},{6,0},{1,3},{3,5},{5,7},{7,1},{8,10},{10,12},{12... | collective-permute-start | bytes 393224 | tf_op jit(solution)/shard_map/ppermute | solution.py:224
  150.6 6.8 %collective-permute-start.15 = (bf16[4,32,512]{2,1,0:T(8,128)(2,1)S(1)}, bf16[4,32,512]{2,1,0:T(8,128)(2,1)S(1)}, u32[]{:S(2)}, u32[]{:S(2)}) collective-permute-start(bf16[4,32,512]{2,1,0:T(8,128)(2,1)S(1)} %shard_map.83.field_ref), channel_id=1, source_target_pairs={{0,4},{2,6},{4,0},{6,2},{1,5},{3,7},{5,1},{7,3},{8,12},{10,14},{12... | collective-permute-start | bytes 393224 | tf_op jit(solution)/shard_map/ppermute | solution.py:224
  157.4 6.1 %copy-start.5 = (bf16[64,512]{1,0:T(8,128)(2,1)S(1)}, bf16[64,512]{1,0:T(8,128)(2,1)}, u32[]{:S(2)}) copy-start(bf16[64,512]{1,0:T(8,128)(2,1)} %trial_ref.1) | copy-start | bytes 196612
  158.7 4.7 %collective-permute-start.18 = (bf16[512,64]{1,0:T(8,128)(2,1)S(1)}, bf16[512,64]{1,0:T(8,128)(2,1)S(1)}, u32[]{:S(2)}, u32[]{:S(2)}) collective-permute-start(bf16[512,64]{1,0:T(8,128)(2,1)S(1)} %get-tuple-element.13), channel_id=1, source_target_pairs={{0,1},{1,0},{2,3},{3,2},{4,5},{5,4},{6,7},{7,6},{8,9},{9,8},{10,11... | collective-permute-start | bytes 196616 | tf_op jit(solution)/shard_map/ppermute | solution.py:29
